TPU v7x, 32 devices: a whole 2x2x4 slice. The times are simulated.
32 devices in a mesh: sys: 4 (over x, core), slab: 8 (over z, y).
Axes of the slice: x: 2, y: 2, z: 4, core: 2. Of those that a mesh axis runs over, the one named last changes fastest.
Arguments:
- right_side: float32 [128, 512, 128], P('slab', 'sys'), parts along dimension 1, may hold values from -8 to 8
- diagonal: float32 [128, 512, 128], P('slab', 'sys'), parts along dimension 1, may hold values from 0.25 to 2
Outputs:
- solution_field: float32 [128, 512, 128], P('slab', 'sys'), parts along dimension 1
- residual: float32 [128, 512, 128], P('slab', 'sys'), parts along dimension 1
There are 4 independent parts, one for each index of `sys`. A program takes and returns all parts, laid end to end along the dimension named above; each array names one. Nothing has to cross between parts.
All inputs are finite; a program needn't handle non-finite values.
Results may differ from a plain program's by a relative error of at most 0.0003.
Values sent between devices are 32-bit elements; how exact they have to be, the bound alone decides.
No kernel may reach another device: no remote copies, remote signals or barrier semaphores. Data moves between devices by JAX's collectives and lax.ppermute only.
A program may use at most 64 MiB of HBM per device.

v0:
```python
import jax
import jax.numpy as jnp
from jax import lax
from jax.sharding import PartitionSpec as P

ITERS = 10


def with_halo(cells, sides, width):
    for axis, dim in sides:
        count = lax.axis_size(axis)
        ends = count - 1
        head = lax.slice_in_dim(cells, 0, width, axis=dim)
        tail = lax.slice_in_dim(cells, cells.shape[dim] - width, cells.shape[dim], axis=dim)
        cells = jnp.concatenate(
            [
                lax.ppermute(tail, axis, [(i, (i + 1) % count) for i in range(ends)]),
                cells,
                lax.ppermute(head, axis, [((i + 1) % count, i) for i in range(ends)]),
            ],
            axis=dim,
        )
    return cells


def operate(values, diagonal):
    padded = with_halo(values, (("slab", 0),), 1)
    beside = padded[2:] + padded[:-2]
    beside = beside + jnp.pad(values[:, 1:], ((0, 0), (0, 1), (0, 0)))
    beside = beside + jnp.pad(values[:, :-1], ((0, 0), (1, 0), (0, 0)))
    beside = beside + jnp.pad(values[:, :, 1:], ((0, 0), (0, 0), (0, 1)))
    beside = beside + jnp.pad(values[:, :, :-1], ((0, 0), (0, 0), (1, 0)))
    return (6.0 + diagonal) * values - beside


def merged_sums(residual, applied):
    return lax.psum((jnp.sum(residual * residual), jnp.sum(residual * applied)), "slab")


def local(right_side, diagonal):
    solution_field = jnp.zeros_like(right_side)
    residual = right_side
    applied = operate(residual, diagonal)
    norm_now, product = merged_sums(residual, applied)
    step_size = norm_now / product
    direction, along = (residual, applied)
    for iteration in range(ITERS):
        solution_field = solution_field + step_size * direction
        residual = residual - step_size * along
        if iteration + 1 < ITERS:
            applied = operate(residual, diagonal)
            norm_next, product = merged_sums(residual, applied)
            scaling = norm_next / norm_now
            step_size = norm_next / (product - scaling * norm_next / step_size)
            direction = residual + scaling * direction
            along = applied + scaling * along
            norm_now = norm_next
    return (solution_field, residual)


def solution(mesh):
    placed = (P("slab", "sys", None), P("slab", "sys", None))
    return jax.shard_map(
        local,
        mesh=mesh,
        in_specs=placed,
        out_specs=(P("slab", "sys", None), P("slab", "sys", None)),
        check_vma=False,
    )
```

profile of v0, /device:TPU:0, one launch (start us, length us, event | category | flops | bytes accessed | tf_op | source)
XLA Modules:
  0.0 378.9 jit_solution(1609734094620581891)
XLA Ops:
  2.8 5.7 %collective-permute-start.1 = (f32[1,128,128]{2,1,0:T(8,128)S(1)}, f32[1,128,128]{2,1,0:T(8,128)S(1)}, u32[]{:S(2)}, u32[]{:S(2)}) collective-permute-start(f32[1,128,128]{2,1,0:T(8,128)S(1)} %get-tuple-element.115), channel_id=1, source_target_pairs={{0,1},{1,2},{2,3},{3,4},{4,5},{5,6},{6,7},{8,9},{9,10},{10,11},{11... | collective-permute-start | bytes 196616 | tf_op jit(solution)/shard_map/ppermute | solution.py:17
  13.9 22.6 %all-reduce.49 = (f32[]{:T(128)}, f32[]{:T(128)}) all-reduce(f32[]{:T(128)} %get-tuple-element.21, f32[]{:T(128)} %get-tuple-element.20), channel_id=1, replica_groups=mesh['sys'=4,'slab'=8] {'slab'}, use_global_device_ids=true, to_apply=%region_1.2 | all-reduce | flops 2 | bytes 16 | tf_op jit(solution)/shard_map/psum | solution.py:37
  40.7 4.5 %collective-permute-start.3 = (f32[1,128,128]{2,1,0:T(8,128)S(1)}, f32[1,128,128]{2,1,0:T(8,128)S(1)}, u32[]{:S(2)}, u32[]{:S(2)}) collective-permute-start(f32[1,128,128]{2,1,0:T(8,128)S(1)} %get-tuple-element.109), channel_id=1, source_target_pairs={{0,1},{1,2},{2,3},{3,4},{4,5},{5,6},{6,7},{8,9},{9,10},{10,11},{11... | collective-permute-start | bytes 196616 | tf_op jit(solution)/shard_map/ppermute | solution.py:17
  49.6 20.2 %all-reduce.48 = (f32[]{:T(128)}, f32[]{:T(128)}) all-reduce(f32[]{:T(128)} %get-tuple-element.19, f32[]{:T(128)} %get-tuple-element.18), channel_id=1, replica_groups=mesh['sys'=4,'slab'=8] {'slab'}, use_global_device_ids=true, to_apply=%region_5.6 | all-reduce | flops 2 | bytes 16 | tf_op jit(solution)/shard_map/psum | solution.py:37
  77.8 4.5 %collective-permute-start.5 = (f32[1,128,128]{2,1,0:T(8,128)S(1)}, f32[1,128,128]{2,1,0:T(8,128)S(1)}, u32[]{:S(2)}, u32[]{:S(2)}) collective-permute-start(f32[1,128,128]{2,1,0:T(8,128)S(1)} %get-tuple-element.103), channel_id=1, source_target_pairs={{0,1},{1,2},{2,3},{3,4},{4,5},{5,6},{6,7},{8,9},{9,10},{10,11},{11... | collective-permute-start | bytes 196616 | tf_op jit(solution)/shard_map/ppermute | solution.py:17
  86.7 20.2 %all-reduce.47 = (f32[]{:T(128)}, f32[]{:T(128)}) all-reduce(f32[]{:T(128)} %get-tuple-element.17, f32[]{:T(128)} %get-tuple-element.16), channel_id=1, replica_groups=mesh['sys'=4,'slab'=8] {'slab'}, use_global_device_ids=true, to_apply=%region_9.10 | all-reduce | flops 2 | bytes 16 | tf_op jit(solution)/shard_map/psum | solution.py:37
  115.6 4.5 %collective-permute-start.7 = (f32[1,128,128]{2,1,0:T(8,128)S(1)}, f32[1,128,128]{2,1,0:T(8,128)S(1)}, u32[]{:S(2)}, u32[]{:S(2)}) collective-permute-start(f32[1,128,128]{2,1,0:T(8,128)S(1)} %get-tuple-element.97), channel_id=1, source_target_pairs={{0,1},{1,2},{2,3},{3,4},{4,5},{5,6},{6,7},{8,9},{9,10},{10,11},{11... | collective-permute-start | bytes 196616 | tf_op jit(solution)/shard_map/ppermute | solution.py:17
  124.5 20.1 %all-reduce.46 = (f32[]{:T(128)}, f32[]{:T(128)}) all-reduce(f32[]{:T(128)} %get-tuple-element.15, f32[]{:T(128)} %get-tuple-element.14), channel_id=1, replica_groups=mesh['sys'=4,'slab'=8] {'slab'}, use_global_device_ids=true, to_apply=%region_13.14 | all-reduce | flops 2 | bytes 16 | tf_op jit(solution)/shard_map/psum | solution.py:37
  151.7 4.5 %collective-permute-start.9 = (f32[1,128,128]{2,1,0:T(8,128)S(1)}, f32[1,128,128]{2,1,0:T(8,128)S(1)}, u32[]{:S(2)}, u32[]{:S(2)}) collective-permute-start(f32[1,128,128]{2,1,0:T(8,128)S(1)} %get-tuple-element.91), channel_id=1, source_target_pairs={{0,1},{1,2},{2,3},{3,4},{4,5},{5,6},{6,7},{8,9},{9,10},{10,11},{11... | collective-permute-start | bytes 196616 | tf_op jit(solution)/shard_map/ppermute | solution.py:17
  160.6 20.1 %all-reduce.45 = (f32[]{:T(128)}, f32[]{:T(128)}) all-reduce(f32[]{:T(128)} %get-tuple-element.13, f32[]{:T(128)} %get-tuple-element.12), channel_id=1, replica_groups=mesh['sys'=4,'slab'=8] {'slab'}, use_global_device_ids=true, to_apply=%region_17.18 | all-reduce | flops 2 | bytes 16 | tf_op jit(solution)/shard_map/psum | solution.py:37
  184.3 3.5 multiply_subtract_fusion.5
  189.3 4.5 %collective-permute-start.11 = (f32[1,128,128]{2,1,0:T(8,128)S(1)}, f32[1,128,128]{2,1,0:T(8,128)S(1)}, u32[]{:S(2)}, u32[]{:S(2)}) collective-permute-start(f32[1,128,128]{2,1,0:T(8,128)S(1)} %get-tuple-element.85), channel_id=1, source_target_pairs={{0,1},{1,2},{2,3},{3,4},{4,5},{5,6},{6,7},{8,9},{9,10},{10,11},{11... | collective-permute-start | bytes 196616 | tf_op jit(solution)/shard_map/ppermute | solution.py:17
  198.3 20.1 %all-reduce.44 = (f32[]{:T(128)}, f32[]{:T(128)}) all-reduce(f32[]{:T(128)} %get-tuple-element.11, f32[]{:T(128)} %get-tuple-element.10), channel_id=1, replica_groups=mesh['sys'=4,'slab'=8] {'slab'}, use_global_device_ids=true, to_apply=%region_21.22 | all-reduce | flops 2 | bytes 16 | tf_op jit(solution)/shard_map/psum | solution.py:37
  225.8 4.7 %collective-permute-start.13 = (f32[1,128,128]{2,1,0:T(8,128)S(1)}, f32[1,128,128]{2,1,0:T(8,128)S(1)}, u32[]{:S(2)}, u32[]{:S(2)}) collective-permute-start(f32[1,128,128]{2,1,0:T(8,128)S(1)} %get-tuple-element.79), channel_id=1, source_target_pairs={{0,1},{1,2},{2,3},{3,4},{4,5},{5,6},{6,7},{8,9},{9,10},{10,11},{11... | collective-permute-start | bytes 196616 | tf_op jit(solution)/shard_map/ppermute | solution.py:17
  235.1 20.2 %all-reduce.43 = (f32[]{:T(128)}, f32[]{:T(128)}) all-reduce(f32[]{:T(128)} %get-tuple-element.9, f32[]{:T(128)} %get-tuple-element.8), channel_id=1, replica_groups=mesh['sys'=4,'slab'=8] {'slab'}, use_global_device_ids=true, to_apply=%region_25.26 | all-reduce | flops 2 | bytes 16 | tf_op jit(solution)/shard_map/psum | solution.py:37
  259.0 3.5 multiply_subtract_fusion.3
  264.0 4.5 %collective-permute-start.15 = (f32[1,128,128]{2,1,0:T(8,128)S(1)}, f32[1,128,128]{2,1,0:T(8,128)S(1)}, u32[]{:S(2)}, u32[]{:S(2)}) collective-permute-start(f32[1,128,128]{2,1,0:T(8,128)S(1)} %get-tuple-element.73), channel_id=1, source_target_pairs={{0,1},{1,2},{2,3},{3,4},{4,5},{5,6},{6,7},{8,9},{9,10},{10,11},{11... | collective-permute-start | bytes 196616 | tf_op jit(solution)/shard_map/ppermute | solution.py:17
  272.9 20.2 %all-reduce.42 = (f32[]{:T(128)}, f32[]{:T(128)}) all-reduce(f32[]{:T(128)} %get-tuple-element.7, f32[]{:T(128)} %get-tuple-element.6), channel_id=1, replica_groups=mesh['sys'=4,'slab'=8] {'slab'}, use_global_device_ids=true, to_apply=%region_29.30 | all-reduce | flops 2 | bytes 16 | tf_op jit(solution)/shard_map/psum | solution.py:37
  300.4 4.5 %collective-permute-start.17 = (f32[1,128,128]{2,1,0:T(8,128)S(1)}, f32[1,128,128]{2,1,0:T(8,128)S(1)}, u32[]{:S(2)}, u32[]{:S(2)}) collective-permute-start(f32[1,128,128]{2,1,0:T(8,128)S(1)} %get-tuple-element.67), channel_id=1, source_target_pairs={{0,1},{1,2},{2,3},{3,4},{4,5},{5,6},{6,7},{8,9},{9,10},{10,11},{11... | collective-permute-start | bytes 196616 | tf_op jit(solution)/shard_map/ppermute | solution.py:17
  309.3 20.2 %all-reduce.41 = (f32[]{:T(128)}, f32[]{:T(128)}) all-reduce(f32[]{:T(128)} %get-tuple-element.5, f32[]{:T(128)} %get-tuple-element.4), channel_id=1, replica_groups=mesh['sys'=4,'slab'=8] {'slab'}, use_global_device_ids=true, to_apply=%region_33.34 | all-reduce | flops 2 | bytes 16 | tf_op jit(solution)/shard_map/psum | solution.py:37
  333.5 3.5 multiply_subtract_fusion.1
  338.5 4.5 %collective-permute-start.19 = (f32[1,128,128]{2,1,0:T(8,128)S(1)}, f32[1,128,128]{2,1,0:T(8,128)S(1)}, u32[]{:S(2)}, u32[]{:S(2)}) collective-permute-start(f32[1,128,128]{2,1,0:T(8,128)S(1)} %get-tuple-element.61), channel_id=1, source_target_pairs={{0,1},{1,2},{2,3},{3,4},{4,5},{5,6},{6,7},{8,9},{9,10},{10,11},{11... | collective-permute-start | bytes 196616 | tf_op jit(solution)/shard_map/ppermute | solution.py:17
  347.4 20.2 %all-reduce.40 = (f32[]{:T(128)}, f32[]{:T(128)}) all-reduce(f32[]{:T(128)} %get-tuple-element.3, f32[]{:T(128)} %get-tuple-element.2), channel_id=1, replica_groups=mesh['sys'=4,'slab'=8] {'slab'}, use_global_device_ids=true, to_apply=%region_37.38 | all-reduce | flops 2 | bytes 16 | tf_op jit(solution)/shard_map/psum | solution.py:37
  371.8 5.9 %multiply_add_fusion = f32[16,128,128]{2,1,0:T(8,128)} fusion(f32[16,128,128]{2,1,0:T(8,128)} %copy-done.7, f32[16,128,128]{2,1,0:T(8,128)} %copy-done.6, f32[16,128,128]{2,1,0:T(8,128)} %copy-done.5, f32[16,128,128]{2,1,0:T(8,128)} %copy-done.4, f32[16,128,128]{2,1,0:T(8,128)} %copy-done.3, f32[16,128,128]{2,1,0:T(8,128)} %copy-done.2, ...), kind=kLoop, calls=%fused_computation.81 | loop fusion | flops 9699328 | bytes 11534412 | tf_op jit(solution)/shard_map/add | solution.py:48
  (101 shorter events, 74.1 us)
Async XLA Ops:
  1.5 9.2 %collective-permute-start = (f32[1,128,128]{2,1,0:T(8,128)S(1)}, f32[1,128,128]{2,1,0:T(8,128)S(1)}, u32[]{:S(2)}, u32[]{:S(2)}) collective-permute-start(f32[1,128,128]{2,1,0:T(8,128)S(1)} %get-tuple-element.114), channel_id=1, source_target_pairs={{1,0},{2,1},{3,2},{4,3},{5,4},{6,5},{7,6},{9,8},{10,9},{11,10},{12... | collective-permute-start | bytes 196616 | tf_op jit(solution)/shard_map/ppermute | solution.py:19
  2.8 7.9 %collective-permute-start.1 = (f32[1,128,128]{2,1,0:T(8,128)S(1)}, f32[1,128,128]{2,1,0:T(8,128)S(1)}, u32[]{:S(2)}, u32[]{:S(2)}) collective-permute-start(f32[1,128,128]{2,1,0:T(8,128)S(1)} %get-tuple-element.115), channel_id=1, source_target_pairs={{0,1},{1,2},{2,3},{3,4},{4,5},{5,6},{6,7},{8,9},{9,10},{10,11},{11... | collective-permute-start | bytes 196616 | tf_op jit(solution)/shard_map/ppermute | solution.py:17
  39.4 6.2 %collective-permute-start.2 = (f32[1,128,128]{2,1,0:T(8,128)S(1)}, f32[1,128,128]{2,1,0:T(8,128)S(1)}, u32[]{:S(2)}, u32[]{:S(2)}) collective-permute-start(f32[1,128,128]{2,1,0:T(8,128)S(1)} %get-tuple-element.108), channel_id=1, source_target_pairs={{1,0},{2,1},{3,2},{4,3},{5,4},{6,5},{7,6},{9,8},{10,9},{11,10},{12... | collective-permute-start | bytes 196616 | tf_op jit(solution)/shard_map/ppermute | solution.py:19
  40.7 6.4 %collective-permute-start.3 = (f32[1,128,128]{2,1,0:T(8,128)S(1)}, f32[1,128,128]{2,1,0:T(8,128)S(1)}, u32[]{:S(2)}, u32[]{:S(2)}) collective-permute-start(f32[1,128,128]{2,1,0:T(8,128)S(1)} %get-tuple-element.109), channel_id=1, source_target_pairs={{0,1},{1,2},{2,3},{3,4},{4,5},{5,6},{6,7},{8,9},{9,10},{10,11},{11... | collective-permute-start | bytes 196616 | tf_op jit(solution)/shard_map/ppermute | solution.py:17
  76.5 6.2 %collective-permute-start.4 = (f32[1,128,128]{2,1,0:T(8,128)S(1)}, f32[1,128,128]{2,1,0:T(8,128)S(1)}, u32[]{:S(2)}, u32[]{:S(2)}) collective-permute-start(f32[1,128,128]{2,1,0:T(8,128)S(1)} %get-tuple-element.102), channel_id=1, source_target_pairs={{1,0},{2,1},{3,2},{4,3},{5,4},{6,5},{7,6},{9,8},{10,9},{11,10},{12... | collective-permute-start | bytes 196616 | tf_op jit(solution)/shard_map/ppermute | solution.py:19
  77.8 6.4 %collective-permute-start.5 = (f32[1,128,128]{2,1,0:T(8,128)S(1)}, f32[1,128,128]{2,1,0:T(8,128)S(1)}, u32[]{:S(2)}, u32[]{:S(2)}) collective-permute-start(f32[1,128,128]{2,1,0:T(8,128)S(1)} %get-tuple-element.103), channel_id=1, source_target_pairs={{0,1},{1,2},{2,3},{3,4},{4,5},{5,6},{6,7},{8,9},{9,10},{10,11},{11... | collective-permute-start | bytes 196616 | tf_op jit(solution)/shard_map/ppermute | solution.py:17
  114.3 6.2 %collective-permute-start.6 = (f32[1,128,128]{2,1,0:T(8,128)S(1)}, f32[1,128,128]{2,1,0:T(8,128)S(1)}, u32[]{:S(2)}, u32[]{:S(2)}) collective-permute-start(f32[1,128,128]{2,1,0:T(8,128)S(1)} %get-tuple-element.96), channel_id=1, source_target_pairs={{1,0},{2,1},{3,2},{4,3},{5,4},{6,5},{7,6},{9,8},{10,9},{11,10},{12... | collective-permute-start | bytes 196616 | tf_op jit(solution)/shard_map/ppermute | solution.py:19
  115.6 6.4 %collective-permute-start.7 = (f32[1,128,128]{2,1,0:T(8,128)S(1)}, f32[1,128,128]{2,1,0:T(8,128)S(1)}, u32[]{:S(2)}, u32[]{:S(2)}) collective-permute-start(f32[1,128,128]{2,1,0:T(8,128)S(1)} %get-tuple-element.97), channel_id=1, source_target_pairs={{0,1},{1,2},{2,3},{3,4},{4,5},{5,6},{6,7},{8,9},{9,10},{10,11},{11... | collective-permute-start | bytes 196616 | tf_op jit(solution)/shard_map/ppermute | solution.py:17
  150.1 8.0 %copy-start.2 = (f32[16,128,128]{2,1,0:T(8,128)}, f32[16,128,128]{2,1,0:T(8,128)S(1)}, u32[]{:S(2)}) copy-start(f32[16,128,128]{2,1,0:T(8,128)S(1)} %multiply_subtract_fusion.6) | copy-start | bytes 3145732
  150.4 6.2 %collective-permute-start.8 = (f32[1,128,128]{2,1,0:T(8,128)S(1)}, f32[1,128,128]{2,1,0:T(8,128)S(1)}, u32[]{:S(2)}, u32[]{:S(2)}) collective-permute-start(f32[1,128,128]{2,1,0:T(8,128)S(1)} %get-tuple-element.90), channel_id=1, source_target_pairs={{1,0},{2,1},{3,2},{4,3},{5,4},{6,5},{7,6},{9,8},{10,9},{11,10},{12... | collective-permute-start | bytes 196616 | tf_op jit(solution)/shard_map/ppermute | solution.py:19
  151.7 6.4 %collective-permute-start.9 = (f32[1,128,128]{2,1,0:T(8,128)S(1)}, f32[1,128,128]{2,1,0:T(8,128)S(1)}, u32[]{:S(2)}, u32[]{:S(2)}) collective-permute-start(f32[1,128,128]{2,1,0:T(8,128)S(1)} %get-tuple-element.91), channel_id=1, source_target_pairs={{0,1},{1,2},{2,3},{3,4},{4,5},{5,6},{6,7},{8,9},{9,10},{10,11},{11... | collective-permute-start | bytes 196616 | tf_op jit(solution)/shard_map/ppermute | solution.py:17
  188.0 6.2 %collective-permute-start.10 = (f32[1,128,128]{2,1,0:T(8,128)S(1)}, f32[1,128,128]{2,1,0:T(8,128)S(1)}, u32[]{:S(2)}, u32[]{:S(2)}) collective-permute-start(f32[1,128,128]{2,1,0:T(8,128)S(1)} %get-tuple-element.84), channel_id=1, source_target_pairs={{1,0},{2,1},{3,2},{4,3},{5,4},{6,5},{7,6},{9,8},{10,9},{11,10},{12... | collective-permute-start | bytes 196616 | tf_op jit(solution)/shard_map/ppermute | solution.py:19
  189.3 6.4 %collective-permute-start.11 = (f32[1,128,128]{2,1,0:T(8,128)S(1)}, f32[1,128,128]{2,1,0:T(8,128)S(1)}, u32[]{:S(2)}, u32[]{:S(2)}) collective-permute-start(f32[1,128,128]{2,1,0:T(8,128)S(1)} %get-tuple-element.85), channel_id=1, source_target_pairs={{0,1},{1,2},{2,3},{3,4},{4,5},{5,6},{6,7},{8,9},{9,10},{10,11},{11... | collective-permute-start | bytes 196616 | tf_op jit(solution)/shard_map/ppermute | solution.py:17
  224.2 8.4 %copy-start.4 = (f32[16,128,128]{2,1,0:T(8,128)}, f32[16,128,128]{2,1,0:T(8,128)S(1)}, u32[]{:S(2)}) copy-start(f32[16,128,128]{2,1,0:T(8,128)S(1)} %multiply_subtract_fusion.4) | copy-start | bytes 3145732
  224.5 6.4 %collective-permute-start.12 = (f32[1,128,128]{2,1,0:T(8,128)S(1)}, f32[1,128,128]{2,1,0:T(8,128)S(1)}, u32[]{:S(2)}, u32[]{:S(2)}) collective-permute-start(f32[1,128,128]{2,1,0:T(8,128)S(1)} %get-tuple-element.78), channel_id=1, source_target_pairs={{1,0},{2,1},{3,2},{4,3},{5,4},{6,5},{7,6},{9,8},{10,9},{11,10},{12... | collective-permute-start | bytes 196616 | tf_op jit(solution)/shard_map/ppermute | solution.py:19
  225.8 6.9 %collective-permute-start.13 = (f32[1,128,128]{2,1,0:T(8,128)S(1)}, f32[1,128,128]{2,1,0:T(8,128)S(1)}, u32[]{:S(2)}, u32[]{:S(2)}) collective-permute-start(f32[1,128,128]{2,1,0:T(8,128)S(1)} %get-tuple-element.79), channel_id=1, source_target_pairs={{0,1},{1,2},{2,3},{3,4},{4,5},{5,6},{6,7},{8,9},{9,10},{10,11},{11... | collective-permute-start | bytes 196616 | tf_op jit(solution)/shard_map/ppermute | solution.py:17
  262.5 8.0 %copy-start.5 = (f32[16,128,128]{2,1,0:T(8,128)}, f32[16,128,128]{2,1,0:T(8,128)S(1)}, u32[]{:S(2)}) copy-start(f32[16,128,128]{2,1,0:T(8,128)S(1)} %get-tuple-element.47) | copy-start | bytes 3145732
  262.7 6.2 %collective-permute-start.14 = (f32[1,128,128]{2,1,0:T(8,128)S(1)}, f32[1,128,128]{2,1,0:T(8,128)S(1)}, u32[]{:S(2)}, u32[]{:S(2)}) collective-permute-start(f32[1,128,128]{2,1,0:T(8,128)S(1)} %get-tuple-element.72), channel_id=1, source_target_pairs={{1,0},{2,1},{3,2},{4,3},{5,4},{6,5},{7,6},{9,8},{10,9},{11,10},{12... | collective-permute-start | bytes 196616 | tf_op jit(solution)/shard_map/ppermute | solution.py:19
  264.0 6.4 %collective-permute-start.15 = (f32[1,128,128]{2,1,0:T(8,128)S(1)}, f32[1,128,128]{2,1,0:T(8,128)S(1)}, u32[]{:S(2)}, u32[]{:S(2)}) collective-permute-start(f32[1,128,128]{2,1,0:T(8,128)S(1)} %get-tuple-element.73), channel_id=1, source_target_pairs={{0,1},{1,2},{2,3},{3,4},{4,5},{5,6},{6,7},{8,9},{9,10},{10,11},{11... | collective-permute-start | bytes 196616 | tf_op jit(solution)/shard_map/ppermute | solution.py:17
  298.9 8.0 %copy-start.6 = (f32[16,128,128]{2,1,0:T(8,128)}, f32[16,128,128]{2,1,0:T(8,128)S(1)}, u32[]{:S(2)}) copy-start(f32[16,128,128]{2,1,0:T(8,128)S(1)} %multiply_subtract_fusion.2) | copy-start | bytes 3145732
  299.1 6.2 %collective-permute-start.16 = (f32[1,128,128]{2,1,0:T(8,128)S(1)}, f32[1,128,128]{2,1,0:T(8,128)S(1)}, u32[]{:S(2)}, u32[]{:S(2)}) collective-permute-start(f32[1,128,128]{2,1,0:T(8,128)S(1)} %get-tuple-element.66), channel_id=1, source_target_pairs={{1,0},{2,1},{3,2},{4,3},{5,4},{6,5},{7,6},{9,8},{10,9},{11,10},{12... | collective-permute-start | bytes 196616 | tf_op jit(solution)/shard_map/ppermute | solution.py:19
  300.4 6.4 %collective-permute-start.17 = (f32[1,128,128]{2,1,0:T(8,128)S(1)}, f32[1,128,128]{2,1,0:T(8,128)S(1)}, u32[]{:S(2)}, u32[]{:S(2)}) collective-permute-start(f32[1,128,128]{2,1,0:T(8,128)S(1)} %get-tuple-element.67), channel_id=1, source_target_pairs={{0,1},{1,2},{2,3},{3,4},{4,5},{5,6},{6,7},{8,9},{9,10},{10,11},{11... | collective-permute-start | bytes 196616 | tf_op jit(solution)/shard_map/ppermute | solution.py:17
  337.2 6.2 %collective-permute-start.18 = (f32[1,128,128]{2,1,0:T(8,128)S(1)}, f32[1,128,128]{2,1,0:T(8,128)S(1)}, u32[]{:S(2)}, u32[]{:S(2)}) collective-permute-start(f32[1,128,128]{2,1,0:T(8,128)S(1)} %get-tuple-element.60), channel_id=1, source_target_pairs={{1,0},{2,1},{3,2},{4,3},{5,4},{6,5},{7,6},{9,8},{10,9},{11,10},{12... | collective-permute-start | bytes 196616 | tf_op jit(solution)/shard_map/ppermute | solution.py:19
  338.5 6.4 %collective-permute-start.19 = (f32[1,128,128]{2,1,0:T(8,128)S(1)}, f32[1,128,128]{2,1,0:T(8,128)S(1)}, u32[]{:S(2)}, u32[]{:S(2)}) collective-permute-start(f32[1,128,128]{2,1,0:T(8,128)S(1)} %get-tuple-element.61), channel_id=1, source_target_pairs={{0,1},{1,2},{2,3},{3,4},{4,5},{5,6},{6,7},{8,9},{9,10},{10,11},{11... | collective-permute-start | bytes 196616 | tf_op jit(solution)/shard_map/ppermute | solution.py:17
  (8 other events, 50.4 us)
where the time goes:
time: 380 us; the launch traced here: 379 us
  blocking collectives  204 us (54%)
  starting transfers between devices  59.7 us (16%)
  other arithmetic  54.7 us (14%)
  between operations  37.4 us (10%)
  waiting for transfers between devices  13.9 us (4%)
  local copies, waits for them, and re-layouts  9.01 us (2%)
    psum x10, blocking collectives, merged_sums(): lax.psum((jnp.sum(residual * residual), jnp.sum(residual * applied)), 'sl...  204 us
    ppermute x10, starting transfers between devices, with_halo(): lax.ppermute(tail, axis, [(i, (i + 1) % count) for i in range(ends)])  46.8 us
    reduce_sum x10, other arithmetic, merged_sums(): jnp.sum(residual * applied)  24.5 us
    sub x10, other arithmetic, local(): residual = residual - step_size * along  24.3 us
    ppermute x10, waiting for transfers between devices, with_halo(): lax.ppermute(tail, axis, [(i, (i + 1) % count) for i in range(ends)])  13.9 us
    ppermute x10, starting transfers between devices, with_halo(): lax.ppermute(head, axis, [((i + 1) % count, i) for i in range(ends)])  12.9 us
  transfers between devices with their start and end apart: 20, of which 9 were waited for; matrix products, arithmetic and copies ran while one was open for 1% of the time, Pallas kernels for 0%

commit v1 on v0

v1 whole, which is shorter than its diff:
```python
import functools

import jax
import jax.numpy as jnp
from jax import lax
from jax.experimental import pallas as pl
from jax.experimental.pallas import tpu as pltpu
from jax.sharding import PartitionSpec as P

FIRST = 5
SECOND = 4
LOW, HIGH = 0.25, 14.0
CENTER = (LOW + HIGH) / 2
HALF = (HIGH - LOW) / 2
ROWS, LANES = 16, 128
F32 = jnp.float32


def edges(shape):
    row = lax.broadcasted_iota(jnp.int32, shape, 0)
    lane = lax.broadcasted_iota(jnp.int32, shape, 1)
    return row == 0, row == shape[0] - 1, lane == 0, lane == shape[1] - 1


def advance(cur, above, below, diag, prev=None):
    first_row, last_row, first_lane, last_lane = edges(cur.shape)
    ny, nx = cur.shape
    zero = jnp.zeros_like(cur)
    beside = above + below
    beside = beside + jnp.where(first_row, zero, pltpu.roll(cur, 1, 0))
    beside = beside + jnp.where(last_row, zero, pltpu.roll(cur, ny - 1, 0))
    beside = beside + jnp.where(first_lane, zero, pltpu.roll(cur, 1, 1))
    beside = beside + jnp.where(last_lane, zero, pltpu.roll(cur, nx - 1, 1))
    image = ((6.0 - CENTER) + diag) * cur - beside
    if prev is None:
        return image * (1.0 / HALF)
    return image * (2.0 / HALF) - prev


def interior(cur, prev, diag, one, two):
    planes = cur.shape[0]

    def inner(z, carry):
        old = None if prev is None else prev[z]
        one[z] = advance(cur[z], cur[z + 1], cur[z - 1], diag[z], old)
        return carry

    def outer(z, carry):
        two[z] = advance(one[z], one[z + 1], one[z - 1], diag[z], cur[z])
        return carry

    lax.fori_loop(1, planes - 1, inner, 0)
    lax.fori_loop(2, planes - 2, outer, 0)


def boundary(where, got_a, got_b, cur, prev, ghost, diag, ghost_diag, one, two):
    last = cur.shape[0] - 1
    even = where[0] == 0
    has_low = where[1].astype(F32)
    has_high = where[2].astype(F32)
    pick = lambda k: (
        jnp.where(even, got_b[k], got_a[k]),
        jnp.where(even, got_a[k], got_b[k]),
    )
    (low_far, high_near), (low_near, high_far) = pick(0), pick(1)
    old = lambda ref, k: None if ref is None else ref[k]
    low = has_low * advance(low_near, cur[0], low_far, ghost_diag[0], old(ghost, 0))
    high = has_high * advance(high_near, high_far, cur[last], ghost_diag[1], old(ghost, 1))
    bottom = advance(cur[0], cur[1], low_near, diag[0], old(prev, 0))
    top = advance(cur[last], high_near, cur[last - 1], diag[last], old(prev, last))
    one[0] = bottom
    one[last] = top
    two[0] = advance(bottom, one[1], low, diag[0], cur[0])
    two[1] = advance(one[1], one[2], bottom, diag[1], cur[1])
    two[last] = advance(top, high, one[last - 1], diag[last], cur[last])
    two[last - 1] = advance(one[last - 1], top, one[last - 2], diag[last - 1], cur[last - 1])
    return low, high


def put_sides(where, field, side_a, side_b):
    even = where[0] == 0
    last = field.shape[0] - 1
    for k in range(2):
        low, high = field[k], field[last - 1 + k]
        side_a[k] = jnp.where(even, high, low)
        side_b[k] = jnp.where(even, low, high)


def grid_index():
    shape = (ROWS, LANES)
    return (
        lax.broadcasted_iota(jnp.int32, shape, 0),
        lax.broadcasted_iota(jnp.int32, shape, 1),
    )


def total(tile):
    return jnp.sum(jnp.sum(tile, axis=0, keepdims=True), axis=1, keepdims=True)


def unit(k):
    row = lax.broadcasted_iota(jnp.int32, (1, LANES), 1)
    col = lax.broadcasted_iota(jnp.int32, (ROWS, 1), 0)
    return (col == k).astype(F32), (row == k).astype(F32)


def axpy(scale, a, b):
    return a[0] + scale * b[0], a[1] + scale * b[1]


def apply(mat, mat_t, v):
    return (
        jnp.sum(mat * v[1], axis=1, keepdims=True),
        jnp.sum(mat_t * v[0], axis=0, keepdims=True),
    )


def form(gram, a, b):
    return total(a[0] * gram * b[1])


def steps(gram, mat, mat_t, x, r, p, count):
    norm = form(gram, r, r)
    for k in range(count):
        image = apply(mat, mat_t, p)
        size = norm / form(gram, p, image)
        x = axpy(size, x, p)
        r = axpy(-size, r, image)
        if k + 1 < count:
            new = form(gram, r, r)
            p = axpy(new / norm, r, p)
            norm = new
    return x, r, p, norm


def chebyshev_columns(first, count):
    ri, ci = grid_index()

    def one(ri, ci):
        inside = (ci >= first) & (ci < first + count)
        diag = jnp.where(inside & (ri == ci), CENTER, 0.0)
        down = jnp.where(ci == first, HALF, HALF / 2)
        diag = diag + jnp.where(inside & (ri == ci + 1), down, 0.0)
        return diag + jnp.where(inside & (ci > first) & (ri == ci - 1), HALF / 2, 0.0)

    return one(ri, ci), one(ci, ri)


def to_powers(size, count):
    ri, ci = grid_index()

    def one(ri, ci):
        j = ci - 1
        inside = (j >= 0) & (j < count)
        out = jnp.where((ci == 0) & (ri == 0), 1.0, 0.0)
        out = out + jnp.where(inside & (ri == j), 1.0 - size * CENTER, 0.0)
        down = jnp.where(j == 0, HALF, HALF / 2)
        out = out - jnp.where(inside & (ri == j + 1), size * down, 0.0)
        return out - jnp.where(inside & (j > 0) & (ri == j - 1), size * (HALF / 2), 0.0)

    return one(ri, ci), one(ci, ri)


def gram_tile(sums):
    ri, ci = grid_index()
    out = jnp.zeros((ROWS, LANES), F32)
    rows = {key: jnp.sum(val, axis=0, keepdims=True) for key, val in sums.items()}
    blank = jnp.zeros((1, LANES), F32)
    for j in sorted({j for _, j in rows}):
        stack = jnp.concatenate([rows.get((i, j), blank) for i in range(ROWS)], axis=0)
        col = jnp.sum(stack, axis=1, keepdims=True)
        out = out + jnp.where(ci == j, col, 0.0)
        row = jnp.sum(jnp.where(ri == ci, col, 0.0), axis=0, keepdims=True)
        out = out + jnp.where((ri == j) & (ci < j), row, 0.0)
    return out


def gather_sums(planes, ny, load, pairs):
    keys = list(pairs)

    def body(z, accs):
        accs = list(accs)
        for y in range(ny // 8):
            tiles = load(z, y)
            for k, (i, j) in enumerate(keys):
                accs[k] = accs[k] + tiles[i] * tiles[j]
        return tuple(accs)

    init = tuple(jnp.zeros((8, LANES), F32) for _ in keys)
    accs = lax.fori_loop(0, planes, body, init)
    return dict(zip(keys, accs))


def first_size(sums):
    norm = jnp.sum(sums[0:1, :], axis=1, keepdims=True)
    cross = jnp.sum(sums[1:2, :], axis=1, keepdims=True)
    return norm, norm / (CENTER * norm + HALF * cross)


def tile(ref, z, y):
    return ref[z, pl.ds(8 * y, 8), :]


def shifted(powers, size, count):
    keep = 1.0 - size * CENTER
    move = size * (HALF / 2)
    out = [powers[0], keep * powers[0] - (2.0 * move) * powers[1]]
    for j in range(1, count):
        out.append(keep * powers[j] - move * (powers[j + 1] + powers[j - 1]))
    return out


def call(kernel, outs, aliases=None):
    def run(*args):
        in_specs = [
            pl.BlockSpec(memory_space=pltpu.SMEM if a.dtype == jnp.int32 else pltpu.VMEM)
            for a in args
        ]
        return pl.pallas_call(
            kernel,
            out_shape=[jax.ShapeDtypeStruct(s, F32) for s in outs],
            in_specs=in_specs,
            out_specs=[pl.BlockSpec(memory_space=pltpu.VMEM) for _ in outs],
            input_output_aliases=aliases or {},
            compiler_params=pltpu.CompilerParams(vmem_limit_bytes=40 << 20),
        )(*args)

    return run


def start_kernel(cur, diag, one, two):
    interior(cur, None, diag, one, two)


def next_kernel(cur, prev, diag, one, two):
    interior(cur, prev, diag, one, two)


def next_sums_kernel(cur, prev, diag, rhs, one, two, sums):
    interior(cur, prev, diag, one, two)
    planes, ny, _ = cur.shape
    got = gather_sums(
        planes,
        ny,
        lambda z, y: {0: tile(rhs, z, y), 1: tile(prev, z, y)},
        [(0, 0), (0, 1)],
    )
    rows = [jnp.sum(got[key], axis=0, keepdims=True) for key in ((0, 0), (0, 1))]
    sums[...] = jnp.concatenate(rows + [jnp.zeros((6, LANES), F32)], axis=0)


def open_edge_kernel(where, got_a, got_b, cur, diag, one_in, two_in, one, two, side_a, side_b, ghost, ghost_diag):
    even = where[0] == 0
    ghost_diag[0] = jnp.where(even, got_b[2], got_a[2])
    ghost_diag[1] = jnp.where(even, got_a[2], got_b[2])
    low, high = boundary(where, got_a, got_b, cur, None, None, diag, ghost_diag, one, two)
    ghost[0] = low
    ghost[1] = high
    put_sides(where, two, side_a, side_b)


def restart_edge_kernel(where, got_a, got_b, cur, diag, ghost_diag, one_in, two_in, one, two, side_a, side_b, ghost):
    low, high = boundary(where, got_a, got_b, cur, None, None, diag, ghost_diag, one, two)
    ghost[0] = low
    ghost[1] = high
    put_sides(where, two, side_a, side_b)


def edge_kernel(where, got_a, got_b, cur, prev, old_ghost, diag, ghost_diag, one_in, two_in, one, two, side_a, side_b, ghost):
    low, high = boundary(where, got_a, got_b, cur, prev, old_ghost, diag, ghost_diag, one, two)
    ghost[0] = low
    ghost[1] = high
    put_sides(where, two, side_a, side_b)


def middle_kernel(where, got_a, got_b, cur, prev, old_ghost, diag, ghost_diag, one_in, two_in, sums, t0, t1, t2, one, two, gram):
    boundary(where, got_a, got_b, cur, prev, old_ghost, diag, ghost_diag, one, two)
    planes, ny, _ = cur.shape
    _, size = first_size(sums)
    refs = [t0, t1, t2, prev, cur, one, two]

    def load(z, y):
        return shifted([tile(ref, z, y) for ref in refs], size, FIRST + 1)

    n = FIRST + 2
    pairs = [(i, j) for j in range(1, n) for i in range(j + 1)]
    gram[...] = gram_tile(gather_sums(planes, ny, load, pairs))


def restart_kernel(where, sums, gram, *refs):
    powers = refs[: FIRST + 2]
    field, side_a, side_b, state = refs[FIRST + 2 :]
    norm, size = first_size(sums)
    ri, ci = grid_index()
    top = FIRST + 1
    mat_g = gram[...] + jnp.where((ri == 0) & (ci == 0), norm, 0.0)
    mat, mat_t = chebyshev_columns(1, FIRST)
    open_col = lambda ri, ci: jnp.where(
        ci == 0, jnp.where(ri == 0, 1.0 / size, jnp.where(ri == 1, -1.0 / size, 0.0)), 0.0
    )
    mat = mat + open_col(ri, ci)
    mat_t = mat_t + open_col(ci, ri)
    e0, e1 = unit(0), unit(1)
    x = (size * e0[0], size * e0[1])
    r = e1
    p = axpy(form(mat_g, r, r) / norm, r, e0)
    x, r, p, norm = steps(mat_g, mat, mat_t, x, r, p, FIRST)
    new = form(mat_g, r, r)
    direction = axpy(0.0, (new / norm * p[0], new / norm * p[1]), p)
    change, change_t = to_powers(size, FIRST + 1)
    coef = apply(change, change_t, r)[1]
    scale = [coef[0:1, i : i + 1] for i in range(FIRST + 2)]
    planes, ny, _ = field.shape

    def body(z, carry):
        for y in range(ny // 8):
            acc = scale[0] * tile(powers[0], z, y)
            for i in range(1, FIRST + 2):
                acc = acc + scale[i] * tile(powers[i], z, y)
            field[z, pl.ds(8 * y, 8), :] = acc
        return carry

    lax.fori_loop(0, planes, body, 0)
    put_sides(where, field, side_a, side_b)
    lead = jnp.sum(r[1] * unit(top)[1], axis=1, keepdims=True)
    e_top = unit(top)
    inverse = 1.0 / lead
    swap = tuple(e * (inverse - 1.0) - inverse * (v - lead * e) for e, v in zip(e_top, r))

    def rebase(v):
        return axpy(jnp.sum(v[1] * e_top[1], axis=1, keepdims=True), v, swap)

    p = axpy(1.0, e_top, rebase(direction))
    x = rebase(x)
    mat = mat + swap[0] * jnp.sum(jnp.where(ri == top, mat, 0.0), axis=0, keepdims=True)
    mat_t = mat_t + swap[1] * jnp.sum(jnp.where(ci == top, mat_t, 0.0), axis=1, keepdims=True)
    more, more_t = chebyshev_columns(top, SECOND)
    full = lambda v: jnp.broadcast_to(v, (ROWS, LANES))
    state[0] = jnp.where((ri < top) & (ci < top), mat_g, 0.0)
    state[1] = mat + more
    state[2] = mat_t + more_t
    state[3] = full(p[0])
    state[4] = full(p[1])
    state[5] = full(x[0])
    state[6] = full(x[1])


def late_sums_kernel(cur, prev, diag, sums, v0, t0, t1, t2, t3, t4, t5, one, two, gram):
    interior(cur, prev, diag, one, two)
    planes, ny, _ = cur.shape
    _, size = first_size(sums)
    refs = [t0, t1, t2, t3, t4, t5]
    top = FIRST + 1

    def load(z, y):
        out = shifted([tile(ref, z, y) for ref in refs], size, FIRST)
        return out + [tile(ref, z, y) for ref in (v0, prev, cur)]

    pairs = [(i, j) for j in range(top, top + 3) for i in range(j + 1)]
    gram[...] = gram_tile(gather_sums(planes, ny, load, pairs))


def last_edge_kernel(where, got_a, got_b, cur, prev, old_ghost, diag, ghost_diag, one_in, two_in, sums, early, v0, t0, t1, t2, t3, t4, t5, one, two, gram):
    boundary(where, got_a, got_b, cur, prev, old_ghost, diag, ghost_diag, one, two)
    planes, ny, _ = cur.shape
    _, size = first_size(sums)
    refs = [t0, t1, t2, t3, t4, t5]
    top = FIRST + 1

    def load(z, y):
        out = shifted([tile(ref, z, y) for ref in refs], size, FIRST)
        return out + [tile(ref, z, y) for ref in (v0, prev, cur, one, two)]

    pairs = [(i, j) for j in range(top + 3, top + 5) for i in range(j + 1)]
    gram[...] = early[...] + gram_tile(gather_sums(planes, ny, load, pairs))


def finish_kernel(sums, state, gram, t0, t1, t2, t3, t4, t5, v0, v1, v2, v3, v4, solution_field, residual):
    _, size = first_size(sums)
    ri, ci = grid_index()
    top = FIRST + 1
    mat_g = state[0] + gram[...]
    p = (state[3][:, 0:1], state[4][0:1, :])
    x = (state[5][:, 0:1], state[6][0:1, :])
    x, r, _, _ = steps(mat_g, state[1], state[2], x, unit(top), p, SECOND)
    change, change_t = to_powers(size, FIRST)
    keep = jnp.where((ri == ci) & (ri >= top), 1.0, 0.0)
    low = jnp.where(ri < top, 1.0, 0.0) * jnp.where(ci < top, 1.0, 0.0)
    change = change * low + keep
    change_t = change_t * low + keep
    cx = apply(change, change_t, x)[1]
    cr = apply(change, change_t, r)[1]
    refs = [t0, t1, t2, t3, t4, t5, v0, v1, v2, v3, v4]
    sx = [cx[0:1, i : i + 1] for i in range(len(refs))]
    sr = [cr[0:1, i : i + 1] for i in range(len(refs))]
    planes, ny, _ = t0.shape

    def body(z, carry):
        for y in range(ny // 8):
            tiles = [tile(ref, z, y) for ref in refs]
            ax, ar = sx[0] * tiles[0], sr[0] * tiles[0]
            for i in range(1, len(refs)):
                ar = ar + sr[i] * tiles[i]
                if i + 1 < len(refs):
                    ax = ax + sx[i] * tiles[i]
            solution_field[z, pl.ds(8 * y, 8), :] = ax
            residual[z, pl.ds(8 * y, 8), :] = ar
        return carry

    lax.fori_loop(0, planes, body, 0)


def pairings(count):
    first = [(i, i ^ 1) for i in range(count) if i ^ 1 < count]
    second = [(i, i + 1) for i in range(1, count - 1, 2)]
    return first, second + [(j, i) for i, j in second]


def exchange(side_a, side_b):
    first, second = pairings(lax.axis_size("slab"))
    return lax.ppermute(side_a, "slab", first), lax.ppermute(side_b, "slab", second)


def everywhere(value):
    count = lax.axis_size("slab")
    if count & (count - 1):
        return lax.psum(value, "slab")
    bit = 1
    while bit < count:
        masks = [bit] if 2 * bit >= count else [bit, 2 * bit, 3 * bit]
        others = [lax.ppermute(value, "slab", [(i, i ^ m) for i in range(count)]) for m in masks]
        for other in others:
            value = value + other
        bit *= 4
    return value


def local(right_side, diagonal):
    index = lax.axis_index("slab")
    count = lax.axis_size("slab")
    even = index % 2 == 0
    where = jnp.stack([index % 2, index > 0, index < count - 1]).astype(jnp.int32)
    field = right_side.shape
    two_planes = (2,) + field[1:]
    pair = [field, field]
    sides = [two_planes, two_planes]
    small = (ROWS, LANES)
    low = jnp.concatenate([right_side[:2], diagonal[:1]])
    high = jnp.concatenate([right_side[-2:], diagonal[-1:]])
    got = exchange(jnp.where(even, high, low), jnp.where(even, low, high))

    t0, d = right_side, diagonal
    t1, t2 = call(start_kernel, pair)(t0, d)
    t1, t2, sa, sb, ghost, gd = call(open_edge_kernel, pair + sides + [two_planes] * 2, {5: 0, 6: 1})(
        where, *got, t0, d, t1, t2
    )
    got = exchange(sa, sb)
    t3, t4, sums = call(next_sums_kernel, pair + [(8, LANES)])(t2, t1, d, t0)
    sums = everywhere(sums)
    t3, t4, sa, sb, ghost = call(edge_kernel, pair + sides + [two_planes], {8: 0, 9: 1})(
        where, *got, t2, t1, ghost, d, gd, t3, t4
    )
    got = exchange(sa, sb)
    t5, t6 = call(next_kernel, pair)(t4, t3, d)
    t5, t6, gram = call(middle_kernel, pair + [small], {8: 0, 9: 1})(
        where, *got, t4, t3, ghost, d, gd, t5, t6, sums, t0, t1, t2
    )
    gram = everywhere(gram)
    v0, sa, sb, state = call(restart_kernel, [field] + sides + [(7,) + small])(
        where, sums, gram, t0, t1, t2, t3, t4, t5, t6
    )
    got = exchange(sa, sb)
    v1, v2 = call(start_kernel, pair)(v0, d)
    v1, v2, sa, sb, ghost = call(restart_edge_kernel, pair + sides + [two_planes], {6: 0, 7: 1})(
        where, *got, v0, d, gd, v1, v2
    )
    got = exchange(sa, sb)
    v3, v4, early = call(late_sums_kernel, pair + [small])(v2, v1, d, sums, v0, t0, t1, t2, t3, t4, t5)
    v3, v4, gram = call(last_edge_kernel, pair + [small], {8: 0, 9: 1})(
        where, *got, v2, v1, ghost, d, gd, v3, v4, sums, early, v0, t0, t1, t2, t3, t4, t5
    )
    gram = everywhere(gram)
    return tuple(
        call(finish_kernel, pair)(sums, state, gram, t0, t1, t2, t3, t4, t5, v0, v1, v2, v3, v4)
    )


def solution(mesh):
    placed = (P("slab", "sys", None), P("slab", "sys", None))
    return jax.shard_map(
        local,
        mesh=mesh,
        in_specs=placed,
        out_specs=placed,
        check_vma=False,
    )
```

time: 380 us -> 103 us (0.27)
  blocking collectives: 204 us -> 0 us
  other arithmetic: 54.7 us -> 0.88 us
  between operations: 37.4 us -> 0.87 us
  Pallas kernels: 0 us -> 35.1 us
  starting transfers between devices: 59.7 us -> 38.5 us
  waiting for transfers between devices: 13.9 us -> 21.6 us
    psum x10 -> x0, blocking collectives: 204 us -> none  [merged_sums(): lax.psum((jnp.sum(residual * residual), jnp.sum(residual * applied)), 'sl...]
    pallas_call x0 -> x12, Pallas kernels: none -> 35.1 us  [run(): pl.pallas_call(kernel, out_shape=[jax.ShapeDtypeStruct(s, F32) for s in o...]
    reduce_sum x10 -> x0, other arithmetic: 24.5 us -> none  [merged_sums(): jnp.sum(residual * applied)]
    sub x10 -> x0, other arithmetic: 24.3 us -> none  [local(): residual = residual - step_size * along]
    ppermute x20 -> x22, starting transfers between devices: 59.7 us -> 38.5 us  [the longest x12 19.9 us: everywhere(): lax.ppermute(value, 'slab', [(i, i ^ m) for i in range(count)])]
    ppermute x20 -> x22, waiting for transfers between devices: 13.9 us -> 21.6 us  [the longest x12 16.7 us: everywhere(): lax.ppermute(value, 'slab', [(i, i ^ m) for i in range(count)])]
    slice x30 -> x2, local copies, waits for them, and re-layouts: 8.13 us -> 1.96 us  [local(): high = jnp.concatenate([right_side[-2:], diagonal[-1:]])]
    add x1 -> x6, other arithmetic: 5.89 us -> 0.03 us  [everywhere(): value = value + other]
  transfers between devices with their start and end apart: 20 -> 22, of which waited for: 9 -> 10; matrix products, arithmetic and copies ran while one was open for 1% -> 0% of each run, Pallas kernels for 0% -> 17%
where the time goes in v1:
time: 103 us; the launch traced here: 102 us
  starting transfers between devices  38.5 us (37%)
  Pallas kernels  35.1 us (34%)
  waiting for transfers between devices  21.6 us (21%)
  local copies, waits for them, and re-layouts  5.38 us (5%)
    pallas_call x12, Pallas kernels, run(): pl.pallas_call(kernel, out_shape=[jax.ShapeDtypeStruct(s, F32) for s in o...  35.1 us
    ppermute x12, starting transfers between devices, everywhere(): lax.ppermute(value, 'slab', [(i, i ^ m) for i in range(count)])  19.9 us
    ppermute x12, waiting for transfers between devices, everywhere(): lax.ppermute(value, 'slab', [(i, i ^ m) for i in range(count)])  16.7 us
    ppermute x5, starting transfers between devices, exchange(): lax.ppermute(side_a, 'slab', first)  15.4 us
    ppermute x5, waiting for transfers between devices, exchange(): lax.ppermute(side_a, 'slab', first)  4.92 us
    unnamed x10, local copies, waits for them, and re-layouts  3.42 us
    ppermute x5, starting transfers between devices, exchange(): lax.ppermute(side_b, 'slab', second)  3.3 us
  transfers between devices with their start and end apart: 22, of which 10 were waited for; matrix products, arithmetic and copies ran while one was open for 0% of the time, Pallas kernels for 17%

profile of v1, /device:TPU:0, one launch (start us, length us, event | category | flops | bytes accessed | tf_op | source)
XLA Modules:
  0.0 102.3 jit_solution(2604268118169794959)
XLA Ops:
  4.1 5.8 %collective-permute-start = (f32[3,128,128]{2,1,0:T(8,128)}, f32[3,128,128]{2,1,0:T(8,128)S(1)}, u32[]{:S(2)}, u32[]{:S(2)}) collective-permute-start(f32[3,128,128]{2,1,0:T(8,128)} %get-tuple-element.83), channel_id=1, source_target_pairs={{0,1},{1,0},{2,3},{3,2},{4,5},{5,4},{6,7},{7,6},{8,9},{9,8},{10,11... | collective-permute-start | bytes 589832 | tf_op jit(solution)/shard_map/ppermute | solution.py:421
  11.1 2.7 %shard_map.41 = (f32[16,128,128]{2,1,0:T(8,128)S(1)}, f32[16,128,128]{2,1,0:T(8,128)S(1)}) custom-call(f32[16,128,128]{2,1,0:T(8,128)S(1)} %copy-done.1, f32[16,128,128]{2,1,0:T(8,128)S(1)} %copy-done), custom_call_target="tpu_custom_call" | custom-call | tf_op jit(solution)/shard_map/pallas_call | solution.py:219
  14.9 3.0 %collective-permute-done.got_a = f32[3,128,128]{2,1,0:T(8,128)S(1)} collective-permute-done((f32[3,128,128]{2,1,0:T(8,128)}, f32[3,128,128]{2,1,0:T(8,128)S(1)}, u32[]{:S(2)}, u32[]{:S(2)}) %collective-permute-start) | collective-permute-done | bytes 196640 | tf_op jit(solution)/shard_map/ppermute | solution.py:421
  20.0 2.4 %collective-permute-start.6 = (f32[2,128,128]{2,1,0:T(8,128)S(1)}, f32[2,128,128]{2,1,0:T(8,128)S(1)}, u32[]{:S(2)}, u32[]{:S(2)}) collective-permute-start(f32[2,128,128]{2,1,0:T(8,128)S(1)} %get-tuple-element.45), channel_id=1, source_target_pairs={{0,1},{1,0},{2,3},{3,2},{4,5},{5,4},{6,7},{7,6},{8,9},{9,8},{10,11... | collective-permute-start | bytes 393224 | tf_op jit(solution)/shard_map/ppermute | solution.py:421
  23.1 3.1 %shard_map.43 = (f32[16,128,128]{2,1,0:T(8,128)S(1)}, f32[16,128,128]{2,1,0:T(8,128)S(1)}, f32[8,128]{1,0:T(8,128)S(1)}) custom-call(f32[16,128,128]{2,1,0:T(8,128)S(1)} %get-tuple-element.42.cur.t2.refs_2_, f32[16,128,128]{2,1,0:T(8,128)S(1)} %get-tuple-element.43.prev.t1.refs_1_, f32[16,128,128]{2,1,0:T(8,128)S(1)} %copy-done, f32[16,128,128]{2,1,0:T(8,128)S(1)} %copy-done.2), custom_call_target="tpu_custom_call" | custom-call | tf_op jit(solution)/shard_map/pallas_call | solution.py:219
  26.2 5.4 %collective-permute-start.4 = (f32[8,128]{1,0:T(8,128)S(1)}, f32[8,128]{1,0:T(8,128)S(1)}, u32[]{:S(2)}, u32[]{:S(2)}) collective-permute-start(f32[8,128]{1,0:T(8,128)S(1)} %get-tuple-element.44), channel_id=1, source_target_pairs={{0,3},{1,2},{2,1},{3,0},{4,7},{5,6},{6,5},{7,4},{8,11},{9,10},{10,... | collective-permute-start | bytes 12296 | tf_op jit(solution)/shard_map/ppermute | solution.py:431
  33.2 1.9 %collective-permute-start.8 = (f32[2,128,128]{2,1,0:T(8,128)S(1)}, f32[2,128,128]{2,1,0:T(8,128)S(1)}, u32[]{:S(2)}, u32[]{:S(2)}) collective-permute-start(f32[2,128,128]{2,1,0:T(8,128)S(1)} %get-tuple-element.51), channel_id=1, source_target_pairs={{0,1},{1,0},{2,3},{3,2},{4,5},{5,4},{6,7},{7,6},{8,9},{9,8},{10,11... | collective-permute-start | bytes 393224 | tf_op jit(solution)/shard_map/ppermute | solution.py:421
  35.8 3.8 %collective-permute-start.5 = (f32[8,128]{1,0:T(8,128)S(1)}, f32[8,128]{1,0:T(8,128)S(1)}, u32[]{:S(2)}, u32[]{:S(2)}) collective-permute-start(f32[8,128]{1,0:T(8,128)S(1)} %add_add_fusion.2), channel_id=1, source_target_pairs={{0,4},{1,5},{2,6},{3,7},{4,0},{5,1},{6,2},{7,3},{8,12},{9,13},{10,... | collective-permute-start | bytes 12296 | tf_op jit(solution)/shard_map/ppermute | solution.py:431
  39.6 2.9 %collective-permute-done.5 = f32[8,128]{1,0:T(8,128)S(1)} collective-permute-done((f32[8,128]{1,0:T(8,128)S(1)}, f32[8,128]{1,0:T(8,128)S(1)}, u32[]{:S(2)}, u32[]{:S(2)}) %collective-permute-start.5) | collective-permute-done | bytes 4128 | tf_op jit(solution)/shard_map/ppermute | solution.py:431
  42.4 2.7 %shard_map.45 = (f32[16,128,128]{2,1,0:T(8,128)S(1)}, f32[16,128,128]{2,1,0:T(8,128)S(1)}) custom-call(f32[16,128,128]{2,1,0:T(8,128)S(1)} %get-tuple-element.53.cur.refs_4_.t4, f32[16,128,128]{2,1,0:T(8,128)S(1)} %get-tuple-element.54.prev.refs_3_.t3, f32[16,128,128]{2,1,0:T(8,128)S(1)} %copy-done), custom_call_target="tpu_custom_call" | custom-call | tf_op jit(solution)/shard_map/pallas_call | solution.py:219
  45.2 3.9 %shard_map.46 = (f32[16,128,128]{2,1,0:T(8,128)S(1)}, f32[16,128,128]{2,1,0:T(8,128)S(1)}, f32[16,128]{1,0:T(8,128)S(1)}) custom-call(s32[3]{0:T(128)S(1)} %pad_add_fusion.where, f32[2,128,128]{2,1,0:T(8,128)S(1)} %collective-permute-done.8.got_a, f32[2,128,128]{2,1,0:T(8,128)S(1)} %collective-permute-done.9.got_b, ...), custom_call_target="tpu_custom_call", output_to_operand_aliasing={{0}: (8, {}), {1}: (9, {})} | custom-call | tf_op jit(solution)/shard_map/pallas_call | solution.py:219
  50.8 1.9 %collective-permute-start.11 = (f32[16,128]{1,0:T(8,128)S(1)}, f32[16,128]{1,0:T(8,128)S(1)}, u32[]{:S(2)}, u32[]{:S(2)}) collective-permute-start(f32[16,128]{1,0:T(8,128)S(1)} %get-tuple-element.58), channel_id=1, source_target_pairs={{0,2},{1,3},{2,0},{3,1},{4,6},{5,7},{6,4},{7,5},{8,10},{9,11},{10,... | collective-permute-start | bytes 24584 | tf_op jit(solution)/shard_map/ppermute | solution.py:431
  54.5 1.9 %collective-permute-done.10 = f32[16,128]{1,0:T(8,128)S(1)} collective-permute-done((f32[16,128]{1,0:T(8,128)S(1)}, f32[16,128]{1,0:T(8,128)S(1)}, u32[]{:S(2)}, u32[]{:S(2)}) %collective-permute-start.10) | collective-permute-done | bytes 8224 | tf_op jit(solution)/shard_map/ppermute | solution.py:431
  57.7 3.3 %collective-permute-done.13 = f32[16,128]{1,0:T(8,128)S(1)} collective-permute-done((f32[16,128]{1,0:T(8,128)S(1)}, f32[16,128]{1,0:T(8,128)S(1)}, u32[]{:S(2)}, u32[]{:S(2)}) %collective-permute-start.13) | collective-permute-done | bytes 8224 | tf_op jit(solution)/shard_map/ppermute | solution.py:431
  61.0 3.3 %shard_map.47 = (f32[16,128,128]{2,1,0:T(8,128)S(1)}, f32[2,128,128]{2,1,0:T(8,128)S(1)}, f32[2,128,128]{2,1,0:T(8,128)S(1)}, f32[7,16,128]{2,1,0:T(8,128)S(1)}) custom-call(s32[3]{0:T(128)S(1)} %pad_add_fusion.where, f32[8,128]{1,0:T(8,128)S(1)} %add.45.sums, f32[16,128]{1,0:T(8,128)S(1)} %add.49.gram, f32[16,128,128]{2,1,0:T(8,128)S(1)} %copy-done.2, ...), custom_call_target="tpu_custom_call" | custom-call | tf_op jit(solution)/shard_map/pallas_call | solution.py:219
  65.1 2.7 %shard_map.48 = (f32[16,128,128]{2,1,0:T(8,128)S(1)}, f32[16,128,128]{2,1,0:T(8,128)S(1)}) custom-call(f32[16,128,128]{2,1,0:T(8,128)S(1)} %get-tuple-element.64.cur.v0, f32[16,128,128]{2,1,0:T(8,128)S(1)} %copy-done), custom_call_target="tpu_custom_call" | custom-call | tf_op jit(solution)/shard_map/pallas_call | solution.py:219
  67.8 1.9 %collective-permute-done.14.got_a = f32[2,128,128]{2,1,0:T(8,128)S(1)} collective-permute-done((f32[2,128,128]{2,1,0:T(8,128)S(1)}, f32[2,128,128]{2,1,0:T(8,128)S(1)}, u32[]{:S(2)}, u32[]{:S(2)}) %collective-permute-start.14) | collective-permute-done | bytes 131104 | tf_op jit(solution)/shard_map/ppermute | solution.py:421
  70.7 5.1 %collective-permute-start.16 = (f32[2,128,128]{2,1,0:T(8,128)S(1)}, f32[2,128,128]{2,1,0:T(8,128)S(1)}, u32[]{:S(2)}, u32[]{:S(2)}) collective-permute-start(f32[2,128,128]{2,1,0:T(8,128)S(1)} %get-tuple-element.67), channel_id=1, source_target_pairs={{0,1},{1,0},{2,3},{3,2},{4,5},{5,4},{6,7},{7,6},{8,9},{9,8},{10,11... | collective-permute-start | bytes 393224 | tf_op jit(solution)/shard_map/ppermute | solution.py:421
  76.5 5.4 %shard_map.50 = (f32[16,128,128]{2,1,0:T(8,128)S(1)}, f32[16,128,128]{2,1,0:T(8,128)S(1)}, f32[16,128]{1,0:T(8,128)S(1)}) custom-call(f32[16,128,128]{2,1,0:T(8,128)S(1)} %get-tuple-element.69.cur.v2, f32[16,128,128]{2,1,0:T(8,128)S(1)} %get-tuple-element.70.prev.v1, f32[16,128,128]{2,1,0:T(8,128)S(1)} %copy-done, f32[8,128]{1,0:T(8,128)S(1)} %add.45.sums, ...), custom_call_target="tpu_custom_call" | custom-call | tf_op jit(solution)/shard_map/pallas_call | solution.py:219
  81.9 3.3 %shard_map.51 = (f32[16,128,128]{2,1,0:T(8,128)S(1)}, f32[16,128,128]{2,1,0:T(8,128)S(1)}, f32[16,128]{1,0:T(8,128)S(1)}) custom-call(s32[3]{0:T(128)S(1)} %pad_add_fusion.where, f32[2,128,128]{2,1,0:T(8,128)S(1)} %collective-permute-done.16.got_a, f32[2,128,128]{2,1,0:T(8,128)S(1)} %collective-permute-done.17.got_b, ...), custom_call_target="tpu_custom_call", output_to_operand_aliasing={{0}: (8, {}), {1}: (9, {})} | custom-call | tf_op jit(solution)/shard_map/pallas_call | solution.py:219
  85.2 3.7 %collective-permute-start.20 = (f32[16,128]{1,0:T(8,128)S(1)}, f32[16,128]{1,0:T(8,128)S(1)}, u32[]{:S(2)}, u32[]{:S(2)}) collective-permute-start(f32[16,128]{1,0:T(8,128)S(1)} %get-tuple-element.75), channel_id=1, source_target_pairs={{0,3},{1,2},{2,1},{3,0},{4,7},{5,6},{6,5},{7,4},{8,11},{9,10},{10,... | collective-permute-start | bytes 24584 | tf_op jit(solution)/shard_map/ppermute | solution.py:431
  90.5 2.0 %collective-permute-done.19 = f32[16,128]{1,0:T(8,128)S(1)} collective-permute-done((f32[16,128]{1,0:T(8,128)S(1)}, f32[16,128]{1,0:T(8,128)S(1)}, u32[]{:S(2)}, u32[]{:S(2)}) %collective-permute-start.19) | collective-permute-done | bytes 8224 | tf_op jit(solution)/shard_map/ppermute | solution.py:431
  93.3 3.9 %collective-permute-done.21 = f32[16,128]{1,0:T(8,128)S(1)} collective-permute-done((f32[16,128]{1,0:T(8,128)S(1)}, f32[16,128]{1,0:T(8,128)S(1)}, u32[]{:S(2)}, u32[]{:S(2)}) %collective-permute-start.21) | collective-permute-done | bytes 8224 | tf_op jit(solution)/shard_map/ppermute | solution.py:431
  97.2 5.2 %shard_map.52 = (f32[16,128,128]{2,1,0:T(8,128)}, f32[16,128,128]{2,1,0:T(8,128)}) custom-call(f32[8,128]{1,0:T(8,128)S(1)} %add.45.sums, f32[7,16,128]{2,1,0:T(8,128)S(1)} %get-tuple-element.61.state, f32[16,128]{1,0:T(8,128)S(1)} %add.53.gram, f32[16,128,128]{2,1,0:T(8,128)S(1)} %copy-done.2, f32[16,128,128]{2,1,0:T(8,128)S(1)} %get-tuple-element.43.prev.t1.refs_1_, ...), custom_call_target="tpu_custom_call" | custom-call | tf_op jit(solution)/shard_map/pallas_call | solution.py:219
  (52 shorter events, 20.3 us)
Async XLA Ops:
  0.6 9.2 %copy-start = (f32[16,128,128]{2,1,0:T(8,128)S(1)}, f32[16,128,128]{2,1,0:T(8,128)}, u32[]{:S(2)}) copy-start(f32[16,128,128]{2,1,0:T(8,128)} %diag.19) | copy-start | bytes 3145732
  3.4 11.5 %collective-permute-start.1 = (f32[3,128,128]{2,1,0:T(8,128)}, f32[3,128,128]{2,1,0:T(8,128)S(1)}, u32[]{:S(2)}, u32[]{:S(2)}) collective-permute-start(f32[3,128,128]{2,1,0:T(8,128)} %get-tuple-element.82), channel_id=1, source_target_pairs={{1,2},{3,4},{5,6},{2,1},{4,3},{6,5},{9,10},{11,12},{13,14},{10,9},... | collective-permute-start | bytes 589832 | tf_op jit(solution)/shard_map/ppermute | solution.py:421
  4.1 13.8 %collective-permute-start = (f32[3,128,128]{2,1,0:T(8,128)}, f32[3,128,128]{2,1,0:T(8,128)S(1)}, u32[]{:S(2)}, u32[]{:S(2)}) collective-permute-start(f32[3,128,128]{2,1,0:T(8,128)} %get-tuple-element.83), channel_id=1, source_target_pairs={{0,1},{1,0},{2,3},{3,2},{4,5},{5,4},{6,7},{7,6},{8,9},{9,8},{10,11... | collective-permute-start | bytes 589832 | tf_op jit(solution)/shard_map/ppermute | solution.py:421
  11.1 6.8 %copy-start.2 = (f32[16,128,128]{2,1,0:T(8,128)S(1)}, f32[16,128,128]{2,1,0:T(8,128)}, u32[]{:S(2)}) copy-start(f32[16,128,128]{2,1,0:T(8,128)} %t0.7) | copy-start | bytes 3145732
  20.0 12.2 %collective-permute-start.6 = (f32[2,128,128]{2,1,0:T(8,128)S(1)}, f32[2,128,128]{2,1,0:T(8,128)S(1)}, u32[]{:S(2)}, u32[]{:S(2)}) collective-permute-start(f32[2,128,128]{2,1,0:T(8,128)S(1)} %get-tuple-element.45), channel_id=1, source_target_pairs={{0,1},{1,0},{2,3},{3,2},{4,5},{5,4},{6,7},{7,6},{8,9},{9,8},{10,11... | collective-permute-start | bytes 393224 | tf_op jit(solution)/shard_map/ppermute | solution.py:421
  22.5 9.8 %collective-permute-start.7 = (f32[2,128,128]{2,1,0:T(8,128)S(1)}, f32[2,128,128]{2,1,0:T(8,128)S(1)}, u32[]{:S(2)}, u32[]{:S(2)}) collective-permute-start(f32[2,128,128]{2,1,0:T(8,128)S(1)} %get-tuple-element.46), channel_id=1, source_target_pairs={{1,2},{3,4},{5,6},{2,1},{4,3},{6,5},{9,10},{11,12},{13,14},{10,9},... | collective-permute-start | bytes 393224 | tf_op jit(solution)/shard_map/ppermute | solution.py:421
  26.2 9.5 %collective-permute-start.4 = (f32[8,128]{1,0:T(8,128)S(1)}, f32[8,128]{1,0:T(8,128)S(1)}, u32[]{:S(2)}, u32[]{:S(2)}) collective-permute-start(f32[8,128]{1,0:T(8,128)S(1)} %get-tuple-element.44), channel_id=1, source_target_pairs={{0,3},{1,2},{2,1},{3,0},{4,7},{5,6},{6,5},{7,4},{8,11},{9,10},{10,... | collective-permute-start | bytes 12296 | tf_op jit(solution)/shard_map/ppermute | solution.py:431
  31.6 4.2 %collective-permute-start.3 = (f32[8,128]{1,0:T(8,128)S(1)}, f32[8,128]{1,0:T(8,128)S(1)}, u32[]{:S(2)}, u32[]{:S(2)}) collective-permute-start(f32[8,128]{1,0:T(8,128)S(1)} %get-tuple-element.44), channel_id=1, source_target_pairs={{0,2},{1,3},{2,0},{3,1},{4,6},{5,7},{6,4},{7,5},{8,10},{9,11},{10,... | collective-permute-start | bytes 12296 | tf_op jit(solution)/shard_map/ppermute | solution.py:431
  32.0 3.7 %collective-permute-start.2 = (f32[8,128]{1,0:T(8,128)S(1)}, f32[8,128]{1,0:T(8,128)S(1)}, u32[]{:S(2)}, u32[]{:S(2)}) collective-permute-start(f32[8,128]{1,0:T(8,128)S(1)} %get-tuple-element.44), channel_id=1, source_target_pairs={{0,1},{1,0},{2,3},{3,2},{4,5},{5,4},{6,7},{7,6},{8,9},{9,8},{10,11... | collective-permute-start | bytes 12296 | tf_op jit(solution)/shard_map/ppermute | solution.py:431
  33.2 12.0 %collective-permute-start.8 = (f32[2,128,128]{2,1,0:T(8,128)S(1)}, f32[2,128,128]{2,1,0:T(8,128)S(1)}, u32[]{:S(2)}, u32[]{:S(2)}) collective-permute-start(f32[2,128,128]{2,1,0:T(8,128)S(1)} %get-tuple-element.51), channel_id=1, source_target_pairs={{0,1},{1,0},{2,3},{3,2},{4,5},{5,4},{6,7},{7,6},{8,9},{9,8},{10,11... | collective-permute-start | bytes 393224 | tf_op jit(solution)/shard_map/ppermute | solution.py:421
  35.1 10.1 %collective-permute-start.9 = (f32[2,128,128]{2,1,0:T(8,128)S(1)}, f32[2,128,128]{2,1,0:T(8,128)S(1)}, u32[]{:S(2)}, u32[]{:S(2)}) collective-permute-start(f32[2,128,128]{2,1,0:T(8,128)S(1)} %get-tuple-element.52), channel_id=1, source_target_pairs={{1,2},{3,4},{5,6},{2,1},{4,3},{6,5},{9,10},{11,12},{13,14},{10,9},... | collective-permute-start | bytes 393224 | tf_op jit(solution)/shard_map/ppermute | solution.py:421
  35.8 6.7 %collective-permute-start.5 = (f32[8,128]{1,0:T(8,128)S(1)}, f32[8,128]{1,0:T(8,128)S(1)}, u32[]{:S(2)}, u32[]{:S(2)}) collective-permute-start(f32[8,128]{1,0:T(8,128)S(1)} %add_add_fusion.2), channel_id=1, source_target_pairs={{0,4},{1,5},{2,6},{3,7},{4,0},{5,1},{6,2},{7,3},{8,12},{9,13},{10,... | collective-permute-start | bytes 12296 | tf_op jit(solution)/shard_map/ppermute | solution.py:431
  49.1 4.6 %collective-permute-start.12 = (f32[16,128]{1,0:T(8,128)S(1)}, f32[16,128]{1,0:T(8,128)S(1)}, u32[]{:S(2)}, u32[]{:S(2)}) collective-permute-start(f32[16,128]{1,0:T(8,128)S(1)} %get-tuple-element.58), channel_id=1, source_target_pairs={{0,3},{1,2},{2,1},{3,0},{4,7},{5,6},{6,5},{7,4},{8,11},{9,10},{10,... | collective-permute-start | bytes 24584 | tf_op jit(solution)/shard_map/ppermute | solution.py:431
  50.8 3.7 %collective-permute-start.11 = (f32[16,128]{1,0:T(8,128)S(1)}, f32[16,128]{1,0:T(8,128)S(1)}, u32[]{:S(2)}, u32[]{:S(2)}) collective-permute-start(f32[16,128]{1,0:T(8,128)S(1)} %get-tuple-element.58), channel_id=1, source_target_pairs={{0,2},{1,3},{2,0},{3,1},{4,6},{5,7},{6,4},{7,5},{8,10},{9,11},{10,... | collective-permute-start | bytes 24584 | tf_op jit(solution)/shard_map/ppermute | solution.py:431
  52.8 3.7 %collective-permute-start.10 = (f32[16,128]{1,0:T(8,128)S(1)}, f32[16,128]{1,0:T(8,128)S(1)}, u32[]{:S(2)}, u32[]{:S(2)}) collective-permute-start(f32[16,128]{1,0:T(8,128)S(1)} %get-tuple-element.58), channel_id=1, source_target_pairs={{0,1},{1,0},{2,3},{3,2},{4,5},{5,4},{6,7},{7,6},{8,9},{9,8},{10,11... | collective-permute-start | bytes 24584 | tf_op jit(solution)/shard_map/ppermute | solution.py:431
  56.4 4.5 %collective-permute-start.13 = (f32[16,128]{1,0:T(8,128)S(1)}, f32[16,128]{1,0:T(8,128)S(1)}, u32[]{:S(2)}, u32[]{:S(2)}) collective-permute-start(f32[16,128]{1,0:T(8,128)S(1)} %add_add_fusion.1), channel_id=1, source_target_pairs={{0,4},{1,5},{2,6},{3,7},{4,0},{5,1},{6,2},{7,3},{8,12},{9,13},{10,... | collective-permute-start | bytes 24584 | tf_op jit(solution)/shard_map/ppermute | solution.py:431
  64.3 5.4 %collective-permute-start.14 = (f32[2,128,128]{2,1,0:T(8,128)S(1)}, f32[2,128,128]{2,1,0:T(8,128)S(1)}, u32[]{:S(2)}, u32[]{:S(2)}) collective-permute-start(f32[2,128,128]{2,1,0:T(8,128)S(1)} %get-tuple-element.62), channel_id=1, source_target_pairs={{0,1},{1,0},{2,3},{3,2},{4,5},{5,4},{6,7},{7,6},{8,9},{9,8},{10,11... | collective-permute-start | bytes 393224 | tf_op jit(solution)/shard_map/ppermute | solution.py:421
  64.4 5.4 %collective-permute-start.15 = (f32[2,128,128]{2,1,0:T(8,128)S(1)}, f32[2,128,128]{2,1,0:T(8,128)S(1)}, u32[]{:S(2)}, u32[]{:S(2)}) collective-permute-start(f32[2,128,128]{2,1,0:T(8,128)S(1)} %get-tuple-element.63), channel_id=1, source_target_pairs={{1,2},{3,4},{5,6},{2,1},{4,3},{6,5},{9,10},{11,12},{13,14},{10,9},... | collective-permute-start | bytes 393224 | tf_op jit(solution)/shard_map/ppermute | solution.py:421
  70.7 11.2 %collective-permute-start.16 = (f32[2,128,128]{2,1,0:T(8,128)S(1)}, f32[2,128,128]{2,1,0:T(8,128)S(1)}, u32[]{:S(2)}, u32[]{:S(2)}) collective-permute-start(f32[2,128,128]{2,1,0:T(8,128)S(1)} %get-tuple-element.67), channel_id=1, source_target_pairs={{0,1},{1,0},{2,3},{3,2},{4,5},{5,4},{6,7},{7,6},{8,9},{9,8},{10,11... | collective-permute-start | bytes 393224 | tf_op jit(solution)/shard_map/ppermute | solution.py:421
  75.9 6.0 %collective-permute-start.17 = (f32[2,128,128]{2,1,0:T(8,128)S(1)}, f32[2,128,128]{2,1,0:T(8,128)S(1)}, u32[]{:S(2)}, u32[]{:S(2)}) collective-permute-start(f32[2,128,128]{2,1,0:T(8,128)S(1)} %get-tuple-element.68), channel_id=1, source_target_pairs={{1,2},{3,4},{5,6},{2,1},{4,3},{6,5},{9,10},{11,12},{13,14},{10,9},... | collective-permute-start | bytes 393224 | tf_op jit(solution)/shard_map/ppermute | solution.py:421
  85.2 5.3 %collective-permute-start.20 = (f32[16,128]{1,0:T(8,128)S(1)}, f32[16,128]{1,0:T(8,128)S(1)}, u32[]{:S(2)}, u32[]{:S(2)}) collective-permute-start(f32[16,128]{1,0:T(8,128)S(1)} %get-tuple-element.75), channel_id=1, source_target_pairs={{0,3},{1,2},{2,1},{3,0},{4,7},{5,6},{6,5},{7,4},{8,11},{9,10},{10,... | collective-permute-start | bytes 24584 | tf_op jit(solution)/shard_map/ppermute | solution.py:431
  88.9 3.7 %collective-permute-start.19 = (f32[16,128]{1,0:T(8,128)S(1)}, f32[16,128]{1,0:T(8,128)S(1)}, u32[]{:S(2)}, u32[]{:S(2)}) collective-permute-start(f32[16,128]{1,0:T(8,128)S(1)} %get-tuple-element.75), channel_id=1, source_target_pairs={{0,2},{1,3},{2,0},{3,1},{4,6},{5,7},{6,4},{7,5},{8,10},{9,11},{10,... | collective-permute-start | bytes 24584 | tf_op jit(solution)/shard_map/ppermute | solution.py:431
  88.9 3.7 %collective-permute-start.18 = (f32[16,128]{1,0:T(8,128)S(1)}, f32[16,128]{1,0:T(8,128)S(1)}, u32[]{:S(2)}, u32[]{:S(2)}) collective-permute-start(f32[16,128]{1,0:T(8,128)S(1)} %get-tuple-element.75), channel_id=1, source_target_pairs={{0,1},{1,0},{2,3},{3,2},{4,5},{5,4},{6,7},{7,6},{8,9},{9,8},{10,11... | collective-permute-start | bytes 24584 | tf_op jit(solution)/shard_map/ppermute | solution.py:431
  92.6 4.6 %collective-permute-start.21 = (f32[16,128]{1,0:T(8,128)S(1)}, f32[16,128]{1,0:T(8,128)S(1)}, u32[]{:S(2)}, u32[]{:S(2)}) collective-permute-start(f32[16,128]{1,0:T(8,128)S(1)} %add_add_fusion), channel_id=1, source_target_pairs={{0,4},{1,5},{2,6},{3,7},{4,0},{5,1},{6,2},{7,3},{8,12},{9,13},{10,... | collective-permute-start | bytes 24584 | tf_op jit(solution)/shard_map/ppermute | solution.py:431
  (3 other events, 3.4 us)

commit v2 on v0

v2 whole, which is shorter than its diff:
```python
import functools

import jax
import jax.numpy as jnp
from jax import lax
from jax.experimental import pallas as pl
from jax.experimental.pallas import tpu as pltpu
from jax.sharding import PartitionSpec as P

FIRST = 5
SECOND = 4
LOW, HIGH = 0.25, 14.0
CENTER = (LOW + HIGH) / 2
HALF = (HIGH - LOW) / 2
ROWS, LANES = 16, 128
F32 = jnp.float32


def tile(at, row):
    ref, z = at
    return ref[z, pl.ds(row, 8), :]


def advance(out, cur, above, below, scale, prev=None, keep=None):
    _, ny, nx = cur[0].shape
    row = lax.broadcasted_iota(jnp.int32, (8, nx), 0)
    lane = lax.broadcasted_iota(jnp.int32, (8, nx), 1)
    zero = jnp.zeros((8, nx), F32)
    for at in range(0, ny, 8):
        mid = tile(cur, at)
        beside = tile(above, at) + tile(below, at)
        if at:
            beside = beside + tile(cur, at - 1)
        else:
            beside = beside + jnp.where(row == 0, zero, pltpu.roll(mid, 1, 0))
        if at + 8 < ny:
            beside = beside + tile(cur, at + 1)
        else:
            beside = beside + jnp.where(row == 7, zero, pltpu.roll(mid, 7, 0))
        left = jnp.where(lane == 0, zero, pltpu.roll(mid, 1, 1))
        right = jnp.where(lane == nx - 1, zero, pltpu.roll(mid, nx - 1, 1))
        beside = beside + (left + right)
        image = tile(scale, at) * mid - (2.0 / HALF) * beside
        image = 0.5 * image if prev is None else image - tile(prev, at)
        if keep is not None:
            image = image * keep
        out[0][out[1], pl.ds(at, 8), :] = image


def scaled(diag):
    return (2.0 / HALF) * diag + (2.0 / HALF) * (6.0 - CENTER)


def over(first, last, most, body):
    count = last - first
    step = max(k for k in range(1, most + 1) if count % k == 0)

    def run(i, carry):
        for k in range(step):
            body(first + i * step + k)
        return carry

    lax.fori_loop(0, count // step, run, 0)


def interior(cur, prev, scale, one, two):
    planes = cur.shape[0]

    def inner(z):
        old = None if prev is None else (prev, z)
        advance((one, z), (cur, z), (cur, z + 1), (cur, z - 1), (scale, z), old)

    def outer(z):
        advance((two, z), (one, z), (one, z + 1), (one, z - 1), (scale, z), (cur, z))

    over(1, planes - 1, 7, inner)
    over(2, planes - 2, 6, outer)


def boundary(where, got_a, got_b, cur, prev, old_ghost, scale, ghost_scale, one, two, ghost, near):
    last = cur.shape[0] - 1
    even = where[0] == 0
    has_low = where[1].astype(F32)
    has_high = where[2].astype(F32)
    for k in range(2):
        near[k] = jnp.where(even, got_b[k], got_a[k])
        near[2 + k] = jnp.where(even, got_a[k], got_b[k])
    old = lambda ref, k: None if ref is None else (ref, k)
    advance((ghost, 0), (near, 1), (cur, 0), (near, 0), (ghost_scale, 0), old(old_ghost, 0), has_low)
    advance((ghost, 1), (near, 2), (near, 3), (cur, last), (ghost_scale, 1), old(old_ghost, 1), has_high)
    advance((one, 0), (cur, 0), (cur, 1), (near, 1), (scale, 0), old(prev, 0))
    advance((one, last), (cur, last), (near, 2), (cur, last - 1), (scale, last), old(prev, last))
    advance((two, 0), (one, 0), (one, 1), (ghost, 0), (scale, 0), (cur, 0))
    advance((two, 1), (one, 1), (one, 2), (one, 0), (scale, 1), (cur, 1))
    advance((two, last), (one, last), (ghost, 1), (one, last - 1), (scale, last), (cur, last))
    top = last - 1
    advance((two, top), (one, top), (one, last), (one, top - 1), (scale, top), (cur, top))


def put_sides(where, field, side_a, side_b):
    even = where[0] == 0
    last = field.shape[0] - 1
    for k in range(2):
        low, high = field[k], field[last - 1 + k]
        side_a[k] = jnp.where(even, high, low)
        side_b[k] = jnp.where(even, low, high)


def row_index():
    return lax.broadcasted_iota(jnp.int32, (ROWS, LANES), 0)


def unit(k):
    return jnp.where(row_index() == k, 1.0, 0.0).astype(F32)


def entry(v, k):
    return jnp.broadcast_to(v[k : k + 1, :], (ROWS, LANES))


def columns(mat, count):
    return [jnp.broadcast_to(mat[:, j : j + 1], (ROWS, LANES)) for j in range(count)]


def product(cols, v):
    return functools.reduce(lambda a, b: a + b, [c * entry(v, k) for k, c in enumerate(cols)])


def dot(a, b):
    return jnp.broadcast_to(jnp.sum(a * b, axis=0, keepdims=True), (ROWS, LANES))


def steps(gram, mat, x, r, p, count):
    norm = dot(r, product(gram, r))
    for _ in range(count):
        image = product(mat, p)
        size = norm / dot(p, product(gram, image))
        x = x + size * p
        r = r - size * image
        new = dot(r, product(gram, r))
        last = (new / norm) * p
        p = r + last
        norm = new
    return x, r, last


def chebyshev_column(first, k):
    out = CENTER * unit(k) + (HALF if k == first else HALF / 2) * unit(k + 1)
    return out if k == first else out + (HALF / 2) * unit(k - 1)


def to_powers(size, count):
    cols = [unit(0)]
    for j in range(count):
        cols.append(unit(j) - size * chebyshev_column(0, j))
    return cols


def gram_tile(rows):
    ri = row_index()
    ci = lax.broadcasted_iota(jnp.int32, (ROWS, LANES), 1)
    out = jnp.zeros((ROWS, LANES), F32)
    blank = jnp.zeros((1, LANES), F32)
    for j in sorted({j for _, j in rows}):
        stack = jnp.concatenate([rows.get((i, j), blank) for i in range(ROWS)], axis=0)
        col = jnp.sum(stack, axis=1, keepdims=True)
        out = out + jnp.where(ci == j, col, 0.0)
        row = jnp.sum(jnp.where(ri == ci, col, 0.0), axis=0, keepdims=True)
        out = out + jnp.where((ri == j) & (ci < j), row, 0.0)
    return out


def inner_products(first, last, ny, load, pairs, acc):
    zero = jnp.zeros(acc.shape[1:], F32)
    for k in range(len(pairs)):
        acc[k] = zero

    def body(z, carry):
        sums = [None] * len(pairs)
        for row in range(0, ny, 8):
            tiles = load(z, row)
            for k, (i, j) in enumerate(pairs):
                part = tiles[i] * tiles[j]
                sums[k] = part if row == 0 else sums[k] + part
        for k, val in enumerate(sums):
            acc[k] = acc[k] + val
        return carry

    lax.fori_loop(first, last, body, 0)
    return {pair: jnp.sum(acc[k], axis=0, keepdims=True) for k, pair in enumerate(pairs)}


def pairs_of(first, last):
    return [(i, j) for j in range(first, last) for i in range(j + 1)]


def shifted(powers, size, count):
    keep = 1.0 - size * CENTER
    move = size * (HALF / 2)
    out = [powers[0], keep * powers[0] - (2.0 * move) * powers[1]]
    for j in range(1, count):
        out.append(keep * powers[j] - move * (powers[j + 1] + powers[j - 1]))
    return out


def first_size(sums):
    norm = jnp.sum(sums[0:1, :], axis=1, keepdims=True)
    cross = jnp.sum(sums[1:2, :], axis=1, keepdims=True)
    return norm / (CENTER * norm + HALF * cross)


def gathered(ref):
    return functools.reduce(lambda a, b: a + b, [ref[k] for k in range(ref.shape[0])])


def spread(ref, value):
    for k in range(ref.shape[0]):
        ref[k] = value


def call(kernel, outs, aliases=None, scratch=(), hbm=False):
    def spec(a):
        if a.dtype == jnp.int32:
            return pl.BlockSpec(memory_space=pltpu.SMEM)
        return pl.BlockSpec(memory_space=pltpu.HBM if hbm else pltpu.VMEM)

    def run(*args):
        return pl.pallas_call(
            kernel,
            out_shape=[jax.ShapeDtypeStruct(s, F32) for s in outs],
            in_specs=[spec(a) for a in args],
            out_specs=[pl.BlockSpec(memory_space=pltpu.VMEM) for _ in outs],
            scratch_shapes=list(scratch),
            input_output_aliases=aliases or {},
            compiler_params=pltpu.CompilerParams(vmem_limit_bytes=16 << 20),
        )(*args)

    return run


def side_kernel(where, rhs, diag, side_a, side_b, sems):
    even = where[0] == 0
    last = rhs.shape[0] - 1
    copies = []
    for k, (side, high) in enumerate(((side_a, even), (side_b, jnp.logical_not(even)))):
        field_at = jnp.where(high, last - 1, 0)
        diag_at = jnp.where(high, last, 0)
        copies.append(pltpu.make_async_copy(rhs.at[pl.ds(field_at, 2)], side.at[pl.ds(0, 2)], sems.at[2 * k]))
        copies.append(pltpu.make_async_copy(diag.at[pl.ds(diag_at, 1)], side.at[pl.ds(2, 1)], sems.at[2 * k + 1]))
    for copy in copies:
        copy.start()
    for copy in copies:
        copy.wait()


def open_kernel(rhs, diag, scale, one, two, sums, acc):
    planes, ny, _ = rhs.shape

    def fill(z):
        scale[z] = scaled(diag[z])

    over(0, planes, 4, fill)
    interior(rhs, None, scale, one, two)
    load = lambda z, row: [tile((rhs, z), row), tile((one, z), row)]
    rows = inner_products(1, planes - 1, ny, load, [(0, 0), (0, 1)], acc)
    blank = jnp.zeros((6, LANES), F32)
    spread(sums, jnp.concatenate([rows[0, 0], rows[0, 1], blank], axis=0))


def open_edge_kernel(where, got_a, got_b, cur, scale, sums, one_in, two_in, one, two, side_a, side_b, ghost, ghost_scale, size, near):
    even = where[0] == 0
    ghost_scale[0] = scaled(jnp.where(even, got_b[2], got_a[2]))
    ghost_scale[1] = scaled(jnp.where(even, got_a[2], got_b[2]))
    boundary(where, got_a, got_b, cur, None, None, scale, ghost_scale, one, two, ghost, near)
    put_sides(where, two, side_a, side_b)
    size[...] = jnp.broadcast_to(first_size(gathered(sums)), (8, LANES))


def restart_edge_kernel(where, got_a, got_b, cur, scale, ghost_scale, one_in, two_in, one, two, side_a, side_b, ghost, near):
    boundary(where, got_a, got_b, cur, None, None, scale, ghost_scale, one, two, ghost, near)
    put_sides(where, two, side_a, side_b)


def next_kernel(cur, prev, scale, one, two):
    interior(cur, prev, scale, one, two)


def edge_kernel(where, got_a, got_b, cur, prev, old_ghost, scale, ghost_scale, one_in, two_in, one, two, side_a, side_b, ghost, near):
    boundary(where, got_a, got_b, cur, prev, old_ghost, scale, ghost_scale, one, two, ghost, near)
    put_sides(where, two, side_a, side_b)


def partial_gram(field, vectors, size, count, extra, pairs, acc):
    planes, ny, _ = field.shape

    def load(z, row):
        powers = [tile((ref, z), row) for ref in vectors]
        return shifted(powers, size, count) + [tile((ref, z), row) for ref in extra]

    return gram_tile(inner_products(0, planes, ny, load, pairs, acc))


def third_kernel(cur, prev, scale, size, t0, t1, t2, one, two, gram, acc):
    interior(cur, prev, scale, one, two)
    gram[...] = partial_gram(cur, [t0, t1, t2, prev, cur], size[0:1, 0:1], FIRST - 1, [], pairs_of(0, FIRST), acc)


def third_edge_kernel(where, got_a, got_b, cur, prev, old_ghost, scale, ghost_scale, one_in, two_in, size, early, t0, t1, t2, one, two, gram, ghost, near, acc):
    boundary(where, got_a, got_b, cur, prev, old_ghost, scale, ghost_scale, one, two, ghost, near)
    late = partial_gram(
        cur, [t0, t1, t2, prev, cur, one, two], size[0:1, 0:1], FIRST + 1, [], pairs_of(FIRST, FIRST + 2), acc
    )
    spread(gram, early[...] + late)


def restart_kernel(where, size, gram, *refs):
    powers = refs[: FIRST + 2]
    field, side_a, side_b, state = refs[FIRST + 2 :]
    size = size[0:1, 0:1]
    top = FIRST + 1
    full = gathered(gram)
    mat = [(1.0 / size) * (unit(0) - unit(1))] + [chebyshev_column(1, k) for k in range(1, top)]
    zero = jnp.zeros((ROWS, LANES), F32)
    x, r, last = steps(columns(full, top + 1), mat, zero, unit(0), unit(0), top)
    coef = product(to_powers(size, top), r)
    scale = [coef[i : i + 1, :] for i in range(top + 1)]
    planes, ny, _ = field.shape

    def body(z, carry):
        for row in range(0, ny, 8):
            out = scale[0] * tile((powers[0], z), row)
            for i in range(1, top + 1):
                out = out + scale[i] * tile((powers[i], z), row)
            field[z, pl.ds(row, 8), :] = out
        return carry

    lax.fori_loop(0, planes, body, 0)
    put_sides(where, field, side_a, side_b)
    ri = row_index()
    ci = lax.broadcasted_iota(jnp.int32, (ROWS, LANES), 1)
    inverse = 1.0 / entry(r, top)
    swap = jnp.where(ri == top, inverse, -inverse * r)
    rebase = lambda v: jnp.where(ri == top, 0.0, v) + entry(v, top) * swap
    state[0] = jnp.where((ri < top) & (ci < top), full, 0.0)
    state[1] = unit(top) + rebase(last)
    state[2] = rebase(x)
    state[3] = swap


def fourth_kernel(cur, scale, size, t0, t1, t2, t3, t4, t5, one, two, gram, acc):
    interior(cur, None, scale, one, two)
    top = FIRST + 1
    gram[...] = partial_gram(
        cur, [t0, t1, t2, t3, t4, t5], size[0:1, 0:1], FIRST, [cur], pairs_of(top, top + 1), acc
    )


def fifth_kernel(cur, prev, scale, size, early, v0, t0, t1, t2, t3, t4, t5, one, two, gram, acc):
    interior(cur, prev, scale, one, two)
    top = FIRST + 1
    gram[...] = early[...] + partial_gram(
        cur, [t0, t1, t2, t3, t4, t5], size[0:1, 0:1], FIRST, [v0, prev, cur], pairs_of(top + 1, top + 3), acc
    )


def fifth_edge_kernel(where, got_a, got_b, cur, prev, old_ghost, scale, ghost_scale, one_in, two_in, size, early, v0, t0, t1, t2, t3, t4, t5, one, two, gram, ghost, near, acc):
    boundary(where, got_a, got_b, cur, prev, old_ghost, scale, ghost_scale, one, two, ghost, near)
    top = FIRST + 1
    late = partial_gram(
        cur, [t0, t1, t2, t3, t4, t5], size[0:1, 0:1], FIRST, [v0, prev, cur, one, two], pairs_of(top + 3, top + 5), acc
    )
    spread(gram, early[...] + late)


def finish_kernel(size, state, gram, *refs):
    top = FIRST + 1
    count = top + SECOND + 1
    refs, (solution_field, residual) = refs[:count], refs[count:]
    size = size[0:1, 0:1]
    mat = [(1.0 / size) * (unit(0) - unit(1))] + [chebyshev_column(1, k) for k in range(1, top - 1)]
    mat.append(CENTER * unit(top - 1) + (HALF / 2) * (unit(top - 2) + state[3]))
    mat += [chebyshev_column(top, k) for k in range(top, top + SECOND)]
    full = state[0] + gathered(gram)
    x, r, _ = steps(columns(full, count), mat, state[2], unit(top), state[1], SECOND)
    back = to_powers(size, FIRST) + [unit(k) for k in range(top, count)]
    x, r = product(back, x), product(back, r)
    sx = [x[i : i + 1, :] for i in range(count)]
    sr = [r[i : i + 1, :] for i in range(count)]
    planes, ny, _ = solution_field.shape

    def body(z, carry):
        for row in range(0, ny, 8):
            tiles = [tile((ref, z), row) for ref in refs]
            ax, ar = sx[0] * tiles[0], sr[0] * tiles[0]
            for i in range(1, count):
                ar = ar + sr[i] * tiles[i]
                if i + 1 < count:
                    ax = ax + sx[i] * tiles[i]
            solution_field[z, pl.ds(row, 8), :] = ax
            residual[z, pl.ds(row, 8), :] = ar
        return carry

    lax.fori_loop(0, planes, body, 0)


def pairings(count):
    first = [(i, i ^ 1) for i in range(count) if i ^ 1 < count]
    second = [(i, i + 1) for i in range(1, count - 1, 2)]
    return first, second + [(j, i) for i, j in second]


def exchange(side_a, side_b):
    first, second = pairings(lax.axis_size("slab"))
    return lax.ppermute(side_a, "slab", first), lax.ppermute(side_b, "slab", second)


def swap_all(value):
    return lax.all_to_all(value, "slab", 0, 0)


def local(right_side, diagonal):
    index = lax.axis_index("slab")
    count = lax.axis_size("slab")
    where = jnp.stack([index % 2, index > 0, index < count - 1]).astype(jnp.int32)
    field = right_side.shape
    some = lambda k: (k,) + field[1:]
    pair = [field, field]
    sides = [some(2), some(2)]
    small = (ROWS, LANES)
    wide = (count,) + small
    near = pltpu.VMEM(some(4), F32)
    ghost_near = (pltpu.VMEM(some(2), F32), near)
    acc = lambda k: pltpu.VMEM((k, 8, LANES), F32)

    sa, sb = call(side_kernel, [some(3)] * 2, scratch=(pltpu.SemaphoreType.DMA((4,)),), hbm=True)(
        where, right_side, diagonal
    )
    got = exchange(sa, sb)
    t0 = right_side
    d, t1, t2, sums = call(open_kernel, [field] + pair + [(count, 8, LANES)], scratch=(acc(2),))(t0, diagonal)
    sums = swap_all(sums)
    t1, t2, sa, sb, ghost, gd, size = call(
        open_edge_kernel, pair + sides + [some(2)] * 2 + [(8, LANES)], {6: 0, 7: 1}, (near,)
    )(where, *got, t0, d, sums, t1, t2)
    got = exchange(sa, sb)
    t3, t4 = call(next_kernel, pair)(t2, t1, d)
    t3, t4, sa, sb, ghost = call(edge_kernel, pair + sides + [some(2)], {8: 0, 9: 1}, (near,))(
        where, *got, t2, t1, ghost, d, gd, t3, t4
    )
    got = exchange(sa, sb)
    t5, t6, early = call(third_kernel, pair + [small], scratch=(acc(16),))(t4, t3, d, size, t0, t1, t2)
    t5, t6, gram = call(third_edge_kernel, pair + [wide], {8: 0, 9: 1}, ghost_near + (acc(16),))(
        where, *got, t4, t3, ghost, d, gd, t5, t6, size, early, t0, t1, t2
    )
    gram = swap_all(gram)
    v0, sa, sb, state = call(restart_kernel, [field] + sides + [(4,) + small])(
        where, size, gram, t0, t1, t2, t3, t4, t5, t6
    )
    got = exchange(sa, sb)
    powers = (t0, t1, t2, t3, t4, t5)
    v1, v2, early = call(fourth_kernel, pair + [small], scratch=(acc(8),))(v0, d, size, *powers)
    v1, v2, sa, sb, ghost = call(restart_edge_kernel, pair + sides + [some(2)], {6: 0, 7: 1}, (near,))(
        where, *got, v0, d, gd, v1, v2
    )
    got = exchange(sa, sb)
    v3, v4, early = call(fifth_kernel, pair + [small], scratch=(acc(24),))(v2, v1, d, size, early, v0, *powers)
    v3, v4, gram = call(fifth_edge_kernel, pair + [wide], {8: 0, 9: 1}, ghost_near + (acc(24),))(
        where, *got, v2, v1, ghost, d, gd, v3, v4, size, early, v0, *powers
    )
    gram = swap_all(gram)
    return tuple(call(finish_kernel, pair)(size, state, gram, *powers, v0, v1, v2, v3, v4))


def solution(mesh):
    placed = (P("slab", "sys", None), P("slab", "sys", None))
    return jax.shard_map(
        local,
        mesh=mesh,
        in_specs=placed,
        out_specs=placed,
        check_vma=False,
    )
```

time: 380 us -> 92.1 us (0.24)
  blocking collectives: 204 us -> 38.2 us
  other arithmetic: 54.7 us -> 0.08 us
  starting transfers between devices: 59.7 us -> 17.3 us
  between operations: 37.4 us -> 0.78 us
  Pallas kernels: 0 us -> 28.2 us
  waiting for transfers between devices: 13.9 us -> 4.65 us
  local copies, waits for them, and re-layouts: 9.01 us -> 2.45 us
    psum x10 -> x0, blocking collectives: 204 us -> none  [merged_sums(): lax.psum((jnp.sum(residual * residual), jnp.sum(residual * applied)), 'sl...]
    ppermute x20 -> x10, starting transfers between devices: 59.7 us -> 17.3 us  [the longest x5 14 us: exchange(): lax.ppermute(side_a, 'slab', first)]
    all_to_all x0 -> x3, blocking collectives: none -> 38.2 us  [swap_all(): return lax.all_to_all(value, 'slab', 0, 0)]
    pallas_call x0 -> x13, Pallas kernels: none -> 28.2 us  [run(): pl.pallas_call(kernel, out_shape=[jax.ShapeDtypeStruct(s, F32) for s in o...]
    reduce_sum x10 -> x0, other arithmetic: 24.5 us -> none  [merged_sums(): jnp.sum(residual * applied)]
    sub x10 -> x0, other arithmetic: 24.3 us -> none  [local(): residual = residual - step_size * along]
    ppermute x20 -> x10, waiting for transfers between devices: 13.9 us -> 4.65 us  [the longest x5 4.64 us: exchange(): lax.ppermute(side_a, 'slab', first)]
    slice x30 -> x0, local copies, waits for them, and re-layouts: 8.13 us -> none  [the longest x10 3.61 us: operate(): beside = beside + jnp.pad(values[:, 1:], ((0, 0), (0, 1), (0, 0)))]
  transfers between devices with their start and end apart: 20 -> 10, of which waited for: 9 -> 2; matrix products, arithmetic and copies ran while one was open for 1% -> 0% of each run, Pallas kernels for 0% -> 14%
where the time goes in v2:
time: 92.1 us; the launch traced here: 91.7 us
  blocking collectives  38.2 us (41%)
  Pallas kernels  28.2 us (31%)
  starting transfers between devices  17.3 us (19%)
  waiting for transfers between devices  4.65 us (5%)
  local copies, waits for them, and re-layouts  2.45 us (3%)
    all_to_all x3, blocking collectives, swap_all(): return lax.all_to_all(value, 'slab', 0, 0)  38.2 us
    pallas_call x13, Pallas kernels, run(): pl.pallas_call(kernel, out_shape=[jax.ShapeDtypeStruct(s, F32) for s in o...  28.2 us
    ppermute x5, starting transfers between devices, exchange(): lax.ppermute(side_a, 'slab', first)  14 us
    ppermute x5, waiting for transfers between devices, exchange(): lax.ppermute(side_a, 'slab', first)  4.64 us
    ppermute x5, starting transfers between devices, exchange(): lax.ppermute(side_b, 'slab', second)  3.29 us
    unnamed x6, local copies, waits for them, and re-layouts  2.45 us
  transfers between devices with their start and end apart: 10, of which 2 were waited for; matrix products, arithmetic and copies ran while one was open for 0% of the time, Pallas kernels for 14%

profile of v2, /device:TPU:0, one launch (start us, length us, event | category | flops | bytes accessed | tf_op | source)
XLA Modules:
  0.0 91.7 jit_solution(10859401333681380915)
XLA Ops:
  0.7 1.2 %copy-done = f32[16,128,128]{2,1,0:T(8,128)S(1)} copy-done((f32[16,128,128]{2,1,0:T(8,128)S(1)}, f32[16,128,128]{2,1,0:T(8,128)}, u32[]{:S(2)}) %copy-start) | copy-done | bytes 1048600
  1.9 1.2 %copy-done.2 = f32[16,128,128]{2,1,0:T(8,128)S(1)} copy-done((f32[16,128,128]{2,1,0:T(8,128)S(1)}, f32[16,128,128]{2,1,0:T(8,128)}, u32[]{:S(2)}) %copy-start.2) | copy-done | bytes 1048600
  3.2 1.1 %shard_map.41 = (f32[3,128,128]{2,1,0:T(8,128)S(1)}, f32[3,128,128]{2,1,0:T(8,128)S(1)}) custom-call(s32[3]{0:T(128)S(1)} %pad_add_fusion.where, f32[16,128,128]{2,1,0:T(8,128)S(1)} %copy-done, f32[16,128,128]{2,1,0:T(8,128)S(1)} %copy-done.2), custom_call_target="tpu_custom_call" | custom-call | tf_op jit(solution)/shard_map/pallas_call | solution.py:228
  4.3 3.1 %collective-permute-start = (f32[3,128,128]{2,1,0:T(8,128)S(1)}, f32[3,128,128]{2,1,0:T(8,128)S(1)}, u32[]{:S(2)}, u32[]{:S(2)}) collective-permute-start(f32[3,128,128]{2,1,0:T(8,128)S(1)} %get-tuple-element.46), channel_id=1, source_target_pairs={{0,1},{1,0},{2,3},{3,2},{4,5},{5,4},{6,7},{7,6},{8,9},{9,8},{10,11... | collective-permute-start | bytes 589832 | tf_op jit(solution)/shard_map/ppermute | solution.py:414
  7.3 0.7 collective-permute-start.1
  8.0 1.6 %shard_map.42 = (f32[16,128,128]{2,1,0:T(8,128)S(1)}, f32[16,128,128]{2,1,0:T(8,128)S(1)}, f32[16,128,128]{2,1,0:T(8,128)S(1)}, f32[8,8,128]{2,1,0:T(8,128)S(1)}) custom-call(f32[16,128,128]{2,1,0:T(8,128)S(1)} %copy-done.1, f32[16,128,128]{2,1,0:T(8,128)S(1)} %copy-done.2), custom_call_target="tpu_custom_call" | custom-call | tf_op jit(solution)/shard_map/pallas_call | solution.py:228
  9.6 14.1 %all_to_all.15.sums = f32[8,8,128]{2,1,0:T(8,128)S(1)} all-to-all(f32[8,8,128]{2,1,0:T(8,128)S(1)} %get-tuple-element.49), channel_id=1, replica_groups=mesh['sys'=4,'slab'=8] {'slab'}, dimensions={0} | all-to-all | bytes 65536 | tf_op jit(solution)/shard_map/all_to_all | solution.py:418
  23.7 0.9 %shard_map.43 = (f32[16,128,128]{2,1,0:T(8,128)S(1)}, f32[16,128,128]{2,1,0:T(8,128)S(1)}, f32[2,128,128]{2,1,0:T(8,128)S(1)}, f32[2,128,128]{2,1,0:T(8,128)S(1)...) custom-call(s32[3]{0:T(128)S(1)} %pad_add_fusion.where, ...), custom_call_target="tpu_custom_call", output_to_operand_aliasing={{0}: (6, {}), {1}: (7, {})} | custom-call | tf_op jit(solution)/shard_map/pallas_call | solution.py:228
  25.8 1.2 %shard_map.44 = (f32[16,128,128]{2,1,0:T(8,128)S(1)}, f32[16,128,128]{2,1,0:T(8,128)S(1)}) custom-call(f32[16,128,128]{2,1,0:T(8,128)S(1)} %get-tuple-element.55.cur.t2.refs_2_, f32[16,128,128]{2,1,0:T(8,128)S(1)} %get-tuple-element.56.prev.t1.refs_1_, f32[16,128,128]{2,1,0:T(8,128)S(1)} %get-tuple-element.48.scale), custom_call_target="tpu_custom_call" | custom-call | tf_op jit(solution)/shard_map/pallas_call | solution.py:228
  27.1 2.6 %collective-permute-done.2.got_a = f32[2,128,128]{2,1,0:T(8,128)S(1)} collective-permute-done((f32[2,128,128]{2,1,0:T(8,128)S(1)}, f32[2,128,128]{2,1,0:T(8,128)S(1)}, u32[]{:S(2)}, u32[]{:S(2)}) %collective-permute-start.2) | collective-permute-done | bytes 131104 | tf_op jit(solution)/shard_map/ppermute | solution.py:414
  29.7 0.9 %shard_map.45 = (f32[16,128,128]{2,1,0:T(8,128)S(1)}, f32[16,128,128]{2,1,0:T(8,128)S(1)}, f32[2,128,128]{2,1,0:T(8,128)S(1)}, f32[2,128,128]{2,1,0:T(8,128)S(1)}, f32[2,128,128]{2,1,0:T(8,128)S(1)}) custom-call(s32[3]{0:T(128)S(1)} %pad_add_fusion.where, ...), custom_call_target="tpu_custom_call", output_to_operand_aliasing={{0}: (8, {}), {1}: (9, {})} | custom-call | tf_op jit(solution)/shard_map/pallas_call | solution.py:228
  30.6 4.9 %collective-permute-start.4 = (f32[2,128,128]{2,1,0:T(8,128)S(1)}, f32[2,128,128]{2,1,0:T(8,128)S(1)}, u32[]{:S(2)}, u32[]{:S(2)}) collective-permute-start(f32[2,128,128]{2,1,0:T(8,128)S(1)} %get-tuple-element.61), channel_id=1, source_target_pairs={{0,1},{1,0},{2,3},{3,2},{4,5},{5,4},{6,7},{7,6},{8,9},{9,8},{10,11... | collective-permute-start | bytes 393224 | tf_op jit(solution)/shard_map/ppermute | solution.py:414
  36.1 3.3 %shard_map.46 = (f32[16,128,128]{2,1,0:T(8,128)S(1)}, f32[16,128,128]{2,1,0:T(8,128)S(1)}, f32[16,128]{1,0:T(8,128)S(1)}) custom-call(f32[16,128,128]{2,1,0:T(8,128)S(1)} %get-tuple-element.63.cur.refs_4_.t4, f32[16,128,128]{2,1,0:T(8,128)S(1)} %get-tuple-element.64.prev.refs_3_.t3, f32[16,128,128]{2,1,0:T(8,128)S(1)} %get-tuple-element.48.scale, ...), custom_call_target="tpu_custom_call" | custom-call | tf_op jit(solution)/shard_map/pallas_call | solution.py:228
  39.5 3.2 %shard_map.47 = (f32[16,128,128]{2,1,0:T(8,128)S(1)}, f32[16,128,128]{2,1,0:T(8,128)S(1)}, f32[8,16,128]{2,1,0:T(8,128)S(1)}) custom-call(s32[3]{0:T(128)S(1)} %pad_add_fusion.where, f32[2,128,128]{2,1,0:T(8,128)S(1)} %collective-permute-done.4.got_a, f32[2,128,128]{2,1,0:T(8,128)S(1)} %collective-permute-done.5.got_b, ...), custom_call_target="tpu_custom_call", output_to_operand_aliasing={{0}: (8, {}), {1}: (9, {})} | custom-call | tf_op jit(solution)/shard_map/pallas_call | solution.py:228
  42.7 12.3 %all_to_all.16.gram = f32[8,16,128]{2,1,0:T(8,128)S(1)} all-to-all(f32[8,16,128]{2,1,0:T(8,128)S(1)} %get-tuple-element.69), channel_id=1, replica_groups=mesh['sys'=4,'slab'=8] {'slab'}, dimensions={0} | all-to-all | bytes 131072 | tf_op jit(solution)/shard_map/all_to_all | solution.py:418
  55.1 1.7 %shard_map.48 = (f32[16,128,128]{2,1,0:T(8,128)S(1)}, f32[2,128,128]{2,1,0:T(8,128)S(1)}, f32[2,128,128]{2,1,0:T(8,128)S(1)}, f32[4,16,128]{2,1,0:T(8,128)S(1)}) custom-call(s32[3]{0:T(128)S(1)} %pad_add_fusion.where, f32[8,128]{1,0:T(8,128)S(1)} %get-tuple-element.52.size, f32[8,16,128]{2,1,0:T(8,128)S(1)} %all_to_all.16.gram, ...), custom_call_target="tpu_custom_call" | custom-call | tf_op jit(solution)/shard_map/pallas_call | solution.py:228
  57.9 2.9 %shard_map.49 = (f32[16,128,128]{2,1,0:T(8,128)S(1)}, f32[16,128,128]{2,1,0:T(8,128)S(1)}, f32[16,128]{1,0:T(8,128)S(1)}) custom-call(f32[16,128,128]{2,1,0:T(8,128)S(1)} %get-tuple-element.75.cur.v0.refs_6_, f32[16,128,128]{2,1,0:T(8,128)S(1)} %get-tuple-element.48.scale, f32[8,128]{1,0:T(8,128)S(1)} %get-tuple-element.52.size, ...), custom_call_target="tpu_custom_call" | custom-call | tf_op jit(solution)/shard_map/pallas_call | solution.py:228
  60.7 2.0 %collective-permute-done.6.got_a = f32[2,128,128]{2,1,0:T(8,128)S(1)} collective-permute-done((f32[2,128,128]{2,1,0:T(8,128)S(1)}, f32[2,128,128]{2,1,0:T(8,128)S(1)}, u32[]{:S(2)}, u32[]{:S(2)}) %collective-permute-start.6) | collective-permute-done | bytes 131104 | tf_op jit(solution)/shard_map/ppermute | solution.py:414
  62.8 0.9 %shard_map.50 = (f32[16,128,128]{2,1,0:T(8,128)S(1)}, f32[16,128,128]{2,1,0:T(8,128)S(1)}, f32[2,128,128]{2,1,0:T(8,128)S(1)}, f32[2,128,128]{2,1,0:T(8,128)S(1)}, f32[2,128,128]{2,1,0:T(8,128)S(1)}) custom-call(s32[3]{0:T(128)S(1)} %pad_add_fusion.where, ...), custom_call_target="tpu_custom_call", output_to_operand_aliasing={{0}: (6, {}), {1}: (7, {})} | custom-call | tf_op jit(solution)/shard_map/pallas_call | solution.py:228
  63.7 5.1 %collective-permute-start.8 = (f32[2,128,128]{2,1,0:T(8,128)S(1)}, f32[2,128,128]{2,1,0:T(8,128)S(1)}, u32[]{:S(2)}, u32[]{:S(2)}) collective-permute-start(f32[2,128,128]{2,1,0:T(8,128)S(1)} %get-tuple-element.78), channel_id=1, source_target_pairs={{0,1},{1,0},{2,3},{3,2},{4,5},{5,4},{6,7},{7,6},{8,9},{9,8},{10,11... | collective-permute-start | bytes 393224 | tf_op jit(solution)/shard_map/ppermute | solution.py:414
  69.5 3.5 %shard_map.51 = (f32[16,128,128]{2,1,0:T(8,128)S(1)}, f32[16,128,128]{2,1,0:T(8,128)S(1)}, f32[16,128]{1,0:T(8,128)S(1)}) custom-call(f32[16,128,128]{2,1,0:T(8,128)S(1)} %get-tuple-element.80.cur.refs_8_, f32[16,128,128]{2,1,0:T(8,128)S(1)} %get-tuple-element.81.prev.refs_7_, f32[16,128,128]{2,1,0:T(8,128)S(1)} %get-tuple-element.48.scale, ...), custom_call_target="tpu_custom_call" | custom-call | tf_op jit(solution)/shard_map/pallas_call | solution.py:228
  73.0 3.4 %shard_map.52 = (f32[16,128,128]{2,1,0:T(8,128)S(1)}, f32[16,128,128]{2,1,0:T(8,128)S(1)}, f32[8,16,128]{2,1,0:T(8,128)S(1)}) custom-call(s32[3]{0:T(128)S(1)} %pad_add_fusion.where, f32[2,128,128]{2,1,0:T(8,128)S(1)} %collective-permute-done.8.got_a, f32[2,128,128]{2,1,0:T(8,128)S(1)} %collective-permute-done.9.got_b, ...), custom_call_target="tpu_custom_call", output_to_operand_aliasing={{0}: (8, {}), {1}: (9, {})} | custom-call | tf_op jit(solution)/shard_map/pallas_call | solution.py:228
  76.4 11.8 %all_to_all.17.gram = f32[8,16,128]{2,1,0:T(8,128)S(1)} all-to-all(f32[8,16,128]{2,1,0:T(8,128)S(1)} %get-tuple-element.87), channel_id=1, replica_groups=mesh['sys'=4,'slab'=8] {'slab'}, dimensions={0} | all-to-all | bytes 131072 | tf_op jit(solution)/shard_map/all_to_all | solution.py:418
  88.2 3.5 %shard_map.53 = (f32[16,128,128]{2,1,0:T(8,128)}, f32[16,128,128]{2,1,0:T(8,128)}) custom-call(f32[8,128]{1,0:T(8,128)S(1)} %get-tuple-element.52.size, f32[4,16,128]{2,1,0:T(8,128)S(1)} %get-tuple-element.72.state, f32[8,16,128]{2,1,0:T(8,128)S(1)} %all_to_all.17.gram, f32[16,128,128]{2,1,0:T(8,128)S(1)} %copy-done.1, ...), custom_call_target="tpu_custom_call" | custom-call | tf_op jit(solution)/shard_map/pallas_call | solution.py:228
  (19 shorter events, 3.7 us)
Async XLA Ops:
  0.7 1.2 %copy-start = (f32[16,128,128]{2,1,0:T(8,128)S(1)}, f32[16,128,128]{2,1,0:T(8,128)}, u32[]{:S(2)}) copy-start(f32[16,128,128]{2,1,0:T(8,128)} %refs_0_.3) | copy-start | bytes 3145732
  1.9 1.2 %copy-start.2 = (f32[16,128,128]{2,1,0:T(8,128)S(1)}, f32[16,128,128]{2,1,0:T(8,128)}, u32[]{:S(2)}) copy-start(f32[16,128,128]{2,1,0:T(8,128)} %diag.3) | copy-start | bytes 3145732
  3.2 4.8 %copy-start.1 = (f32[16,128,128]{2,1,0:T(8,128)S(1)}, f32[16,128,128]{2,1,0:T(8,128)}, u32[]{:S(2)}) copy-start(f32[16,128,128]{2,1,0:T(8,128)} %refs_0_.3) | copy-start | bytes 3145732
  4.3 19.4 %collective-permute-start = (f32[3,128,128]{2,1,0:T(8,128)S(1)}, f32[3,128,128]{2,1,0:T(8,128)S(1)}, u32[]{:S(2)}, u32[]{:S(2)}) collective-permute-start(f32[3,128,128]{2,1,0:T(8,128)S(1)} %get-tuple-element.46), channel_id=1, source_target_pairs={{0,1},{1,0},{2,3},{3,2},{4,5},{5,4},{6,7},{7,6},{8,9},{9,8},{10,11... | collective-permute-start | bytes 589832 | tf_op jit(solution)/shard_map/ppermute | solution.py:414
  7.3 16.4 %collective-permute-start.1 = (f32[3,128,128]{2,1,0:T(8,128)S(1)}, f32[3,128,128]{2,1,0:T(8,128)S(1)}, u32[]{:S(2)}, u32[]{:S(2)}) collective-permute-start(f32[3,128,128]{2,1,0:T(8,128)S(1)} %get-tuple-element.47), channel_id=1, source_target_pairs={{1,2},{3,4},{5,6},{2,1},{4,3},{6,5},{9,10},{11,12},{13,14},{10,9},... | collective-permute-start | bytes 589832 | tf_op jit(solution)/shard_map/ppermute | solution.py:414
  24.6 5.0 %collective-permute-start.2 = (f32[2,128,128]{2,1,0:T(8,128)S(1)}, f32[2,128,128]{2,1,0:T(8,128)S(1)}, u32[]{:S(2)}, u32[]{:S(2)}) collective-permute-start(f32[2,128,128]{2,1,0:T(8,128)S(1)} %get-tuple-element.53), channel_id=1, source_target_pairs={{0,1},{1,0},{2,3},{3,2},{4,5},{5,4},{6,7},{7,6},{8,9},{9,8},{10,11... | collective-permute-start | bytes 393224 | tf_op jit(solution)/shard_map/ppermute | solution.py:414
  25.2 4.5 %collective-permute-start.3 = (f32[2,128,128]{2,1,0:T(8,128)S(1)}, f32[2,128,128]{2,1,0:T(8,128)S(1)}, u32[]{:S(2)}, u32[]{:S(2)}) collective-permute-start(f32[2,128,128]{2,1,0:T(8,128)S(1)} %get-tuple-element.54), channel_id=1, source_target_pairs={{1,2},{3,4},{5,6},{2,1},{4,3},{6,5},{9,10},{11,12},{13,14},{10,9},... | collective-permute-start | bytes 393224 | tf_op jit(solution)/shard_map/ppermute | solution.py:414
  30.6 8.8 %collective-permute-start.4 = (f32[2,128,128]{2,1,0:T(8,128)S(1)}, f32[2,128,128]{2,1,0:T(8,128)S(1)}, u32[]{:S(2)}, u32[]{:S(2)}) collective-permute-start(f32[2,128,128]{2,1,0:T(8,128)S(1)} %get-tuple-element.61), channel_id=1, source_target_pairs={{0,1},{1,0},{2,3},{3,2},{4,5},{5,4},{6,7},{7,6},{8,9},{9,8},{10,11... | collective-permute-start | bytes 393224 | tf_op jit(solution)/shard_map/ppermute | solution.py:414
  35.5 4.0 %collective-permute-start.5 = (f32[2,128,128]{2,1,0:T(8,128)S(1)}, f32[2,128,128]{2,1,0:T(8,128)S(1)}, u32[]{:S(2)}, u32[]{:S(2)}) collective-permute-start(f32[2,128,128]{2,1,0:T(8,128)S(1)} %get-tuple-element.62), channel_id=1, source_target_pairs={{1,2},{3,4},{5,6},{2,1},{4,3},{6,5},{9,10},{11,12},{13,14},{10,9},... | collective-permute-start | bytes 393224 | tf_op jit(solution)/shard_map/ppermute | solution.py:414
  56.7 6.0 %collective-permute-start.6 = (f32[2,128,128]{2,1,0:T(8,128)S(1)}, f32[2,128,128]{2,1,0:T(8,128)S(1)}, u32[]{:S(2)}, u32[]{:S(2)}) collective-permute-start(f32[2,128,128]{2,1,0:T(8,128)S(1)} %get-tuple-element.73), channel_id=1, source_target_pairs={{0,1},{1,0},{2,3},{3,2},{4,5},{5,4},{6,7},{7,6},{8,9},{9,8},{10,11... | collective-permute-start | bytes 393224 | tf_op jit(solution)/shard_map/ppermute | solution.py:414
  57.2 5.6 %collective-permute-start.7 = (f32[2,128,128]{2,1,0:T(8,128)S(1)}, f32[2,128,128]{2,1,0:T(8,128)S(1)}, u32[]{:S(2)}, u32[]{:S(2)}) collective-permute-start(f32[2,128,128]{2,1,0:T(8,128)S(1)} %get-tuple-element.74), channel_id=1, source_target_pairs={{1,2},{3,4},{5,6},{2,1},{4,3},{6,5},{9,10},{11,12},{13,14},{10,9},... | collective-permute-start | bytes 393224 | tf_op jit(solution)/shard_map/ppermute | solution.py:414
  63.7 9.3 %collective-permute-start.8 = (f32[2,128,128]{2,1,0:T(8,128)S(1)}, f32[2,128,128]{2,1,0:T(8,128)S(1)}, u32[]{:S(2)}, u32[]{:S(2)}) collective-permute-start(f32[2,128,128]{2,1,0:T(8,128)S(1)} %get-tuple-element.78), channel_id=1, source_target_pairs={{0,1},{1,0},{2,3},{3,2},{4,5},{5,4},{6,7},{7,6},{8,9},{9,8},{10,11... | collective-permute-start | bytes 393224 | tf_op jit(solution)/shard_map/ppermute | solution.py:414
  68.8 4.2 %collective-permute-start.9 = (f32[2,128,128]{2,1,0:T(8,128)S(1)}, f32[2,128,128]{2,1,0:T(8,128)S(1)}, u32[]{:S(2)}, u32[]{:S(2)}) collective-permute-start(f32[2,128,128]{2,1,0:T(8,128)S(1)} %get-tuple-element.79), channel_id=1, source_target_pairs={{1,2},{3,4},{5,6},{2,1},{4,3},{6,5},{9,10},{11,12},{13,14},{10,9},... | collective-permute-start | bytes 393224 | tf_op jit(solution)/shard_map/ppermute | solution.py:414

commit v3 on v2

v3 whole, which is shorter than its diff:
```python
import functools

import jax
import jax.numpy as jnp
from jax import lax
from jax.experimental import pallas as pl
from jax.experimental.pallas import tpu as pltpu
from jax.sharding import PartitionSpec as P

FIRST = 4
SECOND = 5
WIDTH = 5
LOW, HIGH = 0.25, 14.0
CENTER = (LOW + HIGH) / 2
HALF = (HIGH - LOW) / 2
ROWS, LANES = 16, 128
F32 = jnp.float32


def tile(at, row):
    ref, z = at
    return ref[z, pl.ds(row, 8), :]


def advance(out, cur, above, below, scale, prev=None, keep=None):
    _, ny, nx = cur[0].shape
    row = lax.broadcasted_iota(jnp.int32, (8, nx), 0)
    lane = lax.broadcasted_iota(jnp.int32, (8, nx), 1)
    zero = jnp.zeros((8, nx), F32)
    for at in range(0, ny, 8):
        mid = tile(cur, at)
        beside = tile(above, at) + tile(below, at)
        if at:
            beside = beside + tile(cur, at - 1)
        else:
            beside = beside + jnp.where(row == 0, zero, pltpu.roll(mid, 1, 0))
        if at + 8 < ny:
            beside = beside + tile(cur, at + 1)
        else:
            beside = beside + jnp.where(row == 7, zero, pltpu.roll(mid, 7, 0))
        left = jnp.where(lane == 0, zero, pltpu.roll(mid, 1, 1))
        right = jnp.where(lane == nx - 1, zero, pltpu.roll(mid, nx - 1, 1))
        beside = beside + (left + right)
        image = tile(scale, at) * mid - (2.0 / HALF) * beside
        image = 0.5 * image if prev is None else image - tile(prev, at)
        if keep is not None:
            image = image * keep
        out[0][out[1], pl.ds(at, 8), :] = image


def scaled(diag):
    return (2.0 / HALF) * diag + (2.0 / HALF) * (6.0 - CENTER)


def over(first, last, most, body):
    count = last - first
    step = max(k for k in range(1, most + 1) if count % k == 0)

    def run(i, carry):
        for k in range(step):
            body(first + i * step + k)
        return carry

    lax.fori_loop(0, count // step, run, 0)


def interior(fields, scale):
    planes = scale.shape[0]
    for j in range(1, WIDTH + 1):

        def body(z, j=j):
            old = None if j == 1 else (fields[j - 2], z)
            cur = fields[j - 1]
            advance((fields[j], z), (cur, z), (cur, z + 1), (cur, z - 1), (scale, z), old)

        over(j, planes - j, 7, body)


def edge(where, use_a, planes):
    even = where[0] == 0
    high = even if use_a else jnp.logical_not(even)
    base = jnp.where(high, planes - 1, 0)
    inward = jnp.where(high, -1, 1)
    return high, base, inward, jnp.where(high, where[2], where[1]).astype(F32)


def wedge(fields, ghosts, scale, ghost_scale, base, inward, keep):
    def at(j, i):
        return (fields[j], base + inward * i) if i >= 0 else (ghosts[j], -1 - i)

    def scale_at(i):
        return (scale, base + inward * i) if i >= 0 else (ghost_scale, -1 - i)

    for j in range(1, WIDTH + 1):
        for i in range(j - WIDTH, j):
            old = None if j == 1 else at(j - 2, i)
            mask = keep if i < 0 else None
            advance(at(j, i), at(j - 1, i), at(j - 1, i + 1), at(j - 1, i - 1), scale_at(i), old, mask)


def put_sides(where, field, side_a, side_b):
    planes = field.shape[0]
    for side, use_a in ((side_a, True), (side_b, False)):
        _, base, inward, _ = edge(where, use_a, planes)
        for k in range(WIDTH):
            side[k] = field[base + inward * k]


def row_index():
    return lax.broadcasted_iota(jnp.int32, (ROWS, LANES), 0)


def unit(k):
    return jnp.where(row_index() == k, 1.0, 0.0).astype(F32)


def entry(v, k):
    return jnp.broadcast_to(v[k : k + 1, :], (ROWS, LANES))


def columns(mat, count):
    return [jnp.broadcast_to(mat[:, j : j + 1], (ROWS, LANES)) for j in range(count)]


def product(cols, v):
    return functools.reduce(lambda a, b: a + b, [c * entry(v, k) for k, c in enumerate(cols)])


def dot(a, b):
    return jnp.broadcast_to(jnp.sum(a * b, axis=0, keepdims=True), (ROWS, LANES))


def steps(gram, mat, x, r, p, count):
    norm = dot(r, product(gram, r))
    for _ in range(count):
        image = product(mat, p)
        size = norm / dot(p, product(gram, image))
        x = x + size * p
        r = r - size * image
        new = dot(r, product(gram, r))
        last = (new / norm) * p
        p = r + last
        norm = new
    return x, r, last


def chebyshev_column(first, k):
    out = CENTER * unit(k) + (HALF if k == first else HALF / 2) * unit(k + 1)
    return out if k == first else out + (HALF / 2) * unit(k - 1)


def to_powers(size, count):
    cols = [unit(0)]
    for j in range(count):
        cols.append(unit(j) - size * chebyshev_column(0, j))
    return cols


def gram_tile(rows):
    ri = row_index()
    ci = lax.broadcasted_iota(jnp.int32, (ROWS, LANES), 1)
    out = jnp.zeros((ROWS, LANES), F32)
    blank = jnp.zeros((1, LANES), F32)
    for j in sorted({j for _, j in rows}):
        stack = jnp.concatenate([rows.get((i, j), blank) for i in range(ROWS)], axis=0)
        col = jnp.sum(stack, axis=1, keepdims=True)
        out = out + jnp.where(ci == j, col, 0.0)
        row = jnp.sum(jnp.where(ri == ci, col, 0.0), axis=0, keepdims=True)
        out = out + jnp.where((ri == j) & (ci < j), row, 0.0)
    return out


def inner_products(first, count, ny, load, pairs, acc):
    zero = jnp.zeros(acc.shape[1:], F32)
    for k in range(len(pairs)):
        acc[k] = zero

    def body(k, carry):
        z = first + k
        sums = [None] * len(pairs)
        for row in range(0, ny, 8):
            tiles = load(z, row)
            for k, (i, j) in enumerate(pairs):
                part = tiles[i] * tiles[j]
                sums[k] = part if row == 0 else sums[k] + part
        for k, val in enumerate(sums):
            acc[k] = acc[k] + val
        return carry

    lax.fori_loop(0, count, body, 0)
    return {pair: jnp.sum(acc[k], axis=0, keepdims=True) for k, pair in enumerate(pairs)}


def pairs_of(first, last):
    return [(i, j) for j in range(first, last) for i in range(j + 1)]


def shifted(powers, size, count):
    keep = 1.0 - size * CENTER
    move = size * (HALF / 2)
    out = [powers[0], keep * powers[0] - (2.0 * move) * powers[1]]
    for j in range(1, count):
        out.append(keep * powers[j] - move * (powers[j + 1] + powers[j - 1]))
    return out


def first_size(sums):
    norm = jnp.sum(sums[0:1, :], axis=1, keepdims=True)
    cross = jnp.sum(sums[1:2, :], axis=1, keepdims=True)
    return norm / (CENTER * norm + HALF * cross)


def gathered(ref):
    return functools.reduce(lambda a, b: a + b, [ref[k] for k in range(ref.shape[0])])


def spread(ref, value):
    for k in range(ref.shape[0]):
        ref[k] = value


def call(kernel, outs, aliases=None, scratch=(), hbm=False):
    def spec(a):
        if a.dtype == jnp.int32:
            return pl.BlockSpec(memory_space=pltpu.SMEM)
        return pl.BlockSpec(memory_space=pltpu.HBM if hbm else pltpu.VMEM)

    def run(*args):
        return pl.pallas_call(
            kernel,
            out_shape=[jax.ShapeDtypeStruct(s, F32) for s in outs],
            in_specs=[spec(a) for a in args],
            out_specs=[pl.BlockSpec(memory_space=pltpu.VMEM) for _ in outs],
            scratch_shapes=list(scratch),
            input_output_aliases=aliases or {},
            compiler_params=pltpu.CompilerParams(vmem_limit_bytes=16 << 20),
        )(*args)

    return run


def side_kernel(where, rhs, diag, side_a, side_b, sems):
    copies = []
    for side, use_a in ((side_a, True), (side_b, False)):
        _, base, inward, _ = edge(where, use_a, rhs.shape[0])
        for k in range(2 * WIDTH - 1):
            source = rhs.at[pl.ds(base + inward * k, 1)] if k < WIDTH else diag.at[pl.ds(base + inward * (k - WIDTH), 1)]
            copies.append(pltpu.make_async_copy(source, side.at[pl.ds(k, 1)], sems.at[len(copies)]))
    for copy in copies:
        copy.start()
    for copy in copies:
        copy.wait()


def open_kernel(rhs, diag, side_in, scale, *refs):
    powers, (side, sums, acc) = (rhs,) + refs[:WIDTH], refs[WIDTH:]
    planes, ny, _ = rhs.shape

    def fill(z):
        scale[z] = scaled(diag[z])

    over(0, planes, 4, fill)
    interior(powers, scale)
    load = lambda z, row: [tile((rhs, z), row), tile((powers[1], z), row)]
    rows = inner_products(1, planes - 2, ny, load, [(0, 0), (0, 1)], acc)
    blank = jnp.zeros((6, LANES), F32)
    spread(sums, jnp.concatenate([rows[0, 0], rows[0, 1], blank], axis=0))


def low_gram(powers, size, first, count, acc):
    ny = powers[0].shape[1]
    load = lambda z, row: shifted([tile((ref, z), row) for ref in powers], size, FIRST + 1)
    return gram_tile(inner_products(first, count, ny, load, pairs_of(0, FIRST + 2), acc))


def high_gram(powers, fields, size, first, count, acc):
    ny = powers[0].shape[1]

    def load(z, row):
        out = shifted([tile((ref, z), row) for ref in powers], size, FIRST)
        return out + [tile((ref, z), row) for ref in fields]

    top = FIRST + 1
    return gram_tile(inner_products(first, count, ny, load, pairs_of(top, top + SECOND + 1), acc))


def lower(base, high):
    return jnp.where(high, base - (WIDTH - 1), base)


def first_wedge_kernel(where, got, scale, sums, t0, *refs):
    powers, (ghost_scale, size, gram) = (t0,) + refs[WIDTH : 2 * WIDTH], refs[2 * WIDTH : 2 * WIDTH + 3]
    ghosts, acc = refs[2 * WIDTH + 3 : -1], refs[-1]
    high, base, inward, keep = edge(where, True, t0.shape[0])
    for k in range(WIDTH - 1):
        ghost_scale[k] = scaled(got[WIDTH + k])
    wedge(powers, (got,) + ghosts, scale, ghost_scale, base, inward, keep)
    size[...] = jnp.broadcast_to(first_size(gathered(sums)), (8, LANES))
    first = jnp.where(high, WIDTH, 0)
    gram[...] = low_gram(powers, size[0:1, 0:1], first, t0.shape[0] - WIDTH, acc)


def second_wedge_kernel(where, got, scale, size, early, t0, *refs):
    powers, (ghost_scale, gram) = (t0,) + refs[WIDTH : 2 * WIDTH], refs[2 * WIDTH : 2 * WIDTH + 2]
    ghosts, acc = refs[2 * WIDTH + 2 : -1], refs[-1]
    high, base, inward, keep = edge(where, False, t0.shape[0])
    for k in range(WIDTH - 1):
        ghost_scale[k] = scaled(got[WIDTH + k])
    wedge(powers, (got,) + ghosts, scale, ghost_scale, base, inward, keep)
    spread(gram, early[...] + low_gram(powers, size[0:1, 0:1], lower(base, high), WIDTH, acc))


def third_open_kernel(v0, scale, size, side_in, *refs):
    powers, refs = refs[: FIRST + 1], refs[FIRST + 1 :]
    fields, (side, gram, acc) = (v0,) + refs[:WIDTH], refs[WIDTH:]
    interior(fields, scale)
    gram[...] = high_gram(powers, fields, size[0:1, 0:1], WIDTH, v0.shape[0] - 2 * WIDTH, acc)


def third_wedge(use_a, where, got, scale, ghost_scale, size, early, v0, *refs):
    powers, refs = refs[: FIRST + 1], refs[FIRST + 1 :]
    fields, gram = (v0,) + refs[WIDTH : 2 * WIDTH], refs[2 * WIDTH]
    ghosts, acc = refs[2 * WIDTH + 1 : -1], refs[-1]
    high, base, inward, keep = edge(where, use_a, v0.shape[0])
    wedge(fields, (got,) + ghosts, scale, ghost_scale, base, inward, keep)
    value = early[...] + high_gram(powers, fields, size[0:1, 0:1], lower(base, high), WIDTH, acc)
    if use_a:
        gram[...] = value
    else:
        spread(gram, value)


def restart_kernel(where, size, gram, *refs):
    powers = refs[: FIRST + 2]
    field, side_a, side_b, state = refs[FIRST + 2 :]
    size = size[0:1, 0:1]
    top = FIRST + 1
    full = gathered(gram)
    mat = [(1.0 / size) * (unit(0) - unit(1))] + [chebyshev_column(1, k) for k in range(1, top)]
    zero = jnp.zeros((ROWS, LANES), F32)
    x, r, last = steps(columns(full, top + 1), mat, zero, unit(0), unit(0), top)
    coef = product(to_powers(size, top), r)
    scale = [coef[i : i + 1, :] for i in range(top + 1)]
    planes, ny, _ = field.shape

    def body(z, carry):
        for row in range(0, ny, 8):
            out = scale[0] * tile((powers[0], z), row)
            for i in range(1, top + 1):
                out = out + scale[i] * tile((powers[i], z), row)
            field[z, pl.ds(row, 8), :] = out
        return carry

    lax.fori_loop(0, planes, body, 0)
    put_sides(where, field, side_a, side_b)
    ri = row_index()
    ci = lax.broadcasted_iota(jnp.int32, (ROWS, LANES), 1)
    inverse = 1.0 / entry(r, top)
    swap = jnp.where(ri == top, inverse, -inverse * r)
    rebase = lambda v: jnp.where(ri == top, 0.0, v) + entry(v, top) * swap
    state[0] = jnp.where((ri < top) & (ci < top), full, 0.0)
    state[1] = unit(top) + rebase(last)
    state[2] = rebase(x)
    state[3] = swap


def finish_kernel(size, state, gram, *refs):
    top = FIRST + 1
    count = top + SECOND + 1
    refs, (solution_field, residual) = refs[:count], refs[count:]
    size = size[0:1, 0:1]
    mat = [(1.0 / size) * (unit(0) - unit(1))] + [chebyshev_column(1, k) for k in range(1, top - 1)]
    mat.append(CENTER * unit(top - 1) + (HALF / 2) * (unit(top - 2) + state[3]))
    mat += [chebyshev_column(top, k) for k in range(top, top + SECOND)]
    full = state[0] + gathered(gram)
    x, r, _ = steps(columns(full, count), mat, state[2], unit(top), state[1], SECOND)
    back = to_powers(size, FIRST) + [unit(k) for k in range(top, count)]
    x, r = product(back, x), product(back, r)
    sx = [x[i : i + 1, :] for i in range(count)]
    sr = [r[i : i + 1, :] for i in range(count)]
    planes, ny, _ = solution_field.shape

    def body(z, carry):
        for row in range(0, ny, 8):
            tiles = [tile((ref, z), row) for ref in refs]
            ax, ar = sx[0] * tiles[0], sr[0] * tiles[0]
            for i in range(1, count):
                ar = ar + sr[i] * tiles[i]
                if i + 1 < count:
                    ax = ax + sx[i] * tiles[i]
            solution_field[z, pl.ds(row, 8), :] = ax
            residual[z, pl.ds(row, 8), :] = ar
        return carry

    lax.fori_loop(0, planes, body, 0)


def pairings(count):
    first = [(i, i ^ 1) for i in range(count) if i ^ 1 < count]
    second = [(i, i + 1) for i in range(1, count - 1, 2)]
    return first, second + [(j, i) for i, j in second]


def swap_a(side):
    return lax.ppermute(side, "slab", pairings(lax.axis_size("slab"))[0])


def swap_b(side):
    return lax.ppermute(side, "slab", pairings(lax.axis_size("slab"))[1])


def swap_all(value):
    return lax.all_to_all(value, "slab", 0, 0)


def local(right_side, diagonal):
    index = lax.axis_index("slab")
    count = lax.axis_size("slab")
    where = jnp.stack([index % 2, index > 0, index < count - 1]).astype(jnp.int32)
    field = right_side.shape
    some = lambda k: (k,) + field[1:]
    fields = [field] * WIDTH
    small = (ROWS, LANES)
    wide = (count,) + small
    ghosts = tuple(pltpu.VMEM(some(WIDTH - j), F32) for j in range(1, WIDTH))
    acc = lambda k: pltpu.VMEM((k, 8, LANES), F32)
    ghost_side = some(WIDTH - 1)

    message = some(2 * WIDTH - 1)
    sa, sb = call(
        side_kernel, [message] * 2, scratch=(pltpu.SemaphoreType.DMA((4 * WIDTH - 2,)),), hbm=True
    )(where, *(pltpu.with_memory_space_constraint(a, pltpu.HBM) for a in (right_side, diagonal)))
    got_a = swap_a(sa)
    t0 = right_side
    d, *powers, sb, sums = call(
        open_kernel, [field] + fields + [message, (count, 8, LANES)], {2: 1 + WIDTH}, (acc(2),)
    )(t0, diagonal, sb)
    got_b = swap_b(sb)
    sums = swap_all(sums)
    inner = {5 + k: k for k in range(WIDTH)}
    *powers, gd_a, size, early = call(
        first_wedge_kernel, fields + [ghost_side, (8, LANES), small], inner, ghosts + (acc(24),)
    )(where, got_a, d, sums, t0, *powers)
    inner = {6 + k: k for k in range(WIDTH)}
    *powers, gd_b, gram = call(second_wedge_kernel, fields + [ghost_side, wide], inner, ghosts + (acc(24),))(
        where, got_b, d, size, early, t0, *powers
    )
    gram = swap_all(gram)
    powers = [t0] + powers
    v0, sa, sb, state = call(restart_kernel, [field] + [some(WIDTH)] * 2 + [(4,) + small])(
        where, size, gram, *powers
    )
    powers = powers[: FIRST + 1]
    got_a = swap_a(sa)
    last = len(powers)
    *late, sb, early = call(third_open_kernel, fields + [some(WIDTH), small], {3: WIDTH}, (acc(56),))(
        v0, d, size, sb, *powers
    )
    got_b = swap_b(sb)
    inner = {7 + last + k: k for k in range(WIDTH)}
    *late, early = call(functools.partial(third_wedge, True), fields + [small], inner, ghosts + (acc(56),))(
        where, got_a, d, gd_a, size, early, v0, *powers, *late
    )
    *late, gram = call(functools.partial(third_wedge, False), fields + [wide], inner, ghosts + (acc(56),))(
        where, got_b, d, gd_b, size, early, v0, *powers, *late
    )
    gram = swap_all(gram)
    return tuple(call(finish_kernel, [field] * 2)(size, state, gram, *powers, v0, *late))


def solution(mesh):
    placed = (P("slab", "sys", None), P("slab", "sys", None))
    return jax.shard_map(
        local,
        mesh=mesh,
        in_specs=placed,
        out_specs=placed,
        check_vma=False,
    )
```

time: 92.1 us -> 82.8 us (0.90)
  starting transfers between devices: 17.3 us -> 4.89 us
  blocking collectives: 38.2 us -> 48.4 us
  waiting for transfers between devices: 4.65 us -> 1.79 us
  local copies, waits for them, and re-layouts: 2.45 us -> 0.01 us
  Pallas kernels: 28.2 us -> 26.7 us
    ppermute x10 -> x4, starting transfers between devices: 17.3 us -> 4.89 us  [the longest x2 3.51 us: swap_a(): return lax.ppermute(side, 'slab', pairings(lax.axis_size('slab'))[0])]
    all_to_all x3, blocking collectives: 38.2 us -> 48.4 us  [swap_all(): return lax.all_to_all(value, 'slab', 0, 0)]
    ppermute x10 -> x4, waiting for transfers between devices: 4.65 us -> 1.79 us  [the longest x2 1.79 us: swap_a(): return lax.ppermute(side, 'slab', pairings(lax.axis_size('slab'))[0])]
    unnamed x6 -> x4, local copies, waits for them, and re-layouts: 2.45 us -> 0.01 us
    pallas_call x13 -> x9, Pallas kernels: 28.2 us -> 26.7 us  [run(): pl.pallas_call(kernel, out_shape=[jax.ShapeDtypeStruct(s, F32) for s in o...]
  transfers between devices with their start and end apart: 10 -> 4, of which waited for: 2 -> 1; matrix products, arithmetic and copies ran while one was open for 0% -> 0% of each run, Pallas kernels for 14% -> 17%
where the time goes in v3:
time: 82.8 us; the launch traced here: 82.5 us
  blocking collectives  48.4 us (58%)
  Pallas kernels  26.7 us (32%)
  starting transfers between devices  4.89 us (6%)
  waiting for transfers between devices  1.79 us (2%)
    all_to_all x3, blocking collectives, swap_all(): return lax.all_to_all(value, 'slab', 0, 0)  48.4 us
    pallas_call x9, Pallas kernels, run(): pl.pallas_call(kernel, out_shape=[jax.ShapeDtypeStruct(s, F32) for s in o...  26.7 us
    ppermute x2, starting transfers between devices, swap_a(): return lax.ppermute(side, 'slab', pairings(lax.axis_size('slab'))[0])  3.51 us
    ppermute x2, waiting for transfers between devices, swap_a(): return lax.ppermute(side, 'slab', pairings(lax.axis_size('slab'))[0])  1.79 us
  transfers between devices with their start and end apart: 4, of which 1 were waited for; matrix products, arithmetic and copies ran while one was open for 0% of the time, Pallas kernels for 17%

profile of v3, /device:TPU:0, one launch (start us, length us, event | category | flops | bytes accessed | tf_op | source)
XLA Modules:
  0.0 82.5 jit_solution(14937921498384041717)
XLA Ops:
  0.6 0.1 pad_add_fusion.where
  0.7 0.0 copy-start
  0.7 2.1 %shard_map.41 = (f32[9,128,128]{2,1,0:T(8,128)S(1)}, f32[9,128,128]{2,1,0:T(8,128)S(1)}) custom-call(s32[3]{0:T(128)S(1)} %pad_add_fusion.where, f32[16,128,128]{2,1,0:T(8,128)} %refs_0_.9, f32[16,128,128]{2,1,0:T(8,128)} %diag.3), custom_call_target="tpu_custom_call" | custom-call | tf_op jit(solution)/shard_map/pallas_call | solution.py:229
  2.8 3.1 %collective-permute-start = (f32[9,128,128]{2,1,0:T(8,128)S(1)}, f32[9,128,128]{2,1,0:T(8,128)S(1)}, u32[]{:S(2)}, u32[]{:S(2)}) collective-permute-start(f32[9,128,128]{2,1,0:T(8,128)S(1)} %get-tuple-element.50), channel_id=1, source_target_pairs={{0,1},{1,0},{2,3},{3,2},{4,5},{5,4},{6,7},{7,6},{8,9},{9,8},{10,11... | collective-permute-start | bytes 1769480 | tf_op jit(solution)/shard_map/ppermute | solution.py:405
  5.8 0.0 copy-done
  5.8 0.0 copy-done.1
  5.9 2.8 %shard_map.42 = (f32[16,128,128]{2,1,0:T(8,128)S(1)}, f32[16,128,128]{2,1,0:T(8,128)S(1)}, f32[16,128,128]{2,1,0:T(8,128)S(1)}, f32[16,128,128]{2,1,0:T(8,128)S(...) custom-call(f32[16,128,128]{2,1,0:T(8,128)S(1)} %copy-done, ...), custom_call_target="tpu_custom_call", output_to_operand_aliasing={{6}: (2, {})} | custom-call | tf_op jit(solution)/shard_map/pallas_call | solution.py:229
  8.6 0.7 collective-permute-start.1
  9.3 22.1 %all_to_all.15.sums = f32[8,8,128]{2,1,0:T(8,128)S(1)} all-to-all(f32[8,8,128]{2,1,0:T(8,128)S(1)} %get-tuple-element.53), channel_id=1, replica_groups=mesh['sys'=4,'slab'=8] {'slab'}, dimensions={0} | all-to-all | bytes 65536 | tf_op jit(solution)/shard_map/all_to_all | solution.py:413
  31.4 0.0 collective-permute-done.got
  31.4 3.5 %shard_map.43 = (f32[16,128,128]{2,1,0:T(8,128)S(1)}, f32[16,128,128]{2,1,0:T(8,128)S(1)}, f32[16,128,128]{2,1,0:T(8,128)S(1)}, f32[16,128,128]{2,1,0:T(8,128)S(...) custom-call(s32[3]{0:T(128)S(1)} %pad_add_fusion.where, ...), custom_call_target="tpu_custom_call", output_to_operand_aliasing={{0}: (5, {}), {1}: (6, {}), {2}: (7, {}), {3}: (8, {}), {4}... | custom-call | tf_op jit(solution)/shard_map/pallas_call | solution.py:229
  35.0 0.0 collective-permute-done.1.got
  35.0 2.5 %shard_map.44 = (f32[16,128,128]{2,1,0:T(8,128)S(1)}, f32[16,128,128]{2,1,0:T(8,128)S(1)}, f32[16,128,128]{2,1,0:T(8,128)S(1)}, f32[16,128,128]{2,1,0:T(8,128)S(...) custom-call(s32[3]{0:T(128)S(1)} %pad_add_fusion.where, ...), custom_call_target="tpu_custom_call", output_to_operand_aliasing={{0}: (6, {}), {1}: (7, {}), {2}: (8, {}), {3}: (9, {}), {4}... | custom-call | tf_op jit(solution)/shard_map/pallas_call | solution.py:229
  37.5 12.5 %all_to_all.16.gram = f32[8,16,128]{2,1,0:T(8,128)S(1)} all-to-all(f32[8,16,128]{2,1,0:T(8,128)S(1)} %get-tuple-element.67), channel_id=1, replica_groups=mesh['sys'=4,'slab'=8] {'slab'}, dimensions={0} | all-to-all | bytes 131072 | tf_op jit(solution)/shard_map/all_to_all | solution.py:413
  50.0 1.4 %shard_map.45 = (f32[16,128,128]{2,1,0:T(8,128)S(1)}, f32[5,128,128]{2,1,0:T(8,128)S(1)}, f32[5,128,128]{2,1,0:T(8,128)S(1)}, f32[4,16,128]{2,1,0:T(8,128)S(1)}) custom-call(s32[3]{0:T(128)S(1)} %pad_add_fusion.where, f32[8,128]{1,0:T(8,128)S(1)} %get-tuple-element.59.size, f32[8,16,128]{2,1,0:T(8,128)S(1)} %all_to_all.16.gram, f32[16,128,128]{2,1,0:T(8,128)S(1)} %copy-done, ...), custom_call_target="tpu_custom_call" | custom-call | tf_op jit(solution)/shard_map/pallas_call | solution.py:229
  51.4 0.5 collective-permute-start.3
  51.9 4.3 %shard_map.46 = (f32[16,128,128]{2,1,0:T(8,128)S(1)}, f32[16,128,128]{2,1,0:T(8,128)S(1)}, f32[16,128,128]{2,1,0:T(8,128)S(1)}, f32[16,128,128]{2,1,0:T(8,128)S(...) custom-call(f32[16,128,128]{2,1,0:T(8,128)S(1)} %get-tuple-element.7, ...), custom_call_target="tpu_custom_call", output_to_operand_aliasing={{5}: (3, {})} | custom-call | tf_op jit(solution)/shard_map/pallas_call | solution.py:229
  56.2 0.7 collective-permute-start.2
  56.9 1.8 %collective-permute-done.3.got = f32[5,128,128]{2,1,0:T(8,128)S(1)} collective-permute-done((f32[5,128,128]{2,1,0:T(8,128)S(1)}, f32[5,128,128]{2,1,0:T(8,128)S(1)}, u32[]{:S(2)}, u32[]{:S(2)}) %collective-permute-start.3) | collective-permute-done | bytes 327712 | tf_op jit(solution)/shard_map/ppermute | solution.py:405
  58.7 3.2 %shard_map.47 = (f32[16,128,128]{2,1,0:T(8,128)S(1)}, f32[16,128,128]{2,1,0:T(8,128)S(1)}, f32[16,128,128]{2,1,0:T(8,128)S(1)}, f32[16,128,128]{2,1,0:T(8,128)S(...) custom-call(s32[3]{0:T(128)S(1)} %pad_add_fusion.where, ...), custom_call_target="tpu_custom_call", output_to_operand_aliasing={{0}: (12, {}), {1}: (13, {}), {2}: (14, {}), {3}: (15, {}),... | custom-call | tf_op jit(solution)/shard_map/pallas_call | solution.py:229
  61.9 0.0 collective-permute-done.2.got
  61.9 3.3 %shard_map.48 = (f32[16,128,128]{2,1,0:T(8,128)S(1)}, f32[16,128,128]{2,1,0:T(8,128)S(1)}, f32[16,128,128]{2,1,0:T(8,128)S(1)}, f32[16,128,128]{2,1,0:T(8,128)S(...) custom-call(s32[3]{0:T(128)S(1)} %pad_add_fusion.where, ...), custom_call_target="tpu_custom_call", output_to_operand_aliasing={{0}: (12, {}), {1}: (13, {}), {2}: (14, {}), {3}: (15, {}),... | custom-call | tf_op jit(solution)/shard_map/pallas_call | solution.py:229
  65.2 13.8 %all_to_all.17.gram = f32[8,16,128]{2,1,0:T(8,128)S(1)} all-to-all(f32[8,16,128]{2,1,0:T(8,128)S(1)} %get-tuple-element.92), channel_id=1, replica_groups=mesh['sys'=4,'slab'=8] {'slab'}, dimensions={0} | all-to-all | bytes 131072 | tf_op jit(solution)/shard_map/all_to_all | solution.py:413
  78.9 3.6 %shard_map.49 = (f32[16,128,128]{2,1,0:T(8,128)}, f32[16,128,128]{2,1,0:T(8,128)}) custom-call(f32[8,128]{1,0:T(8,128)S(1)} %get-tuple-element.59.size, f32[4,16,128]{2,1,0:T(8,128)S(1)} %get-tuple-element.73.state, f32[8,16,128]{2,1,0:T(8,128)S(1)} %all_to_all.17.gram, f32[16,128,128]{2,1,0:T(8,128)S(1)} %copy-done, ...), custom_call_target="tpu_custom_call" | custom-call | tf_op jit(solution)/shard_map/pallas_call | solution.py:229
  (1 shorter events, 0.0 us)
Async XLA Ops:
  0.7 5.1 %copy-start = (f32[16,128,128]{2,1,0:T(8,128)S(1)}, f32[16,128,128]{2,1,0:T(8,128)}, u32[]{:S(2)}) copy-start(f32[16,128,128]{2,1,0:T(8,128)} %refs_0_.9) | copy-start | bytes 3145732
  0.7 5.1 %copy-start.1 = (f32[16,128,128]{2,1,0:T(8,128)S(1)}, f32[16,128,128]{2,1,0:T(8,128)}, u32[]{:S(2)}) copy-start(f32[16,128,128]{2,1,0:T(8,128)} %diag.3) | copy-start | bytes 3145732
  2.8 28.6 %collective-permute-start = (f32[9,128,128]{2,1,0:T(8,128)S(1)}, f32[9,128,128]{2,1,0:T(8,128)S(1)}, u32[]{:S(2)}, u32[]{:S(2)}) collective-permute-start(f32[9,128,128]{2,1,0:T(8,128)S(1)} %get-tuple-element.50), channel_id=1, source_target_pairs={{0,1},{1,0},{2,3},{3,2},{4,5},{5,4},{6,7},{7,6},{8,9},{9,8},{10,11... | collective-permute-start | bytes 1769480 | tf_op jit(solution)/shard_map/ppermute | solution.py:405
  8.6 26.3 %collective-permute-start.1 = (f32[9,128,128]{2,1,0:T(8,128)S(1)}, f32[9,128,128]{2,1,0:T(8,128)S(1)}, u32[]{:S(2)}, u32[]{:S(2)}) collective-permute-start(f32[9,128,128]{2,1,0:T(8,128)S(1)} %get-tuple-element.60), channel_id=1, source_target_pairs={{1,2},{3,4},{5,6},{2,1},{4,3},{6,5},{9,10},{11,12},{13,14},{10,9},... | collective-permute-start | bytes 1769480 | tf_op jit(solution)/shard_map/ppermute | solution.py:409
  51.4 7.2 %collective-permute-start.3 = (f32[5,128,128]{2,1,0:T(8,128)S(1)}, f32[5,128,128]{2,1,0:T(8,128)S(1)}, u32[]{:S(2)}, u32[]{:S(2)}) collective-permute-start(f32[5,128,128]{2,1,0:T(8,128)S(1)} %get-tuple-element.78), channel_id=1, source_target_pairs={{0,1},{1,0},{2,3},{3,2},{4,5},{5,4},{6,7},{7,6},{8,9},{9,8},{10,11... | collective-permute-start | bytes 983048 | tf_op jit(solution)/shard_map/ppermute | solution.py:405
  56.2 5.7 %collective-permute-start.2 = (f32[5,128,128]{2,1,0:T(8,128)S(1)}, f32[5,128,128]{2,1,0:T(8,128)S(1)}, u32[]{:S(2)}, u32[]{:S(2)}) collective-permute-start(f32[5,128,128]{2,1,0:T(8,128)S(1)} %get-tuple-element.76), channel_id=1, source_target_pairs={{1,2},{3,4},{5,6},{2,1},{4,3},{6,5},{9,10},{11,12},{13,14},{10,9},... | collective-permute-start | bytes 983048 | tf_op jit(solution)/shard_map/ppermute | solution.py:409

commit v4 on v3

v4 whole, which is shorter than its diff:
```python
import functools

import jax
import jax.numpy as jnp
from jax import lax
from jax.experimental import pallas as pl
from jax.experimental.pallas import tpu as pltpu
from jax.sharding import PartitionSpec as P

WIDTH = 5
LAST = 2 * WIDTH
LOW, HIGH = 0.25, 14.0
CENTER = (LOW + HIGH) / 2
HALF = (HIGH - LOW) / 2
ROWS, LANES = 16, 128
PARTS = 4
F32 = jnp.float32


def tile(at, row):
    ref, z = at
    return ref[z, pl.ds(row, 8), :]


def advance(out, cur, above, below, scale, prev=None, keep=None):
    _, ny, nx = cur[0].shape
    row = lax.broadcasted_iota(jnp.int32, (8, nx), 0)
    lane = lax.broadcasted_iota(jnp.int32, (8, nx), 1)
    zero = jnp.zeros((8, nx), F32)
    for at in range(0, ny, 8):
        mid = tile(cur, at)
        beside = tile(above, at) + tile(below, at)
        if at:
            beside = beside + tile(cur, at - 1)
        else:
            beside = beside + jnp.where(row == 0, zero, pltpu.roll(mid, 1, 0))
        if at + 8 < ny:
            beside = beside + tile(cur, at + 1)
        else:
            beside = beside + jnp.where(row == 7, zero, pltpu.roll(mid, 7, 0))
        left = jnp.where(lane == 0, zero, pltpu.roll(mid, 1, 1))
        right = jnp.where(lane == nx - 1, zero, pltpu.roll(mid, nx - 1, 1))
        beside = beside + (left + right)
        image = tile(scale, at) * mid - (2.0 / HALF) * beside
        image = 0.5 * image if prev is None else image - tile(prev, at)
        if keep is not None:
            image = image * keep
        out[0][out[1], pl.ds(at, 8), :] = image


def scaled(diag):
    return (2.0 / HALF) * diag + (2.0 / HALF) * (6.0 - CENTER)


def over(first, last, most, body):
    count = last - first
    step = max(k for k in range(1, most + 1) if count % k == 0)

    def run(i, carry):
        for k in range(step):
            body(first + i * step + k)
        return carry

    lax.fori_loop(0, count // step, run, 0)


def interior(fields, scale):
    planes = scale.shape[0]
    for j in range(1, WIDTH + 1):

        def body(z, j=j):
            old = None if j == 1 else (fields[j - 2], z)
            cur = fields[j - 1]
            advance((fields[j], z), (cur, z), (cur, z + 1), (cur, z - 1), (scale, z), old)

        over(j, planes - j, 7, body)


def edge(where, use_a, planes):
    even = where[0] == 0
    high = even if use_a else jnp.logical_not(even)
    base = jnp.where(high, planes - 1, 0)
    inward = jnp.where(high, -1, 1)
    return high, base, inward, jnp.where(high, where[2], where[1]).astype(F32)


def wedge(fields, got, ghosts, scale, ghost_scale, base, inward, keep):
    def at(j, i):
        if i >= 0:
            return fields[j], base + inward * i
        if j:
            return ghosts[j - 1], -1 - i
        return got, jnp.where(inward < 0, -1 - i, WIDTH + i)

    def scale_at(i):
        return (scale, base + inward * i) if i >= 0 else (ghost_scale, -1 - i)

    for j in range(1, WIDTH + 1):
        for i in range(j - WIDTH, j):
            old = None if j == 1 else at(j - 2, i)
            mask = keep if i < 0 else None
            advance(at(j, i), at(j - 1, i), at(j - 1, i + 1), at(j - 1, i - 1), scale_at(i), old, mask)


def lower(base, high, count=WIDTH):
    return jnp.where(high, base - (count - 1), base)


def put_sides(where, field, side_a, side_b):
    planes = field.shape[0]
    for side, use_a in ((side_a, True), (side_b, False)):
        high, base, _, _ = edge(where, use_a, planes)
        first = lower(base, high)
        for k in range(WIDTH):
            side[k] = field[first + k]


def row_index():
    return lax.broadcasted_iota(jnp.int32, (ROWS, LANES), 0)


def unit(k):
    return jnp.where(row_index() == k, 1.0, 0.0).astype(F32)


def entry(v, k):
    return jnp.broadcast_to(v[k : k + 1, :], (ROWS, LANES))


def columns(mat, count):
    return [jnp.broadcast_to(mat[:, j : j + 1], (ROWS, LANES)) for j in range(count)]


def product(cols, v):
    return functools.reduce(lambda a, b: a + b, [c * entry(v, k) for k, c in enumerate(cols)])


def dot(a, b):
    return jnp.broadcast_to(jnp.sum(a * b, axis=0, keepdims=True), (ROWS, LANES))


def steps(gram, mat, count):
    x, r, p = 0.0 * unit(0), unit(0), unit(0)
    norm = dot(r, product(gram, r))
    for _ in range(count):
        image = product(mat, p)
        size = norm / dot(p, product(gram, image))
        x = x + size * p
        r = r - size * image
        new = dot(r, product(gram, r))
        p = r + (new / norm) * p
        norm = new
    return x, r, norm


def chebyshev_column(first, k):
    out = CENTER * unit(k) + (HALF if k == first else HALF / 2) * unit(k + 1)
    return out if k == first else out + (HALF / 2) * unit(k - 1)


def to_powers(size, count):
    cols = [unit(0)]
    for j in range(count):
        cols.append(unit(j) - size * chebyshev_column(0, j))
    return cols


def gram_tile(rows):
    ri = row_index()
    ci = lax.broadcasted_iota(jnp.int32, (ROWS, LANES), 1)
    out = jnp.zeros((ROWS, LANES), F32)
    blank = jnp.zeros((1, LANES), F32)
    for j in sorted({j for _, j in rows}):
        stack = jnp.concatenate([rows.get((i, j), blank) for i in range(ROWS)], axis=0)
        col = jnp.sum(stack, axis=1, keepdims=True)
        out = out + jnp.where(ci == j, col, 0.0)
        row = jnp.sum(jnp.where(ri == ci, col, 0.0), axis=0, keepdims=True)
        out = out + jnp.where((ri == j) & (ci < j), row, 0.0)
    return out


def inner_products(first, count, ny, load, pairs, acc):
    zero = jnp.zeros(acc.shape[1:], F32)
    for k in range(len(pairs)):
        acc[k] = zero

    def body(k, carry):
        z = first + k
        sums = [None] * len(pairs)
        for row in range(0, ny, 8):
            tiles = load(z, row)
            for k, (i, j) in enumerate(pairs):
                part = tiles[i] * tiles[j]
                sums[k] = part if row == 0 else sums[k] + part
        for k, val in enumerate(sums):
            acc[k] = acc[k] + val
        return carry

    lax.fori_loop(0, count, body, 0)
    return {pair: jnp.sum(acc[k], axis=0, keepdims=True) for k, pair in enumerate(pairs)}


def pairs_of(first, last):
    return [(i, j) for j in range(first, last) for i in range(j + 1)]


def shifted(powers, size, count):
    keep = 1.0 - size * CENTER
    move = size * (HALF / 2)
    out = [powers[0], keep * powers[0] - (2.0 * move) * powers[1]]
    for j in range(1, count):
        out.append(keep * powers[j] - move * (powers[j + 1] + powers[j - 1]))
    return out


def gathered(ref):
    return functools.reduce(lambda a, b: a + b, [ref[k] for k in range(ref.shape[0])])


def spread(ref, value):
    for k in range(ref.shape[0]):
        ref[k] = value


def call(kernel, outs, aliases=None, scratch=(), hbm=(), out_space=pltpu.VMEM):
    def spec(k, a):
        if a.dtype == jnp.int32:
            return pl.BlockSpec(memory_space=pltpu.SMEM)
        return pl.BlockSpec(memory_space=pltpu.HBM if k in hbm else pltpu.VMEM)

    def run(*args):
        return pl.pallas_call(
            kernel,
            out_shape=[jax.ShapeDtypeStruct(s, F32) for s in outs],
            in_specs=[spec(k, a) for k, a in enumerate(args)],
            out_specs=[pl.BlockSpec(memory_space=out_space) for _ in outs],
            scratch_shapes=list(scratch),
            input_output_aliases=aliases or {},
            compiler_params=pltpu.CompilerParams(vmem_limit_bytes=16 << 20),
        )(*args)

    return run


def side_kernel(where, rhs, diag, side_a, side_b, sems):
    copies = []
    for side, use_a in ((side_a, True), (side_b, False)):
        high, base, _, _ = edge(where, use_a, rhs.shape[0])
        for source, at, count in ((rhs, 0, WIDTH), (diag, WIDTH, WIDTH - 1)):
            planes = source.at[pl.ds(lower(base, high, count), count)]
            copies.append(pltpu.make_async_copy(planes, side.at[pl.ds(at, count)], sems.at[len(copies)]))
    for copy in copies:
        copy.start()
    for copy in copies:
        copy.wait()


def open_kernel(rhs_far, diag_far, side_in, scale, *refs):
    powers, (side, gram, acc, diag, sems) = refs[: WIDTH + 1], refs[WIDTH + 1 :]
    rhs = powers[0]
    planes, ny, _ = rhs.shape
    copies = [
        pltpu.make_async_copy(far, near, sems.at[k])
        for k, (far, near) in enumerate(((diag_far, diag), (rhs_far, rhs)))
    ]
    for copy in copies:
        copy.start()
    for copy in copies:
        copy.wait()

    def fill(z):
        scale[z] = scaled(diag[z])

    over(0, planes, 4, fill)
    interior(powers, scale)
    load = lambda z, row: [tile((ref, z), row) for ref in powers]
    pairs = pairs_of(0, WIDTH + 1)
    spread(gram, gram_tile(inner_products(WIDTH, planes - 2 * WIDTH, ny, load, pairs, acc)))


def basis_gram(powers, fields, size, first, count, pairs, acc):
    ny = powers[0].shape[1]

    def load(z, row):
        out = shifted([tile((ref, z), row) for ref in powers], size, WIDTH - 1)
        return out + [tile((ref, z), row) for ref in fields]

    rows = {}
    for at in range(0, len(pairs), 26):
        rows.update(inner_products(first, count, ny, load, pairs[at : at + 26], acc))
    return gram_tile(rows)


def restart(sampled):
    gram = columns(sampled, WIDTH + 1)
    norm, cross = entry(gram[0], 0), entry(gram[0], 1)
    size = norm / (CENTER * norm + HALF * cross)
    size = jnp.where((size > 0.5 / HIGH) & (size < 2.0 / LOW), size, 1.0 / CENTER)
    _, coef, left = steps(gram, [chebyshev_column(0, k) for k in range(WIDTH)], WIDTH)
    plain = unit(WIDTH - 1) - size * chebyshev_column(0, WIDTH - 1)
    return size, jnp.where((left > 0.0) & (left < 0.25 * norm), coef, plain)


def wedges_kernel(where, got_a, got_b, scale, sampled, t0, *refs):
    powers, refs = (t0,) + refs[WIDTH : 2 * WIDTH], refs[2 * WIDTH :]
    ghost_scales, (field, side_a, side_b, state), refs = refs[:2], refs[2:6], refs[6:]
    ghosts = refs[: WIDTH - 1], refs[WIDTH - 1 :]
    planes, ny, _ = t0.shape
    for use_a, got, ghost_scale, ghost in zip((True, False), (got_a, got_b), ghost_scales, ghosts):
        high, base, inward, keep = edge(where, use_a, planes)
        for k in range(WIDTH - 1):
            ghost_scale[k] = scaled(got[jnp.where(high, WIDTH + k, 2 * WIDTH - 2 - k)])
        wedge(powers, got, ghost, scale, ghost_scale, base, inward, keep)
    size, coef = restart(gathered(sampled))
    state[0] = size
    state[1] = coef
    weights = [coef[i : i + 1, :] for i in range(WIDTH + 1)]

    def body(z, carry):
        for row in range(0, ny, 8):
            out = weights[0] * tile((powers[0], z), row)
            for i in range(1, WIDTH + 1):
                out = out + weights[i] * tile((powers[i], z), row)
            field[z, pl.ds(row, 8), :] = out
        return carry

    lax.fori_loop(0, planes, body, 0)
    put_sides(where, field, side_a, side_b)


LOW_PAIRS = pairs_of(0, WIDTH)
HIGH_PAIRS = pairs_of(WIDTH, LAST + 1)


def fresh_kernel(v0, scale, state, side_in, *refs):
    powers, refs = refs[:WIDTH], refs[WIDTH:]
    fields, (side, gram, acc) = (v0,) + refs[:WIDTH], refs[WIDTH:]
    planes = v0.shape[0]
    size = state[0, 0:1, 0:1]
    interior(fields, scale)
    gram[...] = basis_gram(powers, (), size, 0, planes, LOW_PAIRS, acc)


def inner_kernel(v0, state, early, *refs):
    powers, fields, (gram, acc) = refs[:WIDTH], (v0,) + refs[WIDTH : 2 * WIDTH], refs[2 * WIDTH :]
    inner = v0.shape[0] - 2 * WIDTH
    gram[...] = early[...] + basis_gram(powers, fields, state[0, 0:1, 0:1], WIDTH, inner, HIGH_PAIRS, acc)


def fresh_wedge(use_a, where, got, scale, ghost_scale, state, early, v0, *refs):
    powers, refs = refs[:WIDTH], refs[WIDTH:]
    fields, gram = (v0,) + refs[WIDTH : 2 * WIDTH], refs[2 * WIDTH]
    ghosts, acc = refs[2 * WIDTH + 1 : -1], refs[-1]
    high, base, inward, keep = edge(where, use_a, v0.shape[0])
    wedge(fields, got, ghosts, scale, ghost_scale, base, inward, keep)
    first = lower(base, high)
    late = basis_gram(powers, fields, state[0, 0:1, 0:1], first, WIDTH, HIGH_PAIRS, acc)
    if use_a:
        gram[...] = early[...] + late
    else:
        spread(gram, early[...] + late)


def operator_columns(size, coef):
    powers = [unit(0)]
    for j in range(WIDTH - 1):
        image = (1.0 / size) * (powers[j] - unit(1 + j)) - CENTER * powers[j]
        powers.append((1.0 / HALF) * image if j == 0 else (2.0 / HALF) * image - powers[j - 1])
    rest = unit(WIDTH) - product(powers, coef)
    powers.append(rest / entry(coef, WIDTH))
    beyond = (HALF / 2) * (powers[WIDTH] + powers[WIDTH - 2]) + CENTER * powers[WIDTH - 1]
    beyond = powers[WIDTH - 1] - size * beyond
    out = [(1.0 / size) * (unit(0) - unit(1))]
    out += [chebyshev_column(1, k) for k in range(1, WIDTH - 1)]
    out.append(CENTER * unit(WIDTH - 1) + (HALF / 2) * (unit(WIDTH - 2) + beyond))
    return out + [chebyshev_column(WIDTH, k) for k in range(WIDTH, LAST)]


def finish_kernel(state, gram, *refs):
    count = LAST + 1
    refs, outs, rooms, sems = refs[:count], refs[count : count + 2], refs[count + 2 : count + 4], refs[-1]
    size = state[0]
    full = columns(gathered(gram), count)
    x, r, _ = steps(full, operator_columns(size, state[1]), LAST)
    back = to_powers(size, WIDTH - 1) + [unit(k) for k in range(WIDTH, count)]
    x, r = product(back, x), product(back, r)
    sx = [x[i : i + 1, :] for i in range(count)]
    sr = [r[i : i + 1, :] for i in range(count)]
    planes, ny, _ = refs[0].shape

    def body(z, carry):
        for row in range(0, ny, 8):
            tiles = [tile((ref, z), row) for ref in refs]
            ax, ar = sx[0] * tiles[0], sr[0] * tiles[0]
            for i in range(1, count):
                ar = ar + sr[i] * tiles[i]
                if i + 1 < count:
                    ax = ax + sx[i] * tiles[i]
            rooms[0][z, pl.ds(row, 8), :] = ax
            rooms[1][z, pl.ds(row, 8), :] = ar
        return carry

    copies = []
    part = planes // PARTS
    for k in range(PARTS):
        lax.fori_loop(k * part, (k + 1) * part, body, 0)
        here = pl.ds(k * part, part)
        for room, out in zip(rooms, outs):
            copies.append(pltpu.make_async_copy(room.at[here], out.at[here], sems.at[len(copies)]))
            copies[-1].start()
    for copy in copies:
        copy.wait()


def pairings(count):
    first = [(i, i ^ 1) for i in range(count) if i ^ 1 < count]
    second = [(i, i + 1) for i in range(1, count - 1, 2)]
    return first, second + [(j, i) for i, j in second]


def swap_a(side):
    return lax.ppermute(side, "slab", pairings(lax.axis_size("slab"))[0])


def swap_b(side):
    return lax.ppermute(side, "slab", pairings(lax.axis_size("slab"))[1])


def swap_all(value):
    return lax.all_to_all(value, "slab", 0, 0)


def local(right_side, diagonal):
    index = lax.axis_index("slab")
    count = lax.axis_size("slab")
    where = jnp.stack([index % 2, index > 0, index < count - 1]).astype(jnp.int32)
    field = right_side.shape
    some = lambda k: (k,) + field[1:]
    fields = [field] * WIDTH
    small = (ROWS, LANES)
    wide = (count,) + small
    ghosts = tuple(pltpu.VMEM(some(WIDTH - j), F32) for j in range(1, WIDTH))
    acc = lambda k: pltpu.VMEM((k, 8, LANES), F32)
    ghost_side = some(WIDTH - 1)

    message = some(2 * WIDTH - 1)
    rhs, diag = (pltpu.with_memory_space_constraint(a, pltpu.HBM) for a in (right_side, diagonal))
    semaphores = pltpu.SemaphoreType.DMA
    sa, sb = call(side_kernel, [message] * 2, scratch=(semaphores((4,)),), hbm=(1, 2))(where, rhs, diag)
    got_a = swap_a(sa)
    d, t0, *powers, sb, sampled = call(
        open_kernel,
        [field] * 2 + fields + [message, wide],
        {2: 2 + WIDTH},
        (acc(24), pltpu.VMEM(field, F32), semaphores((2,))),
        hbm=(0, 1),
    )(rhs, diag, sb)
    got_b = swap_b(sb)
    sampled = swap_all(sampled)
    inner = {6 + k: k for k in range(WIDTH)}
    side = some(WIDTH)
    *powers, gd_a, gd_b, v0, sa, sb, state = call(
        wedges_kernel, fields + [ghost_side] * 2 + [field, side, side, (2,) + small], inner, ghosts * 2
    )(where, got_a, got_b, d, sampled, t0, *powers)
    powers = [t0] + powers[:-1]
    got_a = swap_a(sa)
    *late, sb, early = call(fresh_kernel, fields + [side, small], {3: WIDTH}, (acc(26),))(v0, d, state, sb, *powers)
    got_b = swap_b(sb)
    early = call(inner_kernel, [small], scratch=(acc(26),))(v0, state, early, *powers, *late)[0]
    inner = {7 + WIDTH + k: k for k in range(WIDTH)}
    scratch = ghosts + (acc(26),)
    *late, early = call(functools.partial(fresh_wedge, True), fields + [small], inner, scratch)(
        where, got_a, d, gd_a, state, early, v0, *powers, *late
    )
    *late, gram = call(functools.partial(fresh_wedge, False), fields + [wide], inner, scratch)(
        where, got_b, d, gd_b, state, early, v0, *powers, *late
    )
    gram = swap_all(gram)
    rooms = (pltpu.VMEM(field, F32),) * 2 + (semaphores((2 * PARTS,)),)
    finish = call(finish_kernel, [field] * 2, scratch=rooms, out_space=pltpu.HBM)
    return tuple(finish(state, gram, *powers, v0, *late))


def solution(mesh):
    placed = (P("slab", "sys", None), P("slab", "sys", None))
    return jax.shard_map(
        local,
        mesh=mesh,
        in_specs=placed,
        out_specs=placed,
        check_vma=False,
    )
```

time: 82.8 us -> 70.8 us (0.86)
  blocking collectives: 48.4 us -> 35.7 us
  starting transfers between devices: 4.89 us -> 6.99 us
  waiting for transfers between devices: 1.79 us -> 0.01 us
    all_to_all x3 -> x2, blocking collectives: 48.4 us -> 35.7 us  [swap_all(): return lax.all_to_all(value, 'slab', 0, 0)]
    ppermute x2, starting transfers between devices: 3.51 us -> 5.61 us  [swap_a(): return lax.ppermute(side, 'slab', pairings(lax.axis_size('slab'))[0])]
    ppermute x2, waiting for transfers between devices: 1.79 us -> 0.01 us  [swap_a(): return lax.ppermute(side, 'slab', pairings(lax.axis_size('slab'))[0])]
    pallas_call x9 -> x8, Pallas kernels: 26.7 us -> 27 us  [run(): pl.pallas_call(kernel, out_shape=[jax.ShapeDtypeStruct(s, F32) for s in o...]
  transfers between devices with their start and end apart: 4 -> 4, of which waited for: 1 -> 0; matrix products, arithmetic and copies ran while one was open for 0% -> 0% of each run, Pallas kernels for 17% -> 21%
where the time goes in v4:
time: 70.8 us; the launch traced here: 70.5 us
  blocking collectives  35.7 us (50%)
  Pallas kernels  27 us (38%)
  starting transfers between devices  6.99 us (10%)
    all_to_all x2, blocking collectives, swap_all(): return lax.all_to_all(value, 'slab', 0, 0)  35.7 us
    pallas_call x8, Pallas kernels, run(): pl.pallas_call(kernel, out_shape=[jax.ShapeDtypeStruct(s, F32) for s in o...  27 us
    ppermute x2, starting transfers between devices, swap_a(): return lax.ppermute(side, 'slab', pairings(lax.axis_size('slab'))[0])  5.61 us
  transfers between devices with their start and end apart: 4, of which 0 were waited for; matrix products, arithmetic and copies ran while one was open for 0% of the time, Pallas kernels for 21%

profile of v4, /device:TPU:0, one launch (start us, length us, event | category | flops | bytes accessed | tf_op | source)
XLA Modules:
  0.0 70.5 jit_solution(15750731942647725553)
XLA Ops:
  0.6 0.1 pad_add_fusion.where
  0.7 1.8 %shard_map.41 = (f32[9,128,128]{2,1,0:T(8,128)S(1)}, f32[9,128,128]{2,1,0:T(8,128)S(1)}) custom-call(s32[3]{0:T(128)S(1)} %pad_add_fusion.where, f32[16,128,128]{2,1,0:T(8,128)} %rhs_far.1, f32[16,128,128]{2,1,0:T(8,128)} %diag_far.1), custom_call_target="tpu_custom_call" | custom-call | tf_op jit(solution)/shard_map/pallas_call | solution.py:232
  2.5 3.1 %collective-permute-start = (f32[9,128,128]{2,1,0:T(8,128)S(1)}, f32[9,128,128]{2,1,0:T(8,128)S(1)}, u32[]{:S(2)}, u32[]{:S(2)}) collective-permute-start(f32[9,128,128]{2,1,0:T(8,128)S(1)} %get-tuple-element.42), channel_id=1, source_target_pairs={{0,1},{1,0},{2,3},{3,2},{4,5},{5,4},{6,7},{7,6},{8,9},{9,8},{10,11... | collective-permute-start | bytes 1769480 | tf_op jit(solution)/shard_map/ppermute | solution.py:422
  5.6 4.9 %shard_map.42 = (f32[16,128,128]{2,1,0:T(8,128)S(1)}, f32[16,128,128]{2,1,0:T(8,128)S(1)}, f32[16,128,128]{2,1,0:T(8,128)S(1)}, f32[16,128,128]{2,1,0:T(8,128)S(...) custom-call(f32[16,128,128]{2,1,0:T(8,128)} %rhs_far.1, ...), custom_call_target="tpu_custom_call", output_to_operand_aliasing={{7}: (2, {})} | custom-call | tf_op jit(solution)/shard_map/pallas_call | solution.py:232
  10.5 0.7 collective-permute-start.1
  11.2 20.3 %all_to_all.10.sampled = f32[8,16,128]{2,1,0:T(8,128)S(1)} all-to-all(f32[8,16,128]{2,1,0:T(8,128)S(1)} %get-tuple-element.46), channel_id=1, replica_groups=mesh['sys'=4,'slab'=8] {'slab'}, dimensions={0} | all-to-all | bytes 131072 | tf_op jit(solution)/shard_map/all_to_all | solution.py:430
  31.5 0.0 collective-permute-done.got_a
  31.5 0.0 collective-permute-done.1.got_b
  31.5 3.5 %shard_map.43 = (f32[16,128,128]{2,1,0:T(8,128)S(1)}, f32[16,128,128]{2,1,0:T(8,128)S(1)}, f32[16,128,128]{2,1,0:T(8,128)S(1)}, f32[16,128,128]{2,1,0:T(8,128)S(...) custom-call(s32[3]{0:T(128)S(1)} %pad_add_fusion.where, ...), custom_call_target="tpu_custom_call", output_to_operand_aliasing={{0}: (6, {}), {1}: (7, {}), {2}: (8, {}), {3}: (9, {}), {4}... | custom-call | tf_op jit(solution)/shard_map/pallas_call | solution.py:232
  35.0 2.5 %collective-permute-start.3 = (f32[5,128,128]{2,1,0:T(8,128)S(1)}, f32[5,128,128]{2,1,0:T(8,128)S(1)}, u32[]{:S(2)}, u32[]{:S(2)}) collective-permute-start(f32[5,128,128]{2,1,0:T(8,128)S(1)} %get-tuple-element.62), channel_id=1, source_target_pairs={{0,1},{1,0},{2,3},{3,2},{4,5},{5,4},{6,7},{7,6},{8,9},{9,8},{10,11... | collective-permute-start | bytes 983048 | tf_op jit(solution)/shard_map/ppermute | solution.py:422
  37.6 4.6 %shard_map.44 = (f32[16,128,128]{2,1,0:T(8,128)S(1)}, f32[16,128,128]{2,1,0:T(8,128)S(1)}, f32[16,128,128]{2,1,0:T(8,128)S(1)}, f32[16,128,128]{2,1,0:T(8,128)S(...) custom-call(f32[16,128,128]{2,1,0:T(8,128)S(1)} %get-tuple-element.5, ...), custom_call_target="tpu_custom_call", output_to_operand_aliasing={{5}: (3, {})} | custom-call | tf_op jit(solution)/shard_map/pallas_call | solution.py:232
  42.2 0.7 collective-permute-start.2
  42.9 2.1 %shard_map.45.early = f32[16,128]{1,0:T(8,128)S(1)} custom-call(f32[16,128,128]{2,1,0:T(8,128)S(1)} %get-tuple-element.54.v0.refs_5_, f32[2,16,128]{2,1,0:T(8,128)S(1)} %get-tuple-element.53.state, f32[16,128]{1,0:T(8,128)S(1)} %get-tuple-element.64.early, f32[16,128,128]{2,1,0:T(8,128)S(1)} %get-tuple-element.47.t0.refs_0_, ...), custom_call_target="tpu_custom_call" | custom-call | tf_op jit(solution)/shard_map/pallas_call | solution.py:232
  45.0 0.0 collective-permute-done.3.got
  45.0 3.5 %shard_map.46 = (f32[16,128,128]{2,1,0:T(8,128)S(1)}, f32[16,128,128]{2,1,0:T(8,128)S(1)}, f32[16,128,128]{2,1,0:T(8,128)S(1)}, f32[16,128,128]{2,1,0:T(8,128)S(...) custom-call(s32[3]{0:T(128)S(1)} %pad_add_fusion.where, ...), custom_call_target="tpu_custom_call", output_to_operand_aliasing={{0}: (12, {}), {1}: (13, {}), {2}: (14, {}), {3}: (15, {}),... | custom-call | tf_op jit(solution)/shard_map/pallas_call | solution.py:232
  48.5 0.0 collective-permute-done.2.got
  48.5 3.5 %shard_map.47 = (f32[16,128,128]{2,1,0:T(8,128)S(1)}, f32[16,128,128]{2,1,0:T(8,128)S(1)}, f32[16,128,128]{2,1,0:T(8,128)S(1)}, f32[16,128,128]{2,1,0:T(8,128)S(...) custom-call(s32[3]{0:T(128)S(1)} %pad_add_fusion.where, ...), custom_call_target="tpu_custom_call", output_to_operand_aliasing={{0}: (12, {}), {1}: (13, {}), {2}: (14, {}), {3}: (15, {}),... | custom-call | tf_op jit(solution)/shard_map/pallas_call | solution.py:232
  52.0 15.4 %all_to_all.11.gram = f32[8,16,128]{2,1,0:T(8,128)S(1)} all-to-all(f32[8,16,128]{2,1,0:T(8,128)S(1)} %get-tuple-element.76), channel_id=1, replica_groups=mesh['sys'=4,'slab'=8] {'slab'}, dimensions={0} | all-to-all | bytes 131072 | tf_op jit(solution)/shard_map/all_to_all | solution.py:430
  67.4 3.1 %shard_map.48 = (f32[16,128,128]{2,1,0:T(8,128)}, f32[16,128,128]{2,1,0:T(8,128)}) custom-call(f32[2,16,128]{2,1,0:T(8,128)S(1)} %get-tuple-element.53.state, f32[8,16,128]{2,1,0:T(8,128)S(1)} %all_to_all.11.gram, f32[16,128,128]{2,1,0:T(8,128)S(1)} %get-tuple-element.47.t0.refs_0_, f32[16,128,128]{2,1,0:T(8,128)S(1)} %get-tuple-element.56.refs_1_, ...), custom_call_target="tpu_custom_call" | custom-call | tf_op jit(solution)/shard_map/pallas_call | solution.py:232
Async XLA Ops:
  2.5 29.0 %collective-permute-start = (f32[9,128,128]{2,1,0:T(8,128)S(1)}, f32[9,128,128]{2,1,0:T(8,128)S(1)}, u32[]{:S(2)}, u32[]{:S(2)}) collective-permute-start(f32[9,128,128]{2,1,0:T(8,128)S(1)} %get-tuple-element.42), channel_id=1, source_target_pairs={{0,1},{1,0},{2,3},{3,2},{4,5},{5,4},{6,7},{7,6},{8,9},{9,8},{10,11... | collective-permute-start | bytes 1769480 | tf_op jit(solution)/shard_map/ppermute | solution.py:422
  10.5 21.1 %collective-permute-start.1 = (f32[9,128,128]{2,1,0:T(8,128)S(1)}, f32[9,128,128]{2,1,0:T(8,128)S(1)}, u32[]{:S(2)}, u32[]{:S(2)}) collective-permute-start(f32[9,128,128]{2,1,0:T(8,128)S(1)} %get-tuple-element.44), channel_id=1, source_target_pairs={{1,2},{3,4},{5,6},{2,1},{4,3},{6,5},{9,10},{11,12},{13,14},{10,9},... | collective-permute-start | bytes 1769480 | tf_op jit(solution)/shard_map/ppermute | solution.py:426
  35.0 10.0 %collective-permute-start.3 = (f32[5,128,128]{2,1,0:T(8,128)S(1)}, f32[5,128,128]{2,1,0:T(8,128)S(1)}, u32[]{:S(2)}, u32[]{:S(2)}) collective-permute-start(f32[5,128,128]{2,1,0:T(8,128)S(1)} %get-tuple-element.62), channel_id=1, source_target_pairs={{0,1},{1,0},{2,3},{3,2},{4,5},{5,4},{6,7},{7,6},{8,9},{9,8},{10,11... | collective-permute-start | bytes 983048 | tf_op jit(solution)/shard_map/ppermute | solution.py:422
  42.2 6.3 %collective-permute-start.2 = (f32[5,128,128]{2,1,0:T(8,128)S(1)}, f32[5,128,128]{2,1,0:T(8,128)S(1)}, u32[]{:S(2)}, u32[]{:S(2)}) collective-permute-start(f32[5,128,128]{2,1,0:T(8,128)S(1)} %get-tuple-element.60), channel_id=1, source_target_pairs={{1,2},{3,4},{5,6},{2,1},{4,3},{6,5},{9,10},{11,12},{13,14},{10,9},... | collective-permute-start | bytes 983048 | tf_op jit(solution)/shard_map/ppermute | solution.py:426

commit v5 on v4

--- a/solution.py
+++ b/solution.py
@@ -13,7 +13,7 @@
 CENTER = (LOW + HIGH) / 2
 HALF = (HIGH - LOW) / 2
 ROWS, LANES = 16, 128
-PARTS = 4
+PARTS = 8
 F32 = jnp.float32
 
 
@@ -179,24 +179,27 @@
     return out
 
 
-def inner_products(first, count, ny, load, pairs, acc):
+def inner_products(ny, load, segments, acc):
+    pairs = list(dict.fromkeys(pair for _, _, some in segments for pair in some))
     zero = jnp.zeros(acc.shape[1:], F32)
     for k in range(len(pairs)):
         acc[k] = zero
-
-    def body(k, carry):
-        z = first + k
-        sums = [None] * len(pairs)
-        for row in range(0, ny, 8):
-            tiles = load(z, row)
-            for k, (i, j) in enumerate(pairs):
-                part = tiles[i] * tiles[j]
-                sums[k] = part if row == 0 else sums[k] + part
-        for k, val in enumerate(sums):
-            acc[k] = acc[k] + val
-        return carry
-
-    lax.fori_loop(0, count, body, 0)
+    for first, count, some in segments:
+        for at in range(0, len(some), 30):
+
+            def body(k, carry, first=first, some=some[at : at + 30]):
+                sums = [None] * len(some)
+                for row in range(0, ny, 8):
+                    tiles = load(first + k, row)
+                    for at, (i, j) in enumerate(some):
+                        part = tiles[i] * tiles[j]
+                        sums[at] = part if row == 0 else sums[at] + part
+                for pair, val in zip(some, sums):
+                    here = pairs.index(pair)
+                    acc[here] = acc[here] + val
+                return carry
+
+            lax.fori_loop(0, count, body, 0)
     return {pair: jnp.sum(acc[k], axis=0, keepdims=True) for k, pair in enumerate(pairs)}
 
 
@@ -274,21 +277,18 @@
     over(0, planes, 4, fill)
     interior(powers, scale)
     load = lambda z, row: [tile((ref, z), row) for ref in powers]
-    pairs = pairs_of(0, WIDTH + 1)
-    spread(gram, gram_tile(inner_products(WIDTH, planes - 2 * WIDTH, ny, load, pairs, acc)))
-
-
-def basis_gram(powers, fields, size, first, count, pairs, acc):
+    segments = [(WIDTH, planes - 2 * WIDTH, pairs_of(0, WIDTH + 1))]
+    spread(gram, gram_tile(inner_products(ny, load, segments, acc)))
+
+
+def basis_gram(powers, fields, size, segments, acc):
     ny = powers[0].shape[1]
 
     def load(z, row):
         out = shifted([tile((ref, z), row) for ref in powers], size, WIDTH - 1)
         return out + [tile((ref, z), row) for ref in fields]
 
-    rows = {}
-    for at in range(0, len(pairs), 26):
-        rows.update(inner_products(first, count, ny, load, pairs[at : at + 26], acc))
-    return gram_tile(rows)
+    return gram_tile(inner_products(ny, load, segments, acc))
 
 
 def restart(sampled):
@@ -329,7 +329,13 @@
 
 
 LOW_PAIRS = pairs_of(0, WIDTH)
-HIGH_PAIRS = pairs_of(WIDTH, LAST + 1)
+CROSS_PAIRS = [(i, j) for i, j in pairs_of(WIDTH, LAST + 1) if i < WIDTH]
+HIGH_PAIRS = CROSS_PAIRS + [pair for pair in pairs_of(WIDTH, LAST + 1) if pair[0] >= WIDTH]
+
+
+def side_segments(base, inward, early):
+    some = lambda i: [pair for pair in HIGH_PAIRS if (pair[1] - WIDTH <= i) == early]
+    return [(base + inward * i, 1, some(i)) for i in range(WIDTH)]
 
 
 def fresh_kernel(v0, scale, state, side_in, *refs):
@@ -338,13 +344,14 @@
     planes = v0.shape[0]
     size = state[0, 0:1, 0:1]
     interior(fields, scale)
-    gram[...] = basis_gram(powers, (), size, 0, planes, LOW_PAIRS, acc)
+    gram[...] = basis_gram(powers, (), size, [(0, planes, LOW_PAIRS)], acc)
 
 
 def inner_kernel(v0, state, early, *refs):
     powers, fields, (gram, acc) = refs[:WIDTH], (v0,) + refs[WIDTH : 2 * WIDTH], refs[2 * WIDTH :]
     inner = v0.shape[0] - 2 * WIDTH
-    gram[...] = early[...] + basis_gram(powers, fields, state[0, 0:1, 0:1], WIDTH, inner, HIGH_PAIRS, acc)
+    segments = [(WIDTH, inner, HIGH_PAIRS)]
+    gram[...] = early[...] + basis_gram(powers, fields, state[0, 0:1, 0:1], segments, acc)
 
 
 def fresh_wedge(use_a, where, got, scale, ghost_scale, state, early, v0, *refs):
@@ -353,12 +360,16 @@
     ghosts, acc = refs[2 * WIDTH + 1 : -1], refs[-1]
     high, base, inward, keep = edge(where, use_a, v0.shape[0])
     wedge(fields, got, ghosts, scale, ghost_scale, base, inward, keep)
-    first = lower(base, high)
-    late = basis_gram(powers, fields, state[0, 0:1, 0:1], first, WIDTH, HIGH_PAIRS, acc)
     if use_a:
-        gram[...] = early[...] + late
+        _, other, step, _ = edge(where, False, v0.shape[0])
+        segments = [(lower(base, high), WIDTH, HIGH_PAIRS)] + side_segments(other, step, True)
     else:
-        spread(gram, early[...] + late)
+        segments = side_segments(base, inward, False)
+    value = early[...] + basis_gram(powers, fields, state[0, 0:1, 0:1], segments, acc)
+    if use_a:
+        gram[...] = value
+    else:
+        spread(gram, value)
 
 
 def operator_columns(size, coef):
@@ -464,11 +475,11 @@
     )(where, got_a, got_b, d, sampled, t0, *powers)
     powers = [t0] + powers[:-1]
     got_a = swap_a(sa)
-    *late, sb, early = call(fresh_kernel, fields + [side, small], {3: WIDTH}, (acc(26),))(v0, d, state, sb, *powers)
+    *late, sb, early = call(fresh_kernel, fields + [side, small], {3: WIDTH}, (acc(56),))(v0, d, state, sb, *powers)
     got_b = swap_b(sb)
-    early = call(inner_kernel, [small], scratch=(acc(26),))(v0, state, early, *powers, *late)[0]
+    early = call(inner_kernel, [small], scratch=(acc(56),))(v0, state, early, *powers, *late)[0]
     inner = {7 + WIDTH + k: k for k in range(WIDTH)}
-    scratch = ghosts + (acc(26),)
+    scratch = ghosts + (acc(56),)
     *late, early = call(functools.partial(fresh_wedge, True), fields + [small], inner, scratch)(
         where, got_a, d, gd_a, state, early, v0, *powers, *late
     )

time: 70.8 us -> 70 us (0.989)
  transfers between devices with their start and end apart: 4 -> 4, of which waited for: 0 -> 0; matrix products, arithmetic and copies ran while one was open for 0% -> 0% of each run, Pallas kernels for 21% -> 22%
where the time goes in v5:
time: 70 us; the launch traced here: 69.8 us
  blocking collectives  35.4 us (51%)
  Pallas kernels  26.6 us (38%)
  starting transfers between devices  6.99 us (10%)
    all_to_all x2, blocking collectives, swap_all(): return lax.all_to_all(value, 'slab', 0, 0)  35.4 us
    pallas_call x8, Pallas kernels, run(): pl.pallas_call(kernel, out_shape=[jax.ShapeDtypeStruct(s, F32) for s in o...  26.6 us
    ppermute x2, starting transfers between devices, swap_a(): return lax.ppermute(side, 'slab', pairings(lax.axis_size('slab'))[0])  5.61 us
  transfers between devices with their start and end apart: 4, of which 0 were waited for; matrix products, arithmetic and copies ran while one was open for 0% of the time, Pallas kernels for 22%

profile of v5, /device:TPU:0, one launch (start us, length us, event | category | flops | bytes accessed | tf_op | source)
XLA Modules:
  0.0 69.8 jit_solution(5240802238398966039)
XLA Ops:
  0.6 0.1 pad_add_fusion.where
  0.7 1.8 %shard_map.41 = (f32[9,128,128]{2,1,0:T(8,128)S(1)}, f32[9,128,128]{2,1,0:T(8,128)S(1)}) custom-call(s32[3]{0:T(128)S(1)} %pad_add_fusion.where, f32[16,128,128]{2,1,0:T(8,128)} %rhs_far.1, f32[16,128,128]{2,1,0:T(8,128)} %diag_far.1), custom_call_target="tpu_custom_call" | custom-call | tf_op jit(solution)/shard_map/pallas_call | solution.py:235
  2.5 3.1 %collective-permute-start = (f32[9,128,128]{2,1,0:T(8,128)S(1)}, f32[9,128,128]{2,1,0:T(8,128)S(1)}, u32[]{:S(2)}, u32[]{:S(2)}) collective-permute-start(f32[9,128,128]{2,1,0:T(8,128)S(1)} %get-tuple-element.42), channel_id=1, source_target_pairs={{0,1},{1,0},{2,3},{3,2},{4,5},{5,4},{6,7},{7,6},{8,9},{9,8},{10,11... | collective-permute-start | bytes 1769480 | tf_op jit(solution)/shard_map/ppermute | solution.py:433
  5.6 4.9 %shard_map.42 = (f32[16,128,128]{2,1,0:T(8,128)S(1)}, f32[16,128,128]{2,1,0:T(8,128)S(1)}, f32[16,128,128]{2,1,0:T(8,128)S(1)}, f32[16,128,128]{2,1,0:T(8,128)S(...) custom-call(f32[16,128,128]{2,1,0:T(8,128)} %rhs_far.1, ...), custom_call_target="tpu_custom_call", output_to_operand_aliasing={{7}: (2, {})} | custom-call | tf_op jit(solution)/shard_map/pallas_call | solution.py:235
  10.5 0.7 %collective-permute-start.1 = (f32[9,128,128]{2,1,0:T(8,128)S(1)}, f32[9,128,128]{2,1,0:T(8,128)S(1)}, u32[]{:S(2)}, u32[]{:S(2)}) collective-permute-start(f32[9,128,128]{2,1,0:T(8,128)S(1)} %get-tuple-element.44), channel_id=1, source_target_pairs={{1,2},{3,4},{5,6},{2,1},{4,3},{6,5},{9,10},{11,12},{13,14},{10,9},... | collective-permute-start | bytes 1769480 | tf_op jit(solution)/shard_map/ppermute | solution.py:437
  11.2 20.3 %all_to_all.10.sampled = f32[8,16,128]{2,1,0:T(8,128)S(1)} all-to-all(f32[8,16,128]{2,1,0:T(8,128)S(1)} %get-tuple-element.46), channel_id=1, replica_groups=mesh['sys'=4,'slab'=8] {'slab'}, dimensions={0} | all-to-all | bytes 131072 | tf_op jit(solution)/shard_map/all_to_all | solution.py:441
  31.5 0.0 collective-permute-done.got_a
  31.5 0.0 collective-permute-done.1.got_b
  31.5 3.5 %shard_map.43 = (f32[16,128,128]{2,1,0:T(8,128)S(1)}, f32[16,128,128]{2,1,0:T(8,128)S(1)}, f32[16,128,128]{2,1,0:T(8,128)S(1)}, f32[16,128,128]{2,1,0:T(8,128)S(...) custom-call(s32[3]{0:T(128)S(1)} %pad_add_fusion.where, ...), custom_call_target="tpu_custom_call", output_to_operand_aliasing={{0}: (6, {}), {1}: (7, {}), {2}: (8, {}), {3}: (9, {}), {4}... | custom-call | tf_op jit(solution)/shard_map/pallas_call | solution.py:235
  35.0 2.5 %collective-permute-start.3 = (f32[5,128,128]{2,1,0:T(8,128)S(1)}, f32[5,128,128]{2,1,0:T(8,128)S(1)}, u32[]{:S(2)}, u32[]{:S(2)}) collective-permute-start(f32[5,128,128]{2,1,0:T(8,128)S(1)} %get-tuple-element.62), channel_id=1, source_target_pairs={{0,1},{1,0},{2,3},{3,2},{4,5},{5,4},{6,7},{7,6},{8,9},{9,8},{10,11... | collective-permute-start | bytes 983048 | tf_op jit(solution)/shard_map/ppermute | solution.py:433
  37.6 4.6 %shard_map.44 = (f32[16,128,128]{2,1,0:T(8,128)S(1)}, f32[16,128,128]{2,1,0:T(8,128)S(1)}, f32[16,128,128]{2,1,0:T(8,128)S(1)}, f32[16,128,128]{2,1,0:T(8,128)S(...) custom-call(f32[16,128,128]{2,1,0:T(8,128)S(1)} %get-tuple-element.5, ...), custom_call_target="tpu_custom_call", output_to_operand_aliasing={{5}: (3, {})} | custom-call | tf_op jit(solution)/shard_map/pallas_call | solution.py:235
  42.2 0.7 collective-permute-start.2
  42.9 1.9 %shard_map.45.early = f32[16,128]{1,0:T(8,128)S(1)} custom-call(f32[16,128,128]{2,1,0:T(8,128)S(1)} %get-tuple-element.54.v0.refs_5_, f32[2,16,128]{2,1,0:T(8,128)S(1)} %get-tuple-element.53.state, f32[16,128]{1,0:T(8,128)S(1)} %get-tuple-element.64.early, f32[16,128,128]{2,1,0:T(8,128)S(1)} %get-tuple-element.47.t0.refs_0_, ...), custom_call_target="tpu_custom_call" | custom-call | tf_op jit(solution)/shard_map/pallas_call | solution.py:235
  44.8 0.0 collective-permute-done.3.got
  44.8 4.0 %shard_map.46 = (f32[16,128,128]{2,1,0:T(8,128)S(1)}, f32[16,128,128]{2,1,0:T(8,128)S(1)}, f32[16,128,128]{2,1,0:T(8,128)S(1)}, f32[16,128,128]{2,1,0:T(8,128)S(...) custom-call(s32[3]{0:T(128)S(1)} %pad_add_fusion.where, ...), custom_call_target="tpu_custom_call", output_to_operand_aliasing={{0}: (12, {}), {1}: (13, {}), {2}: (14, {}), {3}: (15, {}),... | custom-call | tf_op jit(solution)/shard_map/pallas_call | solution.py:235
  48.8 0.0 collective-permute-done.2.got
  48.8 2.8 %shard_map.47 = (f32[16,128,128]{2,1,0:T(8,128)S(1)}, f32[16,128,128]{2,1,0:T(8,128)S(1)}, f32[16,128,128]{2,1,0:T(8,128)S(1)}, f32[16,128,128]{2,1,0:T(8,128)S(...) custom-call(s32[3]{0:T(128)S(1)} %pad_add_fusion.where, ...), custom_call_target="tpu_custom_call", output_to_operand_aliasing={{0}: (12, {}), {1}: (13, {}), {2}: (14, {}), {3}: (15, {}),... | custom-call | tf_op jit(solution)/shard_map/pallas_call | solution.py:235
  51.6 15.1 %all_to_all.11.gram = f32[8,16,128]{2,1,0:T(8,128)S(1)} all-to-all(f32[8,16,128]{2,1,0:T(8,128)S(1)} %get-tuple-element.76), channel_id=1, replica_groups=mesh['sys'=4,'slab'=8] {'slab'}, dimensions={0} | all-to-all | bytes 131072 | tf_op jit(solution)/shard_map/all_to_all | solution.py:441
  66.6 3.1 %shard_map.48 = (f32[16,128,128]{2,1,0:T(8,128)}, f32[16,128,128]{2,1,0:T(8,128)}) custom-call(f32[2,16,128]{2,1,0:T(8,128)S(1)} %get-tuple-element.53.state, f32[8,16,128]{2,1,0:T(8,128)S(1)} %all_to_all.11.gram, f32[16,128,128]{2,1,0:T(8,128)S(1)} %get-tuple-element.47.t0.refs_0_, f32[16,128,128]{2,1,0:T(8,128)S(1)} %get-tuple-element.56.refs_1_, ...), custom_call_target="tpu_custom_call" | custom-call | tf_op jit(solution)/shard_map/pallas_call | solution.py:235
Async XLA Ops:
  2.5 29.0 %collective-permute-start = (f32[9,128,128]{2,1,0:T(8,128)S(1)}, f32[9,128,128]{2,1,0:T(8,128)S(1)}, u32[]{:S(2)}, u32[]{:S(2)}) collective-permute-start(f32[9,128,128]{2,1,0:T(8,128)S(1)} %get-tuple-element.42), channel_id=1, source_target_pairs={{0,1},{1,0},{2,3},{3,2},{4,5},{5,4},{6,7},{7,6},{8,9},{9,8},{10,11... | collective-permute-start | bytes 1769480 | tf_op jit(solution)/shard_map/ppermute | solution.py:433
  10.5 21.1 %collective-permute-start.1 = (f32[9,128,128]{2,1,0:T(8,128)S(1)}, f32[9,128,128]{2,1,0:T(8,128)S(1)}, u32[]{:S(2)}, u32[]{:S(2)}) collective-permute-start(f32[9,128,128]{2,1,0:T(8,128)S(1)} %get-tuple-element.44), channel_id=1, source_target_pairs={{1,2},{3,4},{5,6},{2,1},{4,3},{6,5},{9,10},{11,12},{13,14},{10,9},... | collective-permute-start | bytes 1769480 | tf_op jit(solution)/shard_map/ppermute | solution.py:437
  35.0 9.8 %collective-permute-start.3 = (f32[5,128,128]{2,1,0:T(8,128)S(1)}, f32[5,128,128]{2,1,0:T(8,128)S(1)}, u32[]{:S(2)}, u32[]{:S(2)}) collective-permute-start(f32[5,128,128]{2,1,0:T(8,128)S(1)} %get-tuple-element.62), channel_id=1, source_target_pairs={{0,1},{1,0},{2,3},{3,2},{4,5},{5,4},{6,7},{7,6},{8,9},{9,8},{10,11... | collective-permute-start | bytes 983048 | tf_op jit(solution)/shard_map/ppermute | solution.py:433
  42.2 6.6 %collective-permute-start.2 = (f32[5,128,128]{2,1,0:T(8,128)S(1)}, f32[5,128,128]{2,1,0:T(8,128)S(1)}, u32[]{:S(2)}, u32[]{:S(2)}) collective-permute-start(f32[5,128,128]{2,1,0:T(8,128)S(1)} %get-tuple-element.60), channel_id=1, source_target_pairs={{1,2},{3,4},{5,6},{2,1},{4,3},{6,5},{9,10},{11,12},{13,14},{10,9},... | collective-permute-start | bytes 983048 | tf_op jit(solution)/shard_map/ppermute | solution.py:437
